TPU v7x, 8 devices: a whole 2x2x1 slice. The times are simulated.
8 devices in a mesh: dp: 1 (over z), b: 2 (over y), a: 2 (over x), stage: 2 (over core).
Axes of the slice: x: 2, y: 2, z: 1, core: 2. Of those that a mesh axis runs over, the one named last changes fastest.
Arguments:
- embeds: bfloat16 [2, 6, 768, 4096], P('stage', 'dp')
- attn_gain: float32 [2, 4096], replicated
- w_query: bfloat16 [2, 4096, 4096], P(None, None, ('b', 'a'))
- w_key: bfloat16 [2, 4096, 1024], P(None, None, ('b', 'a'))
- w_value: bfloat16 [2, 4096, 1024], P(None, None, ('b', 'a'))
- w_out: bfloat16 [2, 4096, 4096], P(None, ('b', 'a'))
- mlp_gain: float32 [2, 4096], replicated
- w_gate: bfloat16 [2, 4096, 14336], P(None, None, ('b', 'a'))
- w_up: bfloat16 [2, 4096, 14336], P(None, None, ('b', 'a'))
- w_down: bfloat16 [2, 14336, 4096], P(None, ('b', 'a'))
Outputs:
- output 1: bfloat16 [2, 2, 6, 768, 8, 128], P('stage', None, ('dp', 'a'), None, 'b')
- output 2: bfloat16 [2, 2, 6, 768, 8, 128], P('stage', None, ('dp', 'a'), None, 'b')
- output 3: bfloat16 [2, 6, 4096], P('stage', ('dp', 'a'))
All inputs are finite; a program needn't handle non-finite values.
Results may differ from a plain program's by a relative error of at most 0.02.
Values are sent between devices in bfloat16 or wider.
A program may use at most 1 GiB of HBM per device.

v0:
```python
import functools

import jax
import jax.numpy as jnp
from jax import lax
from jax.experimental import pallas as pl
from jax.experimental.pallas import tpu as pltpu
from jax.sharding import PartitionSpec as P


HEAD_DIM = 128
ROPE_BASE = 500000.0
NORM_EPS = 1e-5
SWAP = [(0, 1), (1, 0)]
FROM_FAR = [(2, 1), (1, 3)]
FROM_NEAR = [(0, 1), (3, 3)]


def rms_norm(hidden, gain_vec):
    as_f32 = hidden.astype(jnp.float32)
    inv_rms = lax.rsqrt(jnp.mean(as_f32 * as_f32, axis=-1, keepdims=True) + NORM_EPS)
    return (as_f32 * inv_rms * gain_vec).astype(jnp.bfloat16)


def rope_tables(seq_len):
    half_dim = HEAD_DIM // 2
    inv_freq = ROPE_BASE ** (-2.0 * jnp.arange(half_dim, dtype=jnp.float32) / HEAD_DIM)
    angles = jnp.arange(seq_len, dtype=jnp.float32)[:, None] * inv_freq[None, :]
    cos_t, sin_t = jnp.cos(angles), jnp.sin(angles)
    return jnp.concatenate([cos_t, cos_t], axis=-1), jnp.concatenate([-sin_t, sin_t], axis=-1)


def matmul(left, right):
    return jnp.dot(left, right, preferred_element_type=jnp.float32)


def add_rounded(left, right):
    return (left.astype(jnp.float32) + right.astype(jnp.float32)).astype(jnp.bfloat16)


def rotate(as_f32, cos_rows, sin_rows):
    return (as_f32 * cos_rows + pltpu.roll(as_f32, HEAD_DIM // 2, 1) * sin_rows).astype(jnp.bfloat16)


def attention_kernel(q_block, group, _, q_ref, k_ref, v_ref, cos_ref, sin_ref, o_ref, kr_ref):
    step = pl.program_id(1)
    seq_len = k_ref.shape[0]

    @pl.when(step == 0)
    def _():
        kr_ref[...] = rotate(k_ref[...].astype(jnp.float32), cos_ref[...], sin_ref[...])

    for i in range(seq_len // q_block):
        @pl.when(step == i)
        def _(i=i):
            keys = min(seq_len, -(-(i + 1) * q_block // 128) * 128)
            rows = pl.ds(i * q_block, q_block)
            cos_rows, sin_rows = cos_ref[rows, :], sin_ref[rows, :]
            q = jnp.concatenate([
                rotate(q_ref[:, g * HEAD_DIM:(g + 1) * HEAD_DIM].astype(jnp.float32), cos_rows, sin_rows)
                for g in range(group)], axis=0)
            row = lax.rem(lax.broadcasted_iota(jnp.int32, (group * q_block, keys), 0), q_block) + i * q_block
            col = lax.broadcasted_iota(jnp.int32, (group * q_block, keys), 1)
            scores = lax.dot_general(q, kr_ref[:keys, :], (((1,), (1,)), ((), ())), preferred_element_type=jnp.float32)
            scores = jnp.where(row >= col, scores * HEAD_DIM ** -0.5, -1e30)
            probs = jnp.exp(scores - jnp.max(scores, axis=-1, keepdims=True))
            probs = probs * (1.0 / jnp.sum(probs, axis=-1, keepdims=True))
            mix = jnp.dot(probs.astype(jnp.bfloat16), v_ref[:keys, :], preferred_element_type=jnp.float32).astype(jnp.bfloat16)
            for g in range(group):
                o_ref[:, g * HEAD_DIM:(g + 1) * HEAD_DIM] = mix[g * q_block:(g + 1) * q_block]


def attention(q, k, v, cos_t, sin_t, order):
    seq_len, kv_width = k.shape
    q_block = seq_len // 8
    group = q.shape[1] // kv_width
    wide = group * HEAD_DIM
    return pl.pallas_call(
        functools.partial(attention_kernel, q_block, group),
        grid_spec=pltpu.PrefetchScalarGridSpec(
            num_scalar_prefetch=1,
            grid=(kv_width // HEAD_DIM, 8),
            in_specs=[
                pl.BlockSpec((q_block, wide), lambda h, i, order_ref: (i, h)),
                pl.BlockSpec((seq_len, HEAD_DIM), lambda h, i, order_ref: (0, h)),
                pl.BlockSpec((seq_len, HEAD_DIM), lambda h, i, order_ref: (0, h)),
                pl.BlockSpec((seq_len, HEAD_DIM), lambda h, i, order_ref: (0, 0)),
                pl.BlockSpec((seq_len, HEAD_DIM), lambda h, i, order_ref: (0, 0)),
            ],
            out_specs=[
                pl.BlockSpec((q_block, wide), lambda h, i, order_ref: (order_ref[i], h)),
                pl.BlockSpec((seq_len, HEAD_DIM), lambda h, i, order_ref: (0, h)),
            ],
        ),
        out_shape=[jax.ShapeDtypeStruct(q.shape, jnp.bfloat16), jax.ShapeDtypeStruct(k.shape, jnp.bfloat16)],
        compiler_params=pltpu.CompilerParams(vmem_limit_bytes=32 * 1024 * 1024),
        cost_estimate=pl.CostEstimate(flops=9_000_000_000, bytes_accessed=5_000_000, transcendentals=4_000_000),
    )(order, q, k, v, cos_t, sin_t)


def kv_kernel(part_ref, x_ref, gain_ref, cos_ref, sin_ref, *refs):
    mine, other, o_ref, normed = refs[:8], refs[8:16], refs[16], refs[17]
    depth, columns = mine[0].shape
    half = 2 * depth
    as_f32 = x_ref[...].astype(jnp.float32)
    inv_rms = lax.rsqrt(jnp.mean(as_f32 * as_f32, axis=-1, keepdims=True) + NORM_EPS)
    whole = (as_f32 * inv_rms * gain_ref[...]).astype(jnp.bfloat16)
    normed[0] = whole[:, :half]
    normed[1] = whole[:, half:]
    part = part_ref[0]
    for piece in range(4):
        product = jnp.dot(normed[part, :, :depth], mine[2 * piece][...], preferred_element_type=jnp.float32)
        product += jnp.dot(normed[part, :, depth:], mine[2 * piece + 1][...], preferred_element_type=jnp.float32)
        product += jnp.dot(normed[1 - part, :, :depth], other[2 * piece][...], preferred_element_type=jnp.float32)
        product += jnp.dot(normed[1 - part, :, depth:], other[2 * piece + 1][...], preferred_element_type=jnp.float32)
        rounded = product.astype(jnp.bfloat16)
        base = piece * columns
        for h in range(columns // 2 // HEAD_DIM):
            cols = slice(h * HEAD_DIM, (h + 1) * HEAD_DIM)
            o_ref[:, base + h * HEAD_DIM:base + (h + 1) * HEAD_DIM] = rotate(rounded[:, cols].astype(jnp.float32), cos_ref[...], sin_ref[...])
        o_ref[:, base + columns // 2:base + columns] = rounded[:, columns // 2:]


def keys_values(x, gain, mine, other, cos_rows, sin_rows, part):
    rows, _ = x.shape
    depth, columns = mine[0].shape
    vmem = pl.BlockSpec(memory_space=pltpu.VMEM)
    return pl.pallas_call(
        kv_kernel,
        in_specs=[pl.BlockSpec(memory_space=pltpu.SMEM)] + [vmem] * 20,
        out_specs=vmem,
        out_shape=jax.ShapeDtypeStruct((rows, 4 * columns), jnp.bfloat16),
        scratch_shapes=[pltpu.VMEM((2, rows, 2 * depth), jnp.bfloat16)],
        compiler_params=pltpu.CompilerParams(vmem_limit_bytes=40 * 1024 * 1024),
        cost_estimate=pl.CostEstimate(flops=32 * rows * depth * columns, bytes_accessed=32 * depth * columns, transcendentals=0),
    )(part, x, gain, cos_rows, sin_rows, *mine, *other)


def tail_kernel(kv_heads, x0_ref, x1_ref, x2_ref, kv0_ref, kv1_ref, kv2_ref, gain_a_ref, gain_m_ref, cos_ref, sin_ref,
                wq_hbm, wo_hbm, wg_hbm, wu_hbm, wd_hbm, o_ref,
                wq, wo, wg, wu, wd, x_src, x_all, q_src, q_all, pk_src, pk_all, mix, p_src, p_all, r_src, r_all,
                w_sem, x_send, x_recv, q_send, q_recv, pk_send, pk_recv, p_send, p_recv, r_send, r_recv):
    a, b, s = lax.axis_index('a'), lax.axis_index('b'), lax.axis_index('stage')
    me = 4 * b + 2 * a + s
    x_refs, kv_refs = (x0_ref, x1_ref, x2_ref), (kv0_ref, kv1_ref, kv2_ref)
    n_chunk = len(x_refs)
    n_rows = o_ref.shape[0]
    group = wq.shape[1] // HEAD_DIM
    eighth, wide = wq.shape[1], wg.shape[1]

    cuts = [
        (wq_hbm.at[1, :, pl.ds(pl.multiple_of(s * eighth, eighth), eighth)], wq),
        (wo_hbm.at[1, pl.ds(pl.multiple_of(s * eighth, eighth), eighth), :], wo),
        (wg_hbm.at[1, :, pl.ds(pl.multiple_of(s * wide, wide), wide)], wg),
        (wu_hbm.at[1, :, pl.ds(pl.multiple_of(s * wide, wide), wide)], wu),
        (wd_hbm.at[1, pl.ds(pl.multiple_of(s * wide, wide), wide), :], wd),
    ]
    fetches = [pltpu.make_async_copy(src, dst, w_sem.at[i]) for i, (src, dst) in enumerate(cuts)]
    for fetch in fetches:
        fetch.start()

    peers = []
    for d in range(1, 8):
        peer_b = 1 - b if d & 4 else b
        peer_a = 1 - a if d & 2 else a
        peer_s = 1 - s if d & 1 else s
        peers.append((4 * peer_b + 2 * peer_a + peer_s, {'b': peer_b, 'a': peer_a, 'stage': peer_s}))

    barrier = pltpu.get_barrier_semaphore()
    for _, where in peers:
        pl.semaphore_signal(barrier, inc=1, device_id=where, device_id_type=pl.DeviceIdType.MESH)
    pl.semaphore_wait(barrier, 7)

    def exchange(source_of, everyone, send, recv):
        copies = [
            pltpu.make_async_remote_copy(
                src_ref=source_of(peer), dst_ref=everyone.at[me], send_sem=send.at[i], recv_sem=recv.at[i],
                device_id=where, device_id_type=pl.DeviceIdType.MESH)
            for i, (peer, where) in enumerate(peers)]
        arrivals = [
            pltpu.make_async_remote_copy(
                src_ref=source_of(peer), dst_ref=everyone.at[peer], send_sem=send.at[i], recv_sem=recv.at[i],
                device_id=where, device_id_type=pl.DeviceIdType.MESH)
            for i, (peer, where) in enumerate(peers)]
        for copy in copies:
            copy.start()
        everyone[me] = source_of(me)[...]
        for arrival in arrivals:
            arrival.wait_recv()
        for copy in copies:
            copy.wait_send()

    def norm(rows, gain_ref):
        inv_rms = lax.rsqrt(jnp.mean(rows * rows, axis=-1, keepdims=True) + NORM_EPS)
        return (rows * inv_rms * gain_ref[...]).astype(jnp.bfloat16)

    row_index = lax.broadcasted_iota(jnp.int32, (n_rows, x0_ref.shape[1]), 0)
    rows = jnp.zeros((n_rows, x0_ref.shape[1]), jnp.float32)
    for c in range(n_chunk):
        last_row = x_refs[c][x_refs[c].shape[0] - 1:, :].astype(jnp.float32)
        rows = jnp.where(row_index == n_chunk * s + c, last_row, rows)
    x_src[...] = rows.astype(jnp.bfloat16)
    is_owner = a + b == 2

    def x_copy(i):
        return pltpu.make_async_remote_copy(
            src_ref=x_src, dst_ref=x_all.at[s], send_sem=x_send.at[i], recv_sem=x_recv.at[s],
            device_id=peers[i][1], device_id_type=pl.DeviceIdType.MESH)

    @pl.when(is_owner)
    def _():
        for i in range(7):
            x_copy(i).start()
        x_all[s] = x_src[...]

    for o in range(2):
        @pl.when(me != 6 + o)
        def _(o=o):
            pltpu.make_async_remote_copy(
                src_ref=x_src, dst_ref=x_all.at[o], send_sem=x_send.at[0], recv_sem=x_recv.at[o],
                device_id=peers[0][1], device_id_type=pl.DeviceIdType.MESH).wait_recv()

    @pl.when(is_owner)
    def _():
        for i in range(7):
            x_copy(i).wait_send()

    last = x_all[0].astype(jnp.float32) + x_all[1].astype(jnp.float32)
    fetches[0].wait()
    q = jnp.dot(norm(last, gain_a_ref), wq[...], preferred_element_type=jnp.float32)
    q_src[...] = q.astype(jnp.bfloat16).astype(jnp.float32)
    exchange(lambda peer: q_src, q_all, q_send, q_recv)

    kv_width = kv_heads * HEAD_DIM
    for piece in range(4):
        head_b = 1 - b if piece & 2 else b
        head_a = 1 - a if piece & 1 else a
        for h in range(kv_heads):
            head = (2 * head_b + head_a) * kv_heads + h
            low = 2 * piece * kv_width + h * HEAD_DIM
            for c in range(n_chunk):
                q_row = q_all[head, pl.ds(n_chunk * s + c, 1), :]
                q_heads = jnp.concatenate([q_row[:, g * HEAD_DIM:(g + 1) * HEAD_DIM] for g in range(group)], axis=0)
                q_heads = rotate(q_heads, cos_ref[...], sin_ref[...])
                k = kv_refs[c][:, low:low + HEAD_DIM]
                v = kv_refs[c][:, low + kv_width:low + kv_width + HEAD_DIM]
                scores = lax.dot_general(q_heads, k, (((1,), (1,)), ((), ())), preferred_element_type=jnp.float32) * HEAD_DIM ** -0.5
                top = jnp.max(scores, axis=-1, keepdims=True)
                probs = jnp.exp(scores - top)
                total = jnp.sum(probs, axis=-1, keepdims=True)
                pk_src[head, c, :, :HEAD_DIM] = jnp.dot(probs.astype(jnp.bfloat16), v, preferred_element_type=jnp.float32)
                pk_src[head, c, :, HEAD_DIM:2 * HEAD_DIM] = jnp.broadcast_to(top, (group, HEAD_DIM))
                pk_src[head, c, :, 2 * HEAD_DIM:] = jnp.broadcast_to(total, (group, HEAD_DIM))
    exchange(lambda peer: pk_src.at[peer], pk_all, pk_send, pk_recv)

    mix[...] = jnp.zeros_like(mix)
    for stage in range(2):
        for c in range(n_chunk):
            found = [pk_all[2 * i + stage, c] for i in range(4)]
            top = found[0][:, HEAD_DIM:2 * HEAD_DIM]
            for part in found[1:]:
                top = jnp.maximum(top, part[:, HEAD_DIM:2 * HEAD_DIM])
            value, total = jnp.zeros_like(top), jnp.zeros_like(top)
            for part in found:
                scale = jnp.exp(part[:, HEAD_DIM:2 * HEAD_DIM] - top)
                value += part[:, :HEAD_DIM] * scale
                total += part[:, 2 * HEAD_DIM:] * scale
            value = value / total
            for g in range(group):
                mix[n_chunk * stage + c:n_chunk * stage + c + 1, g * HEAD_DIM:(g + 1) * HEAD_DIM] = value[g:g + 1, :]

    def summed(everyone):
        total = everyone[0].astype(jnp.float32)
        for i in range(1, 8):
            total += everyone[i].astype(jnp.float32)
        return total.astype(jnp.bfloat16).astype(jnp.float32)

    fetches[1].wait()
    p_src[...] = jnp.dot(mix[...].astype(jnp.bfloat16), wo[...], preferred_element_type=jnp.float32).astype(jnp.bfloat16)
    exchange(lambda peer: p_src, p_all, p_send, p_recv)
    last = (last + summed(p_all)).astype(jnp.bfloat16).astype(jnp.float32)
    normed = norm(last, gain_m_ref)
    fetches[2].wait()
    gate = jnp.dot(normed, wg[...], preferred_element_type=jnp.float32).astype(jnp.bfloat16).astype(jnp.float32)
    fetches[3].wait()
    up = jnp.dot(normed, wu[...], preferred_element_type=jnp.float32).astype(jnp.bfloat16).astype(jnp.float32)
    act = (gate * (1.0 / (1.0 + jnp.exp(-gate))) * up).astype(jnp.bfloat16)
    fetches[4].wait()
    r_src[...] = jnp.dot(act, wd[...], preferred_element_type=jnp.float32).astype(jnp.bfloat16)
    exchange(lambda peer: r_src, r_all, r_send, r_recv)
    o_ref[...] = (last + summed(r_all)).astype(jnp.bfloat16)


def last_rows(finals, kvs, gain_a, gain_m, cos_row, sin_row, w_query, w_out, w_gate, w_up, w_down, kv_heads):
    width = finals[0].shape[1]
    eighth = w_query.shape[2] // 2
    wide = w_gate.shape[2] // 2
    group = eighth // HEAD_DIM
    n_rows = 8
    n_chunk = len(finals)
    vmem = pl.BlockSpec(memory_space=pltpu.VMEM)
    last_block = pl.BlockSpec((n_rows, width), lambda i: (finals[0].shape[0] // n_rows - 1, 0))

    def full(value):
        return pl.BlockSpec(value.shape, lambda i: (0,) * value.ndim)

    seven = pltpu.SemaphoreType.DMA((7,))
    return pl.pallas_call(
        functools.partial(tail_kernel, kv_heads),
        grid=(1,),
        in_specs=[last_block] * n_chunk + [full(kv) for kv in kvs] + [full(v) for v in (gain_a, gain_m, cos_row, sin_row)]
        + [pl.BlockSpec(memory_space=pl.ANY)] * 5,
        out_specs=pl.BlockSpec((n_rows, width), lambda i: (0, 0)),
        out_shape=jax.ShapeDtypeStruct((n_rows, width), jnp.bfloat16),
        scratch_shapes=[
            pltpu.VMEM((width, eighth), jnp.bfloat16),
            pltpu.VMEM((eighth, width), jnp.bfloat16),
            pltpu.VMEM((width, wide), jnp.bfloat16),
            pltpu.VMEM((width, wide), jnp.bfloat16),
            pltpu.VMEM((wide, width), jnp.bfloat16),
            pltpu.VMEM((n_rows, width), jnp.bfloat16),
            pltpu.VMEM((2, n_rows, width), jnp.bfloat16),
            pltpu.VMEM((n_rows, eighth), jnp.float32),
            pltpu.VMEM((8, n_rows, eighth), jnp.float32),
            pltpu.VMEM((8, n_chunk, group, 3 * HEAD_DIM), jnp.float32),
            pltpu.VMEM((8, n_chunk, group, 3 * HEAD_DIM), jnp.float32),
            pltpu.VMEM((n_rows, eighth), jnp.float32),
            pltpu.VMEM((n_rows, width), jnp.bfloat16),
            pltpu.VMEM((8, n_rows, width), jnp.bfloat16),
            pltpu.VMEM((n_rows, width), jnp.bfloat16),
            pltpu.VMEM((8, n_rows, width), jnp.bfloat16),
            pltpu.SemaphoreType.DMA((5,)),
            seven, pltpu.SemaphoreType.DMA((2,)), seven, seven, seven, seven, seven, seven, seven, seven,
        ],
        compiler_params=pltpu.CompilerParams(collective_id=0, has_side_effects=True, vmem_limit_bytes=63 * 1024 * 1024),
        cost_estimate=pl.CostEstimate(flops=9_000_000_000, bytes_accessed=60_000_000, transcendentals=0),
    )(*finals, *kvs, gain_a, gain_m, cos_row, sin_row, w_query, w_out, w_gate, w_up, w_down)


def first_cut_kernel(where_ref, near_ref, far_ref, k_ref, v_ref):
    kv_width = near_ref.shape[-1] // 2
    own_low = where_ref[0] == 0
    near, far = near_ref[0], far_ref[0]
    low, high = jnp.where(own_low, near, far), jnp.where(own_low, far, near)
    k_ref[0, 0, :, :kv_width] = low[:, :kv_width]
    k_ref[0, 0, :, kv_width:] = high[:, :kv_width]
    v_ref[0, 0, :, :kv_width] = low[:, kv_width:]
    v_ref[0, 0, :, kv_width:] = high[:, kv_width:]


def first_cut(near, far, where):
    n_chunk, seq_len, columns = near.shape
    rows = seq_len // 2
    source = pl.BlockSpec((1, rows, columns), lambda c, j, where_ref: (c, j, 0))
    target = pl.BlockSpec((1, 1, rows, columns), lambda c, j, where_ref: (0, c, j, 0))
    return pl.pallas_call(
        first_cut_kernel,
        grid_spec=pltpu.PrefetchScalarGridSpec(num_scalar_prefetch=1, grid=(n_chunk, 2), in_specs=[source] * 2, out_specs=[target] * 2),
        out_shape=[jax.ShapeDtypeStruct((2, n_chunk, seq_len, columns), jnp.bfloat16)] * 2,
        compiler_params=pltpu.CompilerParams(vmem_limit_bytes=32 * 1024 * 1024),
        cost_estimate=pl.CostEstimate(flops=1_000_000_000, bytes_accessed=19_000_000, transcendentals=0),
    )(where, near, far)


def second_cut_kernel(where_ref, near_ref, far_ref, k_in, v_in, k_ref, v_ref):
    columns = near_ref.shape[-1] // 2
    kv_width = columns // 2

    def put(source):
        mine, other = source[:, :columns], source[:, columns:]
        own_low = where_ref[0] + pl.program_id(0) - 2 * where_ref[0] * pl.program_id(0) == 0
        low, high = jnp.where(own_low, mine, other), jnp.where(own_low, other, mine)
        k_ref[0, 0, :, :kv_width] = low[:, :kv_width]
        k_ref[0, 0, :, kv_width:] = high[:, :kv_width]
        v_ref[0, 0, :, :kv_width] = low[:, kv_width:]
        v_ref[0, 0, :, kv_width:] = high[:, kv_width:]

    @pl.when(pl.program_id(0) == 0)
    def _():
        put(near_ref[0])

    @pl.when(pl.program_id(0) == 1)
    def _():
        put(far_ref[0])


def second_cut(near, far, where, k_flat, v_flat, request):
    _, rows, columns = near.shape
    block = rows // 2

    def place(i, j, half, where_ref):
        along_x = where_ref[0] + i - 2 * where_ref[0] * i
        along_y = where_ref[1] + j - 2 * where_ref[1] * j
        return 1, request, (1 - half) * (2 * along_x + along_y) + half * (4 + 2 * along_y + along_x), 0

    source = pl.BlockSpec((1, block, columns), lambda i, j, half, where_ref: (j, half, 0))
    target = pl.BlockSpec((1, 1, block, columns // 2), place)
    whole = pl.BlockSpec(memory_space=pl.ANY)
    return pl.pallas_call(
        second_cut_kernel,
        grid_spec=pltpu.PrefetchScalarGridSpec(
            num_scalar_prefetch=1, grid=(2, 2, 2), in_specs=[source] * 2 + [whole] * 2, out_specs=[target] * 2),
        out_shape=[jax.ShapeDtypeStruct(k_flat.shape, jnp.bfloat16)] * 2,
        input_output_aliases={3: 0, 4: 1},
        compiler_params=pltpu.CompilerParams(vmem_limit_bytes=32 * 1024 * 1024),
        cost_estimate=pl.CostEstimate(flops=300_000_000, bytes_accessed=5_000_000, transcendentals=0),
    )(where, near, far, k_flat, v_flat)


def solution(mesh):
    tp_axes = ('b', 'a')
    weight_cols = P(None, None, tp_axes)
    weight_rows = P(None, tp_axes, None)
    in_specs = (P('stage', 'dp', None, None), P(), weight_cols, weight_cols, weight_cols, weight_rows, P(), weight_cols, weight_cols, weight_rows)
    cache_spec = P('stage', None, ('dp', 'a'), None, 'b', None)
    out_specs = (cache_spec, cache_spec, P('stage', ('dp', 'a'), None))

    def over_x(value):
        return lax.ppermute(value, 'a', SWAP)

    def over_y(value):
        return lax.ppermute(value, 'b', SWAP)

    def across(value):
        return lax.ppermute(value, 'stage', SWAP)

    def hold(values, *after):
        return lax.optimization_barrier((values, after))[0]

    def stage_program(embeds, attn_gain, w_query, w_key, w_value, w_out, mlp_gain, w_gate, w_up, w_down):
        a, b, s = lax.axis_index('a'), lax.axis_index('b'), lax.axis_index('stage')
        n_req, seq_len, width = embeds.shape[1:]
        n_chunk = n_req // 2
        block = seq_len // 8
        kv_width = w_key.shape[2]
        kv_heads = kv_width // HEAD_DIM
        kv2 = 2 * kv_width
        half_rows = seq_len // 2
        half_width = width // 2
        cos_t, sin_t = rope_tables(seq_len)
        chip = 2 * b + a
        part = s.astype(jnp.int32).reshape(1)
        where = jnp.stack([a, b]).astype(jnp.int32)

        fours = jnp.arange(4, dtype=jnp.int32)
        order = jnp.concatenate([jnp.bitwise_xor(fours, 2 * a + b), 4 + jnp.bitwise_xor(fours, chip)]).astype(jnp.int32)

        def own_rows(value):
            return jnp.concatenate([
                lax.dynamic_slice_in_dim(value, block * (2 * a + b), block, 0),
                lax.dynamic_slice_in_dim(value, half_rows + block * chip, block, 0)], axis=0)

        def send_parts(part_sum):
            quarter = 2 * block
            return part_sum[quarter:2 * quarter], part_sum[3 * quarter:]

        def send_wide(sends):
            return over_x(sends[0]), over_y(sends[1])

        def add_wide(part_sum, got):
            quarter = 2 * block
            return add_rounded(part_sum[:quarter], got[0]), add_rounded(part_sum[2 * quarter:3 * quarter], got[1])

        def send_narrow(sums):
            return over_y(sums[0][block:]), over_x(sums[1][block:])

        def add_narrow(residual, sums, got):
            kept = jnp.concatenate([sums[0][:block], sums[1][:block]], axis=0)
            return add_rounded(residual, add_rounded(kept, jnp.concatenate(got, axis=0)))

        def gather_near(own):
            return over_y(own[:block]), over_x(own[block:])

        def join_near(own, got):
            return jnp.concatenate([own[:block], got[0]], axis=0), jnp.concatenate([own[block:], got[1]], axis=0)

        def gather_far(near):
            return over_x(near[0]), over_y(near[1])

        def join_far(near, far):
            return jnp.concatenate([near[0], far[0], near[1], far[1]], axis=0)

        def take(value):
            return lax.ppermute(value, 'stage', [(0, 1)])

        moved0 = take(embeds[0, n_chunk])

        quarter_width = width // 4

        def w_block(half, lower):
            rows = half * half_width + lower * quarter_width
            return jnp.concatenate([lax.dynamic_slice_in_dim(w[1], rows, quarter_width, 0) for w in (w_key, w_value)], axis=1)

        w_top, w_bottom = hold((w_block(s, 0), w_block(s, 1)), embeds[0, n_chunk, :8, :128])
        top_y, bottom_x = over_y(w_top), over_x(w_bottom)
        top_x, bottom_y = over_x(w_top), over_y(w_bottom)

        def project(x):
            normed = rms_norm(x, attn_gain[0])
            q = matmul(normed, w_query[0]).astype(jnp.bfloat16)
            k = matmul(normed, w_key[0]).astype(jnp.bfloat16)
            v = matmul(normed, w_value[0]).astype(jnp.bfloat16)
            return q, k, v

        def attend(q, k, v):
            mix, k_rot = attention(q, k, v, cos_t, sin_t, order)
            return matmul(mix, w_out[0]).astype(jnp.bfloat16), jnp.concatenate([k_rot, v], axis=1)

        def gate_of(normed):
            return matmul(normed, w_gate[0]).astype(jnp.bfloat16)

        def act_of(normed, gate):
            up = matmul(normed, w_up[0]).astype(jnp.bfloat16)
            return (jax.nn.silu(gate.astype(jnp.float32)) * up.astype(jnp.float32)).astype(jnp.bfloat16)

        def down_of(act):
            return matmul(act, w_down[0]).astype(jnp.bfloat16)

        def hidden_of(first, second):
            return jnp.where(s == 0, first, second)

        own_cos, own_sin = own_rows(cos_t), own_rows(sin_t)

        x0 = hidden_of(hold(embeds, moved0)[0, 0], moved0)
        qkv0 = project(x0)
        moved1 = take(hold(embeds, qkv0)[0, n_chunk + 1])
        top_d, bottom_d = over_x(hold(top_y, qkv0)), over_y(hold(bottom_x, qkv0))
        p0, kv0_0 = attend(*qkv0)
        own_x0 = own_rows(x0)
        send = send_parts(p0)
        wide0 = send_wide(send)

        moved2 = take(hold(embeds, send)[0, n_chunk + 2])
        embeds_1, moved1 = hold((embeds, moved1), send, moved1)
        x1 = hidden_of(embeds_1[0, 1], moved1)
        p1, kv0_1 = attend(*project(x1))
        own_x1 = own_rows(x1)
        send = send_parts(p1)
        wide1 = send_wide(send)

        sums0 = add_wide(p0, hold(wide0, send))
        narrow0 = send_narrow(sums0)

        embeds_2, moved2 = hold((embeds, moved2), sums0, moved2)
        x2 = hidden_of(embeds_2[0, 2], moved2)
        p2, kv0_2 = attend(*project(x2))
        own_x2 = own_rows(x2)

        sums1 = add_wide(p1, hold(wide1, p2))
        narrow1 = send_narrow(sums1)
        own1_0 = add_narrow(own_x0, sums0, hold(narrow0, sums1))
        h0 = rms_norm(own1_0, mlp_gain[0])
        near_got0 = gather_near(h0)

        own1_1 = add_narrow(own_x1, sums1, hold(narrow1, h0))
        h1 = rms_norm(own1_1, mlp_gain[0])
        near_got1 = gather_near(h1)
        near0 = join_near(h0, hold(near_got0, h1))
        far0 = gather_far(near0)
        send = hold(send_parts(p2), near0)
        wide2 = send_wide(send)
        near1 = join_near(h1, hold(near_got1, send))
        far1 = gather_far(near1)

        fetched = hold((top_x, bottom_x, top_y, bottom_y, top_d, bottom_d), near1)
        w_mine = [w_top, w_bottom] + list(fetched)
        w_other = [w_block(1 - s, 0), w_block(1 - s, 1)] + [across(piece) for piece in fetched]

        normed = join_far(near0, hold(far0, near1))
        act = act_of(normed, gate_of(normed))
        sums2 = add_wide(p2, hold(wide2, act))
        narrow2 = send_narrow(sums2)
        d0 = down_of(hold(act, sums2))
        send = send_parts(d0)
        wide0 = send_wide(send)

        normed = join_far(near1, hold(far1, send))
        gate = gate_of(normed)
        own1_2 = add_narrow(own_x2, sums2, hold(narrow2, gate))
        h2 = rms_norm(own1_2, mlp_gain[0])
        near_got2 = gather_near(h2)
        act = act_of(hold(normed, h2), gate)
        sums0 = add_wide(d0, hold(wide0, act))
        narrow0 = send_narrow(sums0)
        near2 = join_near(h2, hold(near_got2, sums0))
        far2 = gather_far(near2)
        d1 = down_of(hold(act, near2))
        send = send_parts(d1)
        wide1 = send_wide(send)

        def keys_values_of(final):
            return keys_values(final, attn_gain[1:2], w_mine, w_other, own_cos, own_sin, part)

        def to_decode(value):
            return lax.ppermute(value, ('a', 'stage'), FROM_NEAR), lax.ppermute(value, ('a', 'stage'), FROM_FAR)

        final0 = add_narrow(own1_0, sums0, hold(narrow0, send))
        kv1_0 = keys_values_of(final0)
        cut0 = to_decode(hold(jnp.stack([kv0_0, kv0_1, kv0_2]), kv1_0))

        def along_y(kv, *after):
            return over_y(hold(kv[:, 2 * kv2:], *after))

        def to_decode_rows(kv, got):
            return to_decode(jnp.stack([kv[:, :2 * kv2], got]))

        normed = join_far(near2, hold(far2, kv1_0))
        gate = gate_of(normed)
        got_0 = along_y(kv1_0, gate)
        act = act_of(normed, gate)
        sums1 = add_wide(d1, hold(wide1, act))
        narrow1 = send_narrow(sums1)
        cut1_0 = to_decode_rows(kv1_0, hold(got_0, sums1))
        d2 = down_of(hold(act, sums1))
        send = send_parts(d2)
        wide2 = send_wide(send)
        final1 = add_narrow(own1_1, sums1, hold(narrow1, send))
        kv1_1 = keys_values_of(final1)
        got_1 = along_y(kv1_1)
        k_flat, v_flat = first_cut(*hold(cut0, kv1_1), where)
        sums2 = add_wide(d2, hold(wide2, k_flat))
        narrow2 = send_narrow(sums2)
        k_flat, v_flat = second_cut(*hold(cut1_0, sums2), where, k_flat, v_flat, 0)
        final2 = add_narrow(own1_2, sums2, hold(narrow2, k_flat))
        kv1_2 = keys_values_of(final2)
        got_2 = along_y(kv1_2)
        cut1_1 = to_decode_rows(kv1_1, hold(got_1, kv1_2))
        cut1_2 = to_decode_rows(kv1_2, got_2)

        last = last_rows(
            (final0, final1, final2), (kv1_0, kv1_1, hold(kv1_2, got_2)), attn_gain[1:2], mlp_gain[1:2],
            cos_t[-1:], sin_t[-1:], w_query, w_out, w_gate, w_up, w_down, kv_heads)
        last_out = lax.dynamic_slice_in_dim(last, a * n_chunk, n_chunk, 0)
        last_out = jnp.where(s == 1, last_out, jnp.zeros_like(last_out))

        for c, cut in ((1, cut1_1), (2, cut1_2)):
            k_flat, v_flat = second_cut(*hold(cut, last), where, k_flat, v_flat, c)
        cache_shape = (1, 2, n_chunk, seq_len, 2 * kv_heads, HEAD_DIM)
        return k_flat.reshape(cache_shape), v_flat.reshape(cache_shape), last_out[None]

    return jax.shard_map(stage_program, mesh=mesh, in_specs=in_specs, out_specs=out_specs, check_vma=False)
```

profile of v0, /device:TPU:0, one launch (start us, length us, event | category | flops | bytes accessed | tf_op | source)
XLA Modules:
  0.0 935.6 jit_solution(7762898867546521554)
XLA Ops:
  56.9 15.7 %shard_map.121 = (bf16[768,1024]{1,0:T(8,128)(2,1)S(1)}, bf16[768,256]{1,0:T(8,128)(2,1)S(1)}) custom-call(s32[8]{0:T(128)S(1)} %pad_add_fusion.1._, bf16[768,1024]{1,0:T(8,128)(2,1)S(1)} %fusion.135.q_ref, bf16[768,256]{1,0:T(8,128)(2,1)S(1)} %fusion.150.k_ref, bf16[768,256]{1,0:T(8,128)(2,1)S(1)} %fusion.159.v_ref, ...), custom_call_target="tpu_custom_call" | custom-call | flops 8999999488 | bytes 5000000 | tf_op jit(solution)/shard_map/pallas_call | solution.py:78
  119.7 15.9 %shard_map.122 = (bf16[768,1024]{1,0:T(8,128)(2,1)S(1)}, bf16[768,256]{1,0:T(8,128)(2,1)S(1)}) custom-call(s32[8]{0:T(128)S(1)} %pad_add_fusion.1._, bf16[768,1024]{1,0:T(8,128)(2,1)S(1)} %fusion.138.q_ref, bf16[768,256]{1,0:T(8,128)(2,1)S(1)} %fusion.153.k_ref, bf16[768,256]{1,0:T(8,128)(2,1)S(1)} %fusion.162.v_ref, ...), custom_call_target="tpu_custom_call" | custom-call | flops 8999999488 | bytes 5000000 | tf_op jit(solution)/shard_map/pallas_call | solution.py:78
  179.1 16.1 %shard_map.123 = (bf16[768,1024]{1,0:T(8,128)(2,1)S(1)}, bf16[768,256]{1,0:T(8,128)(2,1)S(1)}) custom-call(s32[8]{0:T(128)S(1)} %pad_add_fusion.1._, bf16[768,1024]{1,0:T(8,128)(2,1)S(1)} %fusion.141.q_ref, bf16[768,256]{1,0:T(8,128)(2,1)S(1)} %fusion.156.k_ref, bf16[768,256]{1,0:T(8,128)(2,1)S(1)} %fusion.165.v_ref, ...), custom_call_target="tpu_custom_call" | custom-call | flops 8999999488 | bytes 5000000 | tf_op jit(solution)/shard_map/pallas_call | solution.py:78
  235.1 17.0 %collective-permute-done.11 = bf16[96,4096]{1,0:T(8,128)(2,1)S(1)} collective-permute-done((bf16[96,4096]{1,0:T(8,128)(2,1)S(1)}, bf16[96,4096]{1,0:T(8,128)(2,1)S(1)}, u32[]{:S(2)}, u32[]{:S(2)}) %collective-permute-start.11) | collective-permute-done | bytes 786464 | tf_op jit(solution)/shard_map/ppermute | solution.py:422
  255.4 17.0 %collective-permute-done.9 = bf16[96,4096]{1,0:T(8,128)(2,1)S(1)} collective-permute-done((bf16[96,4096]{1,0:T(8,128)(2,1)S(1)}, bf16[96,4096]{1,0:T(8,128)(2,1)S(1)}, u32[]{:S(2)}, u32[]{:S(2)}) %collective-permute-start.9) | collective-permute-done | bytes 786464 | tf_op jit(solution)/shard_map/ppermute | solution.py:422
  275.3 17.6 %collective-permute-done.17 = bf16[96,4096]{1,0:T(8,128)(2,1)S(1)} collective-permute-done((bf16[96,4096]{1,0:T(8,128)(2,1)S(1)}, bf16[96,4096]{1,0:T(8,128)(2,1)S(1)}, u32[]{:S(2)}, u32[]{:S(2)}) %collective-permute-start.17) | collective-permute-done | bytes 786464 | tf_op jit(solution)/shard_map/ppermute | solution.py:422
  300.9 14.4 %collective-permute-done.36.refs_7_ = bf16[1024,512]{1,0:T(8,128)(2,1)S(1)} collective-permute-done((bf16[1024,512]{1,0:T(8,128)(2,1)}, bf16[1024,512]{1,0:T(8,128)(2,1)S(1)}, u32[]{:S(2)}, u32[]{:S(2)}) %collective-permute-start.36) | collective-permute-done | bytes 1048608 | tf_op jit(solution)/shard_map/ppermute | solution.py:422
  316.8 13.3 %collective-permute-done.15 = bf16[192,4096]{1,0:T(8,128)(2,1)S(1)} collective-permute-done((bf16[192,4096]{1,0:T(8,128)(2,1)S(1)}, bf16[192,4096]{1,0:T(8,128)(2,1)S(1)}, u32[]{:S(2)}, u32[]{:S(2)}) %collective-permute-start.15) | collective-permute-done | bytes 1572896 | tf_op jit(solution)/shard_map/ppermute | solution.py:419
  331.7 17.3 %collective-permute-done.16 = bf16[192,4096]{1,0:T(8,128)(2,1)S(1)} collective-permute-done((bf16[192,4096]{1,0:T(8,128)(2,1)S(1)}, bf16[192,4096]{1,0:T(8,128)(2,1)S(1)}, u32[]{:S(2)}, u32[]{:S(2)}) %collective-permute-start.16) | collective-permute-done | bytes 1572896 | tf_op jit(solution)/shard_map/ppermute | solution.py:422
  353.5 30.9 %fusion.81 = bf16[768,3584]{1,0:T(8,128)(2,1)} fusion(bf16[768,4096]{1,0:T(8,128)(2,1)} %constant_dynamic-update-slice_fusion, bf16[2,4096,3584]{2,1,0:T(8,128)(2,1)} %wg_hbm.1), kind=kOutput, calls=%fused_computation.81 | convolution fusion | flops 22551330816 | bytes 41156608 | tf_op jit(solution)/shard_map/dot_general | solution.py:34
  384.4 32.3 %fusion.50 = bf16[768,3584]{1,0:T(8,128)(2,1)} fusion(bf16[768,3584]{1,0:T(8,128)(2,1)} %fusion.81, bf16[768,4096]{1,0:T(8,128)(2,1)} %constant_dynamic-update-slice_fusion, bf16[2,4096,3584]{2,1,0:T(8,128)(2,1)} %wu_hbm.1), kind=kOutput, calls=%fused_computation.62 | convolution fusion | flops 22573350912 | bytes 46661632 | tf_op jit(solution)/shard_map/dot_general | solution.py:34
  418.5 28.3 %fusion.63 = bf16[768,4096]{1,0:T(8,128)(2,1)S(1)} fusion(bf16[768,3584]{1,0:T(8,128)(2,1)} %fusion.50, bf16[2,3584,4096]{2,1,0:T(8,128)(2,1)} %wd_hbm.1), kind=kOutput, calls=%fused_computation.75 | convolution fusion | flops 22551724032 | bytes 41156608 | tf_op jit(solution)/shard_map/dot_general | solution.py:34
  459.0 30.9 %fusion.84 = bf16[768,3584]{1,0:T(8,128)(2,1)} fusion(bf16[768,4096]{1,0:T(8,128)(2,1)} %constant_dynamic-update-slice_fusion.6, bf16[2,4096,3584]{2,1,0:T(8,128)(2,1)} %wg_hbm.1), kind=kOutput, calls=%fused_computation.82 | convolution fusion | flops 22551330816 | bytes 41156608 | tf_op jit(solution)/shard_map/dot_general | solution.py:34
  492.9 32.8 %fusion.49 = bf16[768,3584]{1,0:T(8,128)(2,1)} fusion(bf16[768,3584]{1,0:T(8,128)(2,1)} %fusion.84, bf16[768,4096]{1,0:T(8,128)(2,1)} %constant_dynamic-update-slice_fusion.6, bf16[2,4096,3584]{2,1,0:T(8,128)(2,1)} %wu_hbm.1), kind=kOutput, calls=%fused_computation.61 | convolution fusion | flops 22573350912 | bytes 46661632 | tf_op jit(solution)/shard_map/dot_general | solution.py:34
  532.7 12.9 %collective-permute-done.23 = bf16[96,4096]{1,0:T(8,128)(2,1)S(1)} collective-permute-done((bf16[96,4096]{1,0:T(8,128)(2,1)S(1)}, bf16[96,4096]{1,0:T(8,128)(2,1)S(1)}, u32[]{:S(2)}, u32[]{:S(2)}) %collective-permute-start.23) | collective-permute-done | bytes 786464 | tf_op jit(solution)/shard_map/ppermute | solution.py:422
  549.6 29.2 %fusion.66 = bf16[768,4096]{1,0:T(8,128)(2,1)} fusion(bf16[768,3584]{1,0:T(8,128)(2,1)} %fusion.49, bf16[2,3584,4096]{2,1,0:T(8,128)(2,1)} %wd_hbm.1), kind=kOutput, calls=%fused_computation.76 | convolution fusion | flops 22551724032 | bytes 41156608 | tf_op jit(solution)/shard_map/dot_general | solution.py:34
  602.6 18.3 %collective-permute-done.27 = bf16[192,4096]{1,0:T(8,128)(2,1)} collective-permute-done((bf16[192,4096]{1,0:T(8,128)(2,1)S(1)}, bf16[192,4096]{1,0:T(8,128)(2,1)}, u32[]{:S(2)}, u32[]{:S(2)}) %collective-permute-start.27) | collective-permute-done | bytes 1572896 | tf_op jit(solution)/shard_map/ppermute | solution.py:419
  629.8 28.2 %fusion.87 = bf16[768,3584]{1,0:T(8,128)(2,1)S(1)} fusion(bf16[768,4096]{1,0:T(8,128)(2,1)} %constant_dynamic-update-slice_fusion.12, bf16[2,4096,3584]{2,1,0:T(8,128)(2,1)} %wg_hbm.1), kind=kOutput, calls=%fused_computation.83 | convolution fusion | flops 22551330816 | bytes 41156608 | tf_op jit(solution)/shard_map/dot_general | solution.py:34
  658.0 31.9 %fusion.48 = bf16[768,3584]{1,0:T(8,128)(2,1)} fusion(bf16[768,3584]{1,0:T(8,128)(2,1)S(1)} %fusion.87, bf16[768,4096]{1,0:T(8,128)(2,1)} %constant_dynamic-update-slice_fusion.12, bf16[2,4096,3584]{2,1,0:T(8,128)(2,1)} %wu_hbm.1), kind=kOutput, calls=%fused_computation.60 | convolution fusion | flops 22573350912 | bytes 46661632 | tf_op jit(solution)/shard_map/dot_general | solution.py:34
  694.1 29.3 %fusion.69 = bf16[768,4096]{1,0:T(8,128)(2,1)} fusion(bf16[768,3584]{1,0:T(8,128)(2,1)} %fusion.48, bf16[2,3584,4096]{2,1,0:T(8,128)(2,1)} %wd_hbm.1), kind=kOutput, calls=%fused_computation.77 | convolution fusion | flops 22551724032 | bytes 41156608 | tf_op jit(solution)/shard_map/dot_general | solution.py:34
  730.3 21.5 %collective-permute-done.53 = bf16[192,1024]{1,0:T(8,128)(2,1)S(1)} collective-permute-done((bf16[192,1024]{1,0:T(8,128)(2,1)S(1)}, bf16[192,1024]{1,0:T(8,128)(2,1)S(1)}, u32[]{:S(2)}, u32[]{:S(2)}) %collective-permute-start.53) | collective-permute-done | bytes 393248 | tf_op jit(solution)/shard_map/ppermute | solution.py:422
  769.0 19.0 %collective-permute-done.45 = bf16[192,4096]{1,0:T(8,128)(2,1)S(1)} collective-permute-done((bf16[192,4096]{1,0:T(8,128)(2,1)}, bf16[192,4096]{1,0:T(8,128)(2,1)S(1)}, u32[]{:S(2)}, u32[]{:S(2)}) %collective-permute-start.45) | collective-permute-done | bytes 1572896 | tf_op jit(solution)/shard_map/ppermute | solution.py:419
  801.0 10.7 %collective-permute-done.51 = bf16[96,4096]{1,0:T(8,128)(2,1)S(1)} collective-permute-done((bf16[96,4096]{1,0:T(8,128)(2,1)S(1)}, bf16[96,4096]{1,0:T(8,128)(2,1)S(1)}, u32[]{:S(2)}, u32[]{:S(2)}) %collective-permute-start.51) | collective-permute-done | bytes 786464 | tf_op jit(solution)/shard_map/ppermute | solution.py:422
  844.3 54.6 %shard_map.129 = bf16[8,4096]{1,0:T(8,128)(2,1)} custom-call(bf16[192,4096]{1,0:T(8,128)(2,1)} %fusion.108.x_ref.x0_ref, bf16[192,4096]{1,0:T(8,128)(2,1)} %fusion.112.x_ref.x1_ref, bf16[192,4096]{1,0:T(8,128)(2,1)} %fusion.116.x_ref.x2_ref, bf16[192,2048]{1,0:T(8,128)(2,1)} %copy-done.10, bf16[192,2048]{1,0:T(8,128)(2,1)} %copy-done.11, ...), custom_call_target="tpu_custom_call" | custom-call | flops 8999999488 | bytes 60000000 | tf_op jit(solution)/shard_map/pallas_call | solution.py:308
  (347 shorter events, 378.4 us)
Async XLA Ops:
  20.4 254.8 %collective-permute-start.31 = (bf16[1024,512]{1,0:T(8,128)(2,1)}, bf16[1024,512]{1,0:T(8,128)(2,1)}, u32[]{:S(2)}, u32[]{:S(2)}) collective-permute-start(bf16[1024,512]{1,0:T(8,128)(2,1)} %pad_maximum_fusion.7.refs_0_), channel_id=1, source_target_pairs={{0,2},{2,0},{1,3},{3,1},{4,6},{6,4},{5,7},{7,5}} | collective-permute-start | bytes 3145736 | tf_op jit(solution)/shard_map/ppermute | solution.py:419
  22.7 64.0 %collective-permute-start.33 = (bf16[1024,512]{1,0:T(8,128)(2,1)}, bf16[1024,512]{1,0:T(8,128)(2,1)}, u32[]{:S(2)}, u32[]{:S(2)}) collective-permute-start(bf16[1024,512]{1,0:T(8,128)(2,1)} %pad_maximum_fusion.7.refs_0_), channel_id=1, source_target_pairs={{0,4},{4,0},{1,5},{5,1},{2,6},{6,2},{3,7},{7,3}} | collective-permute-start | bytes 3145736 | tf_op jit(solution)/shard_map/ppermute | solution.py:422
  24.2 64.5 %collective-permute-start.32 = (bf16[1024,512]{1,0:T(8,128)(2,1)}, bf16[1024,512]{1,0:T(8,128)(2,1)}, u32[]{:S(2)}, u32[]{:S(2)}) collective-permute-start(bf16[1024,512]{1,0:T(8,128)(2,1)} %pad_maximum_fusion.8.refs_1_), channel_id=1, source_target_pairs={{0,2},{2,0},{1,3},{3,1},{4,6},{6,4},{5,7},{7,5}} | collective-permute-start | bytes 3145736 | tf_op jit(solution)/shard_map/ppermute | solution.py:419
  24.7 274.2 %collective-permute-start.34 = (bf16[1024,512]{1,0:T(8,128)(2,1)}, bf16[1024,512]{1,0:T(8,128)(2,1)}, u32[]{:S(2)}, u32[]{:S(2)}) collective-permute-start(bf16[1024,512]{1,0:T(8,128)(2,1)} %pad_maximum_fusion.8.refs_1_), channel_id=1, source_target_pairs={{0,4},{4,0},{1,5},{5,1},{2,6},{6,2},{3,7},{7,3}} | collective-permute-start | bytes 3145736 | tf_op jit(solution)/shard_map/ppermute | solution.py:422
  86.7 63.0 %collective-permute-start.2 = (bf16[192,4096]{1,0:T(8,128)(2,1)}, bf16[192,4096]{1,0:T(8,128)(2,1)S(1)}, u32[]{:S(2)}, u32[]{:S(2)}) collective-permute-start(bf16[192,4096]{1,0:T(8,128)(2,1)} %get-tuple-element.216), channel_id=1, source_target_pairs={{0,2},{2,0},{1,3},{3,1},{4,6},{6,4},{5,7},{7,5}} | collective-permute-start | bytes 4718600 | tf_op jit(solution)/shard_map/ppermute | solution.py:419
  88.7 61.6 %collective-permute-start.3 = (bf16[192,4096]{1,0:T(8,128)(2,1)}, bf16[192,4096]{1,0:T(8,128)(2,1)}, u32[]{:S(2)}, u32[]{:S(2)}) collective-permute-start(bf16[192,4096]{1,0:T(8,128)(2,1)} %get-tuple-element.215), channel_id=1, source_target_pairs={{0,4},{4,0},{1,5},{5,1},{2,6},{6,2},{3,7},{7,3}} | collective-permute-start | bytes 4718600 | tf_op jit(solution)/shard_map/ppermute | solution.py:422
  96.7 58.1 %collective-permute-start.1 = (bf16[768,4096]{1,0:T(8,128)(2,1)}, bf16[768,4096]{1,0:T(8,128)(2,1)}, u32[]{:S(2)}, u32[]{:S(2)}) collective-permute-start(bf16[768,4096]{1,0:T(8,128)(2,1)} %slice_bitcast_fusion.1), channel_id=1, source_target_pairs={{0,1},{2,3},{4,5},{6,7}} | collective-permute-start | bytes 18874376 | tf_op jit(solution)/shard_map/ppermute | solution.py:484
  149.7 150.3 %collective-permute-start.35 = (bf16[1024,512]{1,0:T(8,128)(2,1)}, bf16[1024,512]{1,0:T(8,128)(2,1)S(1)}, u32[]{:S(2)}, u32[]{:S(2)}) collective-permute-start(bf16[1024,512]{1,0:T(8,128)(2,1)} %collective-permute-done.33.refs_4_), channel_id=1, source_target_pairs={{0,2},{2,0},{1,3},{3,1},{4,6},{6,4},{5,7},{7,5}} | collective-permute-start | bytes 3145736 | tf_op jit(solution)/shard_map/ppermute | solution.py:419
  294.4 54.6 %collective-permute-start.16 = (bf16[192,4096]{1,0:T(8,128)(2,1)S(1)}, bf16[192,4096]{1,0:T(8,128)(2,1)S(1)}, u32[]{:S(2)}, u32[]{:S(2)}) collective-permute-start(bf16[192,4096]{1,0:T(8,128)(2,1)S(1)} %pad_maximum_fusion.2), channel_id=1, source_target_pairs={{0,4},{4,0},{1,5},{5,1},{2,6},{6,2},{3,7},{7,3}} | collective-permute-start | bytes 4718600 | tf_op jit(solution)/shard_map/ppermute | solution.py:422
  298.9 117.8 %collective-permute-start.13 = (bf16[192,4096]{1,0:T(8,128)(2,1)}, bf16[192,4096]{1,0:T(8,128)(2,1)S(1)}, u32[]{:S(2)}, u32[]{:S(2)}) collective-permute-start(bf16[192,4096]{1,0:T(8,128)(2,1)} %get-tuple-element.109), channel_id=1, source_target_pairs={{0,2},{2,0},{1,3},{3,1},{4,6},{6,4},{5,7},{7,5}} | collective-permute-start | bytes 4718600 | tf_op jit(solution)/shard_map/ppermute | solution.py:419
  300.0 117.2 %collective-permute-start.14 = (bf16[192,4096]{1,0:T(8,128)(2,1)}, bf16[192,4096]{1,0:T(8,128)(2,1)S(1)}, u32[]{:S(2)}, u32[]{:S(2)}) collective-permute-start(bf16[192,4096]{1,0:T(8,128)(2,1)} %get-tuple-element.110), channel_id=1, source_target_pairs={{0,4},{4,0},{1,5},{5,1},{2,6},{6,2},{3,7},{7,3}} | collective-permute-start | bytes 4718600 | tf_op jit(solution)/shard_map/ppermute | solution.py:422
  315.3 135.1 %collective-permute-start.21 = (bf16[192,4096]{1,0:T(8,128)(2,1)}, bf16[192,4096]{1,0:T(8,128)(2,1)S(1)}, u32[]{:S(2)}, u32[]{:S(2)}) collective-permute-start(bf16[192,4096]{1,0:T(8,128)(2,1)} %pad_maximum_fusion.3), channel_id=1, source_target_pairs={{0,2},{2,0},{1,3},{3,1},{4,6},{6,4},{5,7},{7,5}} | collective-permute-start | bytes 4718600 | tf_op jit(solution)/shard_map/ppermute | solution.py:419
  330.1 121.9 %collective-permute-start.22 = (bf16[192,4096]{1,0:T(8,128)(2,1)}, bf16[192,4096]{1,0:T(8,128)(2,1)}, u32[]{:S(2)}, u32[]{:S(2)}) collective-permute-start(bf16[192,4096]{1,0:T(8,128)(2,1)} %pad_maximum_fusion.4), channel_id=1, source_target_pairs={{0,4},{4,0},{1,5},{5,1},{2,6},{6,2},{3,7},{7,3}} | collective-permute-start | bytes 4718600 | tf_op jit(solution)/shard_map/ppermute | solution.py:422
  349.0 234.0 %collective-permute-start.37 = (bf16[1024,512]{1,0:T(8,128)(2,1)}, bf16[1024,512]{1,0:T(8,128)(2,1)}, u32[]{:S(2)}, u32[]{:S(2)}) collective-permute-start(bf16[1024,512]{1,0:T(8,128)(2,1)} %collective-permute-done.31.refs_2_), channel_id=1, source_target_pairs={{0,1},{1,0},{2,3},{3,2},{4,5},{5,4},{6,7},{7,6}} | collective-permute-start | bytes 3145736 | tf_op jit(solution)/shard_map/ppermute | solution.py:425
  416.7 166.3 %collective-permute-start.38 = (bf16[1024,512]{1,0:T(8,128)(2,1)}, bf16[1024,512]{1,0:T(8,128)(2,1)}, u32[]{:S(2)}, u32[]{:S(2)}) collective-permute-start(bf16[1024,512]{1,0:T(8,128)(2,1)} %collective-permute-done.32.refs_3_), channel_id=1, source_target_pairs={{0,1},{1,0},{2,3},{3,2},{4,5},{5,4},{6,7},{7,6}} | collective-permute-start | bytes 3145736 | tf_op jit(solution)/shard_map/ppermute | solution.py:425
  417.2 166.3 %collective-permute-start.39 = (bf16[1024,512]{1,0:T(8,128)(2,1)}, bf16[1024,512]{1,0:T(8,128)(2,1)}, u32[]{:S(2)}, u32[]{:S(2)}) collective-permute-start(bf16[1024,512]{1,0:T(8,128)(2,1)} %collective-permute-done.33.refs_4_), channel_id=1, source_target_pairs={{0,1},{1,0},{2,3},{3,2},{4,5},{5,4},{6,7},{7,6}} | collective-permute-start | bytes 3145736 | tf_op jit(solution)/shard_map/ppermute | solution.py:425
  589.3 100.6 %collective-permute-start.43 = (bf16[192,4096]{1,0:T(8,128)(2,1)}, bf16[192,4096]{1,0:T(8,128)(2,1)}, u32[]{:S(2)}, u32[]{:S(2)}) collective-permute-start(bf16[192,4096]{1,0:T(8,128)(2,1)} %get-tuple-element.194), channel_id=1, source_target_pairs={{0,2},{2,0},{1,3},{3,1},{4,6},{6,4},{5,7},{7,5}} | collective-permute-start | bytes 4718600 | tf_op jit(solution)/shard_map/ppermute | solution.py:419
  590.2 99.7 %collective-permute-start.44 = (bf16[192,4096]{1,0:T(8,128)(2,1)}, bf16[192,4096]{1,0:T(8,128)(2,1)}, u32[]{:S(2)}, u32[]{:S(2)}) collective-permute-start(bf16[192,4096]{1,0:T(8,128)(2,1)} %get-tuple-element.193), channel_id=1, source_target_pairs={{0,4},{4,0},{1,5},{5,1},{2,6},{6,2},{3,7},{7,3}} | collective-permute-start | bytes 4718600 | tf_op jit(solution)/shard_map/ppermute | solution.py:422
  600.9 166.4 %collective-permute-start.47 = (bf16[3,768,512]{2,1,0:T(8,128)(2,1)}, bf16[3,768,512]{2,1,0:T(8,128)(2,1)S(1)}, u32[]{:S(2)}, u32[]{:S(2)}) collective-permute-start(bf16[3,768,512]{2,1,0:T(8,128)(2,1)} %pad_maximum_fusion), channel_id=1, source_target_pairs={{0,1},{3,3},{4,5},{7,7}} | collective-permute-start | bytes 7077896 | tf_op jit(solution)/shard_map/ppermute | solution.py:595
  620.9 147.1 %collective-permute-start.48 = (bf16[3,768,512]{2,1,0:T(8,128)(2,1)}, bf16[3,768,512]{2,1,0:T(8,128)(2,1)S(1)}, u32[]{:S(2)}, u32[]{:S(2)}) collective-permute-start(bf16[3,768,512]{2,1,0:T(8,128)(2,1)} %pad_maximum_fusion), channel_id=1, source_target_pairs={{2,1},{1,3},{6,5},{5,7}} | collective-permute-start | bytes 7077896 | tf_op jit(solution)/shard_map/ppermute | solution.py:595
  829.8 70.6 %collective-permute-start.60 = (bf16[2,192,1024]{2,1,0:T(8,128)(2,1)}, bf16[2,192,1024]{2,1,0:T(8,128)(2,1)}, u32[]{:S(2)}, u32[]{:S(2)}) collective-permute-start(bf16[2,192,1024]{2,1,0:T(8,128)(2,1)} %pad_maximum_fusion.13), channel_id=1, source_target_pairs={{0,1},{3,3},{4,5},{7,7}} | collective-permute-start | bytes 2359304 | tf_op jit(solution)/shard_map/ppermute | solution.py:595
  832.0 68.5 %collective-permute-start.61 = (bf16[2,192,1024]{2,1,0:T(8,128)(2,1)}, bf16[2,192,1024]{2,1,0:T(8,128)(2,1)}, u32[]{:S(2)}, u32[]{:S(2)}) collective-permute-start(bf16[2,192,1024]{2,1,0:T(8,128)(2,1)} %pad_maximum_fusion.13), channel_id=1, source_target_pairs={{2,1},{1,3},{6,5},{5,7}} | collective-permute-start | bytes 2359304 | tf_op jit(solution)/shard_map/ppermute | solution.py:595
  835.5 74.8 %collective-permute-start.57 = (bf16[2,192,1024]{2,1,0:T(8,128)(2,1)}, bf16[2,192,1024]{2,1,0:T(8,128)(2,1)}, u32[]{:S(2)}, u32[]{:S(2)}) collective-permute-start(bf16[2,192,1024]{2,1,0:T(8,128)(2,1)} %pad_maximum_fusion.12), channel_id=1, source_target_pairs={{0,1},{3,3},{4,5},{7,7}} | collective-permute-start | bytes 2359304 | tf_op jit(solution)/shard_map/ppermute | solution.py:595
  842.7 67.5 %collective-permute-start.58 = (bf16[2,192,1024]{2,1,0:T(8,128)(2,1)}, bf16[2,192,1024]{2,1,0:T(8,128)(2,1)}, u32[]{:S(2)}, u32[]{:S(2)}) collective-permute-start(bf16[2,192,1024]{2,1,0:T(8,128)(2,1)} %pad_maximum_fusion.12), channel_id=1, source_target_pairs={{2,1},{1,3},{6,5},{5,7}} | collective-permute-start | bytes 2359304 | tf_op jit(solution)/shard_map/ppermute | solution.py:595
  (93 other events, 2437.6 us)
where the time goes:
time: 946 us; the launch traced here: 936 us
  matrix products  346 us (37%)
  waiting for transfers between devices  197 us (21%)
  Pallas kernels  143 us (15%)
  local copies, waits for them, and re-layouts  110 us (12%)
  starting transfers between devices  77 us (8%)
  other arithmetic  60.6 us (6%)
    dot_general x21, matrix products, matmul(): return jnp.dot(left, right, preferred_element_type=jnp.float32)  346 us
    ppermute x24, waiting for transfers between devices, over_y(): return lax.ppermute(value, 'b', SWAP)  140 us
    ppermute x21, waiting for transfers between devices, over_x(): return lax.ppermute(value, 'a', SWAP)  57.3 us
    pallas_call x1, Pallas kernels, last_rows(): pl.pallas_call(functools.partial(tail_kernel, kv_heads), grid=(1,), in_sp...  54.6 us
    pallas_call x3, Pallas kernels, attention(): pl.pallas_call(functools.partial(attention_kernel, q_block, group), grid_...  47.7 us
    unnamed x122, local copies, waits for them, and re-layouts  38.9 us
    pallas_call x3, Pallas kernels, keys_values(): pl.pallas_call(kv_kernel, in_specs=[pl.BlockSpec(memory_space=pltpu.SMEM)...  28 us
    convert_element_type x9, other arithmetic, add_rounded(): (left.astype(jnp.float32) + right.astype(jnp.float32)).astype(jnp.bfloat16)  23.9 us
  transfers between devices with their start and end apart: 62, of which 18 were waited for; matrix products, arithmetic and copies ran while one was open for 51% of the time, Pallas kernels for 15%

commit v1 on v0

--- a/solution.py
+++ b/solution.py
@@ -337,26 +337,29 @@
     )(*finals, *kvs, gain_a, gain_m, cos_row, sin_row, w_query, w_out, w_gate, w_up, w_down)
 
 
+def write_heads(k_ref, v_ref, low, high):
+    rows, kv2 = low.shape
+    for ref, start in ((k_ref, 0), (v_ref, kv2 // 2)):
+        heads = jnp.concatenate([low[:, start:start + kv2 // 2], high[:, start:start + kv2 // 2]], axis=1)
+        ref[0, 0, 0] = heads.reshape(rows, kv2 // HEAD_DIM, HEAD_DIM)
+
+
 def first_cut_kernel(where_ref, near_ref, far_ref, k_ref, v_ref):
-    kv_width = near_ref.shape[-1] // 2
     own_low = where_ref[0] == 0
     near, far = near_ref[0], far_ref[0]
-    low, high = jnp.where(own_low, near, far), jnp.where(own_low, far, near)
-    k_ref[0, 0, :, :kv_width] = low[:, :kv_width]
-    k_ref[0, 0, :, kv_width:] = high[:, :kv_width]
-    v_ref[0, 0, :, :kv_width] = low[:, kv_width:]
-    v_ref[0, 0, :, kv_width:] = high[:, kv_width:]
+    write_heads(k_ref, v_ref, jnp.where(own_low, near, far), jnp.where(own_low, far, near))
 
 
 def first_cut(near, far, where):
     n_chunk, seq_len, columns = near.shape
     rows = seq_len // 2
+    heads = columns // HEAD_DIM
     source = pl.BlockSpec((1, rows, columns), lambda c, j, where_ref: (c, j, 0))
-    target = pl.BlockSpec((1, 1, rows, columns), lambda c, j, where_ref: (0, c, j, 0))
+    target = pl.BlockSpec((1, 1, 1, rows, heads, HEAD_DIM), lambda c, j, where_ref: (0, 0, c, j, 0, 0))
     return pl.pallas_call(
         first_cut_kernel,
         grid_spec=pltpu.PrefetchScalarGridSpec(num_scalar_prefetch=1, grid=(n_chunk, 2), in_specs=[source] * 2, out_specs=[target] * 2),
-        out_shape=[jax.ShapeDtypeStruct((2, n_chunk, seq_len, columns), jnp.bfloat16)] * 2,
+        out_shape=[jax.ShapeDtypeStruct((1, 2, n_chunk, seq_len, heads, HEAD_DIM), jnp.bfloat16)] * 2,
         compiler_params=pltpu.CompilerParams(vmem_limit_bytes=32 * 1024 * 1024),
         cost_estimate=pl.CostEstimate(flops=1_000_000_000, bytes_accessed=19_000_000, transcendentals=0),
     )(where, near, far)
@@ -364,16 +367,11 @@
 
 def second_cut_kernel(where_ref, near_ref, far_ref, k_in, v_in, k_ref, v_ref):
     columns = near_ref.shape[-1] // 2
-    kv_width = columns // 2
 
     def put(source):
         mine, other = source[:, :columns], source[:, columns:]
         own_low = where_ref[0] + pl.program_id(0) - 2 * where_ref[0] * pl.program_id(0) == 0
-        low, high = jnp.where(own_low, mine, other), jnp.where(own_low, other, mine)
-        k_ref[0, 0, :, :kv_width] = low[:, :kv_width]
-        k_ref[0, 0, :, kv_width:] = high[:, :kv_width]
-        v_ref[0, 0, :, :kv_width] = low[:, kv_width:]
-        v_ref[0, 0, :, kv_width:] = high[:, kv_width:]
+        write_heads(k_ref, v_ref, jnp.where(own_low, mine, other), jnp.where(own_low, other, mine))
 
     @pl.when(pl.program_id(0) == 0)
     def _():
@@ -384,27 +382,28 @@
         put(far_ref[0])
 
 
-def second_cut(near, far, where, k_flat, v_flat, request):
+def second_cut(near, far, where, k_cache, v_cache, request):
     _, rows, columns = near.shape
     block = rows // 2
+    heads = columns // 2 // HEAD_DIM
 
     def place(i, j, half, where_ref):
         along_x = where_ref[0] + i - 2 * where_ref[0] * i
         along_y = where_ref[1] + j - 2 * where_ref[1] * j
-        return 1, request, (1 - half) * (2 * along_x + along_y) + half * (4 + 2 * along_y + along_x), 0
+        return 0, 1, request, (1 - half) * (2 * along_x + along_y) + half * (4 + 2 * along_y + along_x), 0, 0
 
     source = pl.BlockSpec((1, block, columns), lambda i, j, half, where_ref: (j, half, 0))
-    target = pl.BlockSpec((1, 1, block, columns // 2), place)
+    target = pl.BlockSpec((1, 1, 1, block, heads, HEAD_DIM), place)
     whole = pl.BlockSpec(memory_space=pl.ANY)
     return pl.pallas_call(
         second_cut_kernel,
         grid_spec=pltpu.PrefetchScalarGridSpec(
             num_scalar_prefetch=1, grid=(2, 2, 2), in_specs=[source] * 2 + [whole] * 2, out_specs=[target] * 2),
-        out_shape=[jax.ShapeDtypeStruct(k_flat.shape, jnp.bfloat16)] * 2,
+        out_shape=[jax.ShapeDtypeStruct(k_cache.shape, jnp.bfloat16)] * 2,
         input_output_aliases={3: 0, 4: 1},
         compiler_params=pltpu.CompilerParams(vmem_limit_bytes=32 * 1024 * 1024),
         cost_estimate=pl.CostEstimate(flops=300_000_000, bytes_accessed=5_000_000, transcendentals=0),
-    )(where, near, far, k_flat, v_flat)
+    )(where, near, far, k_cache, v_cache)
 
 
 def solution(mesh):
@@ -502,9 +501,12 @@
             v = matmul(normed, w_value[0]).astype(jnp.bfloat16)
             return q, k, v
 
-        def attend(q, k, v):
-            mix, k_rot = attention(q, k, v, cos_t, sin_t, order)
-            return matmul(mix, w_out[0]).astype(jnp.bfloat16), jnp.concatenate([k_rot, v], axis=1)
+        def attend(qkv):
+            mix, k_rot = attention(*qkv, cos_t, sin_t, order)
+            return mix, jnp.concatenate([k_rot, qkv[2]], axis=1)
+
+        def out_of(mix):
+            return matmul(mix, w_out[0]).astype(jnp.bfloat16)
 
         def gate_of(normed):
             return matmul(normed, w_gate[0]).astype(jnp.bfloat16)
@@ -525,7 +527,8 @@
         qkv0 = project(x0)
         moved1 = take(hold(embeds, qkv0)[0, n_chunk + 1])
         top_d, bottom_d = over_x(hold(top_y, qkv0)), over_y(hold(bottom_x, qkv0))
-        p0, kv0_0 = attend(*qkv0)
+        mix0, kv0_0 = attend(qkv0)
+        p0 = out_of(mix0)
         own_x0 = own_rows(x0)
         send = send_parts(p0)
         wide0 = send_wide(send)
@@ -533,46 +536,48 @@
         moved2 = take(hold(embeds, send)[0, n_chunk + 2])
         embeds_1, moved1 = hold((embeds, moved1), send, moved1)
         x1 = hidden_of(embeds_1[0, 1], moved1)
-        p1, kv0_1 = attend(*project(x1))
+        qkv1 = project(x1)
+        sums0 = add_wide(p0, hold(wide0, qkv1))
+        narrow0 = send_narrow(sums0)
+        mix1, kv0_1 = attend(hold(qkv1, sums0))
+        own1_0 = add_narrow(own_x0, sums0, hold(narrow0, mix1))
+        h0 = rms_norm(own1_0, mlp_gain[0])
+        near_got0 = gather_near(h0)
+        p1 = out_of(hold(mix1, h0))
         own_x1 = own_rows(x1)
         send = send_parts(p1)
         wide1 = send_wide(send)
-
-        sums0 = add_wide(p0, hold(wide0, send))
-        narrow0 = send_narrow(sums0)
-
-        embeds_2, moved2 = hold((embeds, moved2), sums0, moved2)
+        near0 = join_near(h0, hold(near_got0, send))
+        far0 = gather_far(near0)
+
+        embeds_2, moved2 = hold((embeds, moved2), near0, moved2)
         x2 = hidden_of(embeds_2[0, 2], moved2)
-        p2, kv0_2 = attend(*project(x2))
+        qkv2 = project(x2)
+        mix2, kv0_2 = attend(qkv2)
+        sums1 = add_wide(p1, hold(wide1, mix2))
+        narrow1 = send_narrow(sums1)
+        p2 = out_of(hold(mix2, sums1))
         own_x2 = own_rows(x2)
-
-        sums1 = add_wide(p1, hold(wide1, p2))
-        narrow1 = send_narrow(sums1)
-        own1_0 = add_narrow(own_x0, sums0, hold(narrow0, sums1))
-        h0 = rms_norm(own1_0, mlp_gain[0])
-        near_got0 = gather_near(h0)
-
-        own1_1 = add_narrow(own_x1, sums1, hold(narrow1, h0))
+        send = send_parts(p2)
+        wide2 = send_wide(send)
+
+        normed = join_far(near0, hold(far0, send))
+        gate = gate_of(normed)
+        own1_1 = add_narrow(own_x1, sums1, hold(narrow1, gate))
         h1 = rms_norm(own1_1, mlp_gain[0])
         near_got1 = gather_near(h1)
-        near0 = join_near(h0, hold(near_got0, h1))
-        far0 = gather_far(near0)
-        send = hold(send_parts(p2), near0)
-        wide2 = send_wide(send)
-        near1 = join_near(h1, hold(near_got1, send))
+        act = act_of(hold(normed, h1), gate)
+        near1 = join_near(h1, hold(near_got1, act))
         far1 = gather_far(near1)
-
-        fetched = hold((top_x, bottom_x, top_y, bottom_y, top_d, bottom_d), near1)
-        w_mine = [w_top, w_bottom] + list(fetched)
-        w_other = [w_block(1 - s, 0), w_block(1 - s, 1)] + [across(piece) for piece in fetched]
-
-        normed = join_far(near0, hold(far0, near1))
-        act = act_of(normed, gate_of(normed))
-        sums2 = add_wide(p2, hold(wide2, act))
+        sums2 = add_wide(p2, hold(wide2, near1))
         narrow2 = send_narrow(sums2)
         d0 = down_of(hold(act, sums2))
         send = send_parts(d0)
         wide0 = send_wide(send)
+
+        fetched = hold((top_x, bottom_x, top_y, bottom_y, top_d, bottom_d), send)
+        w_mine = [w_top, w_bottom] + list(fetched)
+        w_other = [w_block(1 - s, 0), w_block(1 - s, 1)] + [across(piece) for piece in fetched]
 
         normed = join_far(near1, hold(far1, send))
         gate = gate_of(normed)
@@ -580,11 +585,11 @@
         h2 = rms_norm(own1_2, mlp_gain[0])
         near_got2 = gather_near(h2)
         act = act_of(hold(normed, h2), gate)
-        sums0 = add_wide(d0, hold(wide0, act))
+        near2 = join_near(h2, hold(near_got2, act))
+        far2 = gather_far(near2)
+        sums0 = add_wide(d0, hold(wide0, near2))
         narrow0 = send_narrow(sums0)
-        near2 = join_near(h2, hold(near_got2, sums0))
-        far2 = gather_far(near2)
-        d1 = down_of(hold(act, near2))
+        d1 = down_of(hold(act, sums0))
         send = send_parts(d1)
         wide1 = send_wide(send)
 
@@ -594,20 +599,19 @@
         def to_decode(value):
             return lax.ppermute(value, ('a', 'stage'), FROM_NEAR), lax.ppermute(value, ('a', 'stage'), FROM_FAR)
 
-        final0 = add_narrow(own1_0, sums0, hold(narrow0, send))
-        kv1_0 = keys_values_of(final0)
-        cut0 = to_decode(hold(jnp.stack([kv0_0, kv0_1, kv0_2]), kv1_0))
-
         def along_y(kv, *after):
             return over_y(hold(kv[:, 2 * kv2:], *after))
 
         def to_decode_rows(kv, got):
             return to_decode(jnp.stack([kv[:, :2 * kv2], got]))
 
-        normed = join_far(near2, hold(far2, kv1_0))
+        normed = join_far(near2, hold(far2, send))
         gate = gate_of(normed)
-        got_0 = along_y(kv1_0, gate)
-        act = act_of(normed, gate)
+        final0 = add_narrow(own1_0, sums0, hold(narrow0, gate))
+        kv1_0 = keys_values_of(final0)
+        got_0 = along_y(kv1_0)
+        cut0 = to_decode(hold(jnp.stack([kv0_0, kv0_1, kv0_2]), kv1_0))
+        act = act_of(hold(normed, kv1_0), gate)
         sums1 = add_wide(d1, hold(wide1, act))
         narrow1 = send_narrow(sums1)
         cut1_0 = to_decode_rows(kv1_0, hold(got_0, sums1))
@@ -617,11 +621,11 @@
         final1 = add_narrow(own1_1, sums1, hold(narrow1, send))
         kv1_1 = keys_values_of(final1)
         got_1 = along_y(kv1_1)
-        k_flat, v_flat = first_cut(*hold(cut0, kv1_1), where)
-        sums2 = add_wide(d2, hold(wide2, k_flat))
+        k_cache, v_cache = first_cut(*hold(cut0, kv1_1), where)
+        sums2 = add_wide(d2, hold(wide2, k_cache))
         narrow2 = send_narrow(sums2)
-        k_flat, v_flat = second_cut(*hold(cut1_0, sums2), where, k_flat, v_flat, 0)
-        final2 = add_narrow(own1_2, sums2, hold(narrow2, k_flat))
+        k_cache, v_cache = second_cut(*hold(cut1_0, sums2), where, k_cache, v_cache, 0)
+        final2 = add_narrow(own1_2, sums2, hold(narrow2, k_cache))
         kv1_2 = keys_values_of(final2)
         got_2 = along_y(kv1_2)
         cut1_1 = to_decode_rows(kv1_1, hold(got_1, kv1_2))
@@ -634,8 +638,7 @@
         last_out = jnp.where(s == 1, last_out, jnp.zeros_like(last_out))
 
         for c, cut in ((1, cut1_1), (2, cut1_2)):
-            k_flat, v_flat = second_cut(*hold(cut, last), where, k_flat, v_flat, c)
-        cache_shape = (1, 2, n_chunk, seq_len, 2 * kv_heads, HEAD_DIM)
-        return k_flat.reshape(cache_shape), v_flat.reshape(cache_shape), last_out[None]
+            k_cache, v_cache = second_cut(*hold(cut, last), where, k_cache, v_cache, c)
+        return k_cache, v_cache, last_out[None]
 
     return jax.shard_map(stage_program, mesh=mesh, in_specs=in_specs, out_specs=out_specs, check_vma=False)

time: 946 us -> 848 us (0.90)
  waiting for transfers between devices: 197 us -> 106 us
  local copies, waits for them, and re-layouts: 110 us -> 87.2 us
    ppermute x24, waiting for transfers between devices: 140 us -> 71.9 us  [over_y(): return lax.ppermute(value, 'b', SWAP)]
    ppermute x21, waiting for transfers between devices: 57.3 us -> 34.4 us  [over_x(): return lax.ppermute(value, 'a', SWAP)]
    reshape x2 -> x0, local copies, waits for them, and re-layouts: 15.4 us -> none  [the longest x1 7.69 us: stage_program(): k_flat.reshape(cache_shape)]
    unnamed x122 -> x118, local copies, waits for them, and re-layouts: 38.9 us -> 27.3 us
  transfers between devices with their start and end apart: 62 -> 62, of which waited for: 18 -> 13; matrix products, arithmetic and copies ran while one was open for 51% -> 58% of each run, Pallas kernels for 15% -> 17%
where the time goes in v1:
time: 848 us; the launch traced here: 838 us
  matrix products  350 us (41%)
  Pallas kernels  147 us (17%)
  waiting for transfers between devices  106 us (12%)
  local copies, waits for them, and re-layouts  87.2 us (10%)
  starting transfers between devices  80.4 us (9%)
  other arithmetic  65.3 us (8%)
    dot_general x21, matrix products, matmul(): return jnp.dot(left, right, preferred_element_type=jnp.float32)  350 us
    ppermute x24, waiting for transfers between devices, over_y(): return lax.ppermute(value, 'b', SWAP)  71.9 us
    pallas_call x1, Pallas kernels, last_rows(): pl.pallas_call(functools.partial(tail_kernel, kv_heads), grid=(1,), in_sp...  56.1 us
    pallas_call x3, Pallas kernels, attention(): pl.pallas_call(functools.partial(attention_kernel, q_block, group), grid_...  47.7 us
    ppermute x21, waiting for transfers between devices, over_x(): return lax.ppermute(value, 'a', SWAP)  34.4 us
    unnamed x118, local copies, waits for them, and re-layouts  27.3 us
    ppermute x21, starting transfers between devices, over_x(): return lax.ppermute(value, 'a', SWAP)  26.8 us
    convert_element_type x9, other arithmetic, add_rounded(): (left.astype(jnp.float32) + right.astype(jnp.float32)).astype(jnp.bfloat16)  26.3 us
  transfers between devices with their start and end apart: 62, of which 13 were waited for; matrix products, arithmetic and copies ran while one was open for 58% of the time, Pallas kernels for 17%

profile of v1, /device:TPU:0, one launch (start us, length us, event | category | flops | bytes accessed | tf_op | source)
XLA Modules:
  0.0 838.1 jit_solution(11928998043850663707)
XLA Ops:
  58.4 15.7 %shard_map.121 = (bf16[768,1024]{1,0:T(8,128)(2,1)S(1)}, bf16[768,256]{1,0:T(8,128)(2,1)S(1)}) custom-call(s32[8]{0:T(128)S(1)} %pad_add_fusion.1._, bf16[768,1024]{1,0:T(8,128)(2,1)S(1)} %fusion.135.q_ref, bf16[768,256]{1,0:T(8,128)(2,1)S(1)} %fusion.150.k_ref, bf16[768,256]{1,0:T(8,128)(2,1)S(1)} %fusion.159.v_ref, ...), custom_call_target="tpu_custom_call" | custom-call | flops 8999999488 | bytes 5000000 | tf_op jit(solution)/shard_map/pallas_call | solution.py:78
  74.2 10.5 %fusion.72 = bf16[768,4096]{1,0:T(8,128)(2,1)S(1)} fusion(bf16[768,1024]{1,0:T(8,128)(2,1)S(1)} %get-tuple-element.94, bf16[2,1024,4096]{2,1,0:T(8,128)(2,1)} %wo_hbm.1), kind=kOutput, calls=%fused_computation.78 | convolution fusion | flops 6445596672 | bytes 16252928 | tf_op jit(solution)/shard_map/dot_general | solution.py:34
  111.0 9.1 %fusion.138.q_ref = bf16[768,1024]{1,0:T(8,128)(2,1)S(1)} fusion(bf16[2,4096,1024]{2,1,0:T(8,128)(2,1)} %wq_hbm.1, bf16[768,4096]{1,0:T(8,128)(2,1)S(1)} %get-tuple-element.192, f32[768]{0:T(1024)S(1)} %add_rsqrt_fusion.1, f32[4096]{0:T(1024)S(1)} %bitcast.174), kind=kOutput, calls=%fused_computation.155 | convolution fusion | flops 6455820288 | bytes 16272384 | tf_op jit(solution)/shard_map/dot_general | solution.py:34
  125.9 15.9 %shard_map.122 = (bf16[768,1024]{1,0:T(8,128)(2,1)S(1)}, bf16[768,256]{1,0:T(8,128)(2,1)S(1)}) custom-call(s32[8]{0:T(128)S(1)} %pad_add_fusion.1._, bf16[768,1024]{1,0:T(8,128)(2,1)S(1)} %fusion.138.q_ref, bf16[768,256]{1,0:T(8,128)(2,1)S(1)} %fusion.153.k_ref, bf16[768,256]{1,0:T(8,128)(2,1)S(1)} %fusion.162.v_ref, ...), custom_call_target="tpu_custom_call" | custom-call | flops 8999999488 | bytes 5000000 | tf_op jit(solution)/shard_map/pallas_call | solution.py:78
  147.8 10.5 %fusion.75 = bf16[768,4096]{1,0:T(8,128)(2,1)S(1)} fusion(bf16[768,1024]{1,0:T(8,128)(2,1)S(1)} %get-tuple-element.107, bf16[2,1024,4096]{2,1,0:T(8,128)(2,1)} %wo_hbm.1), kind=kOutput, calls=%fused_computation.79 | convolution fusion | flops 6445596672 | bytes 16252928 | tf_op jit(solution)/shard_map/dot_general | solution.py:34
  171.6 9.3 %fusion.141.q_ref = bf16[768,1024]{1,0:T(8,128)(2,1)S(1)} fusion(bf16[2,4096,1024]{2,1,0:T(8,128)(2,1)} %wq_hbm.1, bf16[768,4096]{1,0:T(8,128)(2,1)S(1)} %get-tuple-element.188, f32[768]{0:T(1024)S(1)} %add_rsqrt_fusion, f32[4096]{0:T(1024)S(1)} %bitcast.175), kind=kOutput, calls=%fused_computation.156 | convolution fusion | flops 6455820288 | bytes 16272384 | tf_op jit(solution)/shard_map/dot_general | solution.py:34
  188.3 16.1 %shard_map.123 = (bf16[768,1024]{1,0:T(8,128)(2,1)S(1)}, bf16[768,256]{1,0:T(8,128)(2,1)S(1)}) custom-call(s32[8]{0:T(128)S(1)} %pad_add_fusion.1._, bf16[768,1024]{1,0:T(8,128)(2,1)S(1)} %fusion.141.q_ref, bf16[768,256]{1,0:T(8,128)(2,1)S(1)} %fusion.156.k_ref, bf16[768,256]{1,0:T(8,128)(2,1)S(1)} %fusion.165.v_ref, ...), custom_call_target="tpu_custom_call" | custom-call | flops 8999999488 | bytes 5000000 | tf_op jit(solution)/shard_map/pallas_call | solution.py:78
  211.4 10.5 %fusion.78 = bf16[768,4096]{1,0:T(8,128)(2,1)S(1)} fusion(bf16[768,1024]{1,0:T(8,128)(2,1)S(1)} %get-tuple-element.115, bf16[2,1024,4096]{2,1,0:T(8,128)(2,1)} %wo_hbm.1), kind=kOutput, calls=%fused_computation.80 | convolution fusion | flops 6445596672 | bytes 16252928 | tf_op jit(solution)/shard_map/dot_general | solution.py:34
  242.4 30.9 %fusion.81 = bf16[768,3584]{1,0:T(8,128)(2,1)} fusion(bf16[768,4096]{1,0:T(8,128)(2,1)} %constant_dynamic-update-slice_fusion, bf16[2,4096,3584]{2,1,0:T(8,128)(2,1)} %wg_hbm.1), kind=kOutput, calls=%fused_computation.81 | convolution fusion | flops 22551330816 | bytes 41156608 | tf_op jit(solution)/shard_map/dot_general | solution.py:34
  282.0 32.3 %fusion.50 = bf16[768,3584]{1,0:T(8,128)(2,1)} fusion(bf16[768,3584]{1,0:T(8,128)(2,1)} %fusion.81, bf16[768,4096]{1,0:T(8,128)(2,1)} %constant_dynamic-update-slice_fusion, bf16[2,4096,3584]{2,1,0:T(8,128)(2,1)} %wu_hbm.1), kind=kOutput, calls=%fused_computation.62 | convolution fusion | flops 22573350912 | bytes 46661632 | tf_op jit(solution)/shard_map/dot_general | solution.py:34
  325.5 29.3 %fusion.63 = bf16[768,4096]{1,0:T(8,128)(2,1)} fusion(bf16[768,3584]{1,0:T(8,128)(2,1)} %fusion.50, bf16[2,3584,4096]{2,1,0:T(8,128)(2,1)} %wd_hbm.1), kind=kOutput, calls=%fused_computation.75 | convolution fusion | flops 22551724032 | bytes 41156608 | tf_op jit(solution)/shard_map/dot_general | solution.py:34
  363.4 11.3 %collective-permute-done.21 = bf16[192,4096]{1,0:T(8,128)(2,1)} collective-permute-done((bf16[192,4096]{1,0:T(8,128)(2,1)}, bf16[192,4096]{1,0:T(8,128)(2,1)}, u32[]{:S(2)}, u32[]{:S(2)}) %collective-permute-start.21) | collective-permute-done | bytes 1572896 | tf_op jit(solution)/shard_map/ppermute | solution.py:418
  375.5 20.7 %collective-permute-done.22 = bf16[192,4096]{1,0:T(8,128)(2,1)S(1)} collective-permute-done((bf16[192,4096]{1,0:T(8,128)(2,1)}, bf16[192,4096]{1,0:T(8,128)(2,1)S(1)}, u32[]{:S(2)}, u32[]{:S(2)}) %collective-permute-start.22) | collective-permute-done | bytes 1572896 | tf_op jit(solution)/shard_map/ppermute | solution.py:421
  402.1 31.1 %fusion.84 = bf16[768,3584]{1,0:T(8,128)(2,1)} fusion(bf16[768,4096]{1,0:T(8,128)(2,1)} %constant_dynamic-update-slice_fusion.6, bf16[2,4096,3584]{2,1,0:T(8,128)(2,1)} %wg_hbm.1), kind=kOutput, calls=%fused_computation.82 | convolution fusion | flops 22551330816 | bytes 41156608 | tf_op jit(solution)/shard_map/dot_general | solution.py:34
  437.3 32.1 %fusion.49 = bf16[768,3584]{1,0:T(8,128)(2,1)} fusion(bf16[768,3584]{1,0:T(8,128)(2,1)} %fusion.84, bf16[768,4096]{1,0:T(8,128)(2,1)} %constant_dynamic-update-slice_fusion.6, bf16[2,4096,3584]{2,1,0:T(8,128)(2,1)} %wu_hbm.1), kind=kOutput, calls=%fused_computation.61 | convolution fusion | flops 22573350912 | bytes 46661632 | tf_op jit(solution)/shard_map/dot_general | solution.py:34
  478.3 29.7 %fusion.66 = bf16[768,4096]{1,0:T(8,128)(2,1)} fusion(bf16[768,3584]{1,0:T(8,128)(2,1)} %fusion.49, bf16[2,3584,4096]{2,1,0:T(8,128)(2,1)} %wd_hbm.1), kind=kOutput, calls=%fused_computation.76 | convolution fusion | flops 22551724032 | bytes 41156608 | tf_op jit(solution)/shard_map/dot_general | solution.py:34
  518.0 14.2 %collective-permute-done.29 = bf16[96,4096]{1,0:T(8,128)(2,1)S(1)} collective-permute-done((bf16[96,4096]{1,0:T(8,128)(2,1)S(1)}, bf16[96,4096]{1,0:T(8,128)(2,1)S(1)}, u32[]{:S(2)}, u32[]{:S(2)}) %collective-permute-start.29) | collective-permute-done | bytes 786464 | tf_op jit(solution)/shard_map/ppermute | solution.py:421
  532.7 30.8 %fusion.87 = bf16[768,3584]{1,0:T(8,128)(2,1)} fusion(bf16[768,4096]{1,0:T(8,128)(2,1)} %copy-done.47, bf16[2,4096,3584]{2,1,0:T(8,128)(2,1)} %wg_hbm.1), kind=kOutput, calls=%fused_computation.83 | convolution fusion | flops 22551330816 | bytes 41156608 | tf_op jit(solution)/shard_map/dot_general | solution.py:34
  579.2 32.3 %fusion.48 = bf16[768,3584]{1,0:T(8,128)(2,1)} fusion(bf16[768,3584]{1,0:T(8,128)(2,1)} %fusion.87, bf16[768,4096]{1,0:T(8,128)(2,1)} %copy-done.47, bf16[2,4096,3584]{2,1,0:T(8,128)(2,1)} %wu_hbm.1), kind=kOutput, calls=%fused_computation.60 | convolution fusion | flops 22573350912 | bytes 46661632 | tf_op jit(solution)/shard_map/dot_general | solution.py:34
  619.8 29.3 %fusion.69 = bf16[768,4096]{1,0:T(8,128)(2,1)} fusion(bf16[768,3584]{1,0:T(8,128)(2,1)} %fusion.48, bf16[2,3584,4096]{2,1,0:T(8,128)(2,1)} %wd_hbm.1), kind=kOutput, calls=%fused_computation.77 | convolution fusion | flops 22551724032 | bytes 41156608 | tf_op jit(solution)/shard_map/dot_general | solution.py:34
  657.2 19.4 %collective-permute-done.53 = bf16[192,1024]{1,0:T(8,128)(2,1)S(1)} collective-permute-done((bf16[192,1024]{1,0:T(8,128)(2,1)S(1)}, bf16[192,1024]{1,0:T(8,128)(2,1)S(1)}, u32[]{:S(2)}, u32[]{:S(2)}) %collective-permute-start.53) | collective-permute-done | bytes 393248 | tf_op jit(solution)/shard_map/ppermute | solution.py:421
  696.7 17.8 %collective-permute-done.45 = bf16[192,4096]{1,0:T(8,128)(2,1)S(1)} collective-permute-done((bf16[192,4096]{1,0:T(8,128)(2,1)}, bf16[192,4096]{1,0:T(8,128)(2,1)S(1)}, u32[]{:S(2)}, u32[]{:S(2)}) %collective-permute-start.45) | collective-permute-done | bytes 1572896 | tf_op jit(solution)/shard_map/ppermute | solution.py:418
  727.1 12.0 %collective-permute-done.51 = bf16[96,4096]{1,0:T(8,128)(2,1)S(1)} collective-permute-done((bf16[96,4096]{1,0:T(8,128)(2,1)S(1)}, bf16[96,4096]{1,0:T(8,128)(2,1)S(1)}, u32[]{:S(2)}, u32[]{:S(2)}) %collective-permute-start.51) | collective-permute-done | bytes 786464 | tf_op jit(solution)/shard_map/ppermute | solution.py:421
  767.0 56.1 %shard_map.129 = bf16[8,4096]{1,0:T(8,128)(2,1)} custom-call(bf16[192,4096]{1,0:T(8,128)(2,1)} %fusion.108.x_ref.x0_ref, bf16[192,4096]{1,0:T(8,128)(2,1)} %fusion.112.x_ref.x1_ref, bf16[192,4096]{1,0:T(8,128)(2,1)} %fusion.116.x_ref.x2_ref, bf16[192,2048]{1,0:T(8,128)(2,1)} %copy-done.7, bf16[192,2048]{1,0:T(8,128)(2,1)} %copy-done.8, ...), custom_call_target="tpu_custom_call" | custom-call | flops 8999999488 | bytes 60000000 | tf_op jit(solution)/shard_map/pallas_call | solution.py:308
  (340 shorter events, 309.0 us)
Async XLA Ops:
  19.6 339.1 %collective-permute-start.31 = (bf16[1024,512]{1,0:T(8,128)(2,1)}, bf16[1024,512]{1,0:T(8,128)(2,1)}, u32[]{:S(2)}, u32[]{:S(2)}) collective-permute-start(bf16[1024,512]{1,0:T(8,128)(2,1)} %pad_maximum_fusion.7.refs_0_), channel_id=1, source_target_pairs={{0,2},{2,0},{1,3},{3,1},{4,6},{6,4},{5,7},{7,5}} | collective-permute-start | bytes 3145736 | tf_op jit(solution)/shard_map/ppermute | solution.py:418
  21.9 67.3 %collective-permute-start.33 = (bf16[1024,512]{1,0:T(8,128)(2,1)}, bf16[1024,512]{1,0:T(8,128)(2,1)S(1)}, u32[]{:S(2)}, u32[]{:S(2)}) collective-permute-start(bf16[1024,512]{1,0:T(8,128)(2,1)} %pad_maximum_fusion.7.refs_0_), channel_id=1, source_target_pairs={{0,4},{4,0},{1,5},{5,1},{2,6},{6,2},{3,7},{7,3}} | collective-permute-start | bytes 3145736 | tf_op jit(solution)/shard_map/ppermute | solution.py:421
  23.5 72.5 %collective-permute-start.32 = (bf16[1024,512]{1,0:T(8,128)(2,1)S(1)}, bf16[1024,512]{1,0:T(8,128)(2,1)S(1)}, u32[]{:S(2)}, u32[]{:S(2)}) collective-permute-start(bf16[1024,512]{1,0:T(8,128)(2,1)S(1)} %pad_maximum_fusion.8.refs_1_), channel_id=1, source_target_pairs={{0,2},{2,0},{1,3},{3,1},{4,6},{6,4},{5,7},{7,5}} | collective-permute-start | bytes 3145736 | tf_op jit(solution)/shard_map/ppermute | solution.py:418
  53.2 48.7 %collective-permute-start.4 = (bf16[768,4096]{1,0:T(8,128)(2,1)}, bf16[768,4096]{1,0:T(8,128)(2,1)}, u32[]{:S(2)}, u32[]{:S(2)}) collective-permute-start(bf16[768,4096]{1,0:T(8,128)(2,1)} %slice_bitcast_fusion), channel_id=1, source_target_pairs={{0,1},{2,3},{4,5},{6,7}} | collective-permute-start | bytes 18874376 | tf_op jit(solution)/shard_map/ppermute | solution.py:483
  96.0 70.5 %collective-permute-start.1 = (bf16[768,4096]{1,0:T(8,128)(2,1)}, bf16[768,4096]{1,0:T(8,128)(2,1)}, u32[]{:S(2)}, u32[]{:S(2)}) collective-permute-start(bf16[768,4096]{1,0:T(8,128)(2,1)} %slice_bitcast_fusion.1), channel_id=1, source_target_pairs={{0,1},{2,3},{4,5},{6,7}} | collective-permute-start | bytes 18874376 | tf_op jit(solution)/shard_map/ppermute | solution.py:483
  161.9 46.6 %collective-permute-start.9 = (bf16[192,4096]{1,0:T(8,128)(2,1)}, bf16[192,4096]{1,0:T(8,128)(2,1)}, u32[]{:S(2)}, u32[]{:S(2)}) collective-permute-start(bf16[192,4096]{1,0:T(8,128)(2,1)} %get-tuple-element.218), channel_id=1, source_target_pairs={{0,2},{2,0},{1,3},{3,1},{4,6},{6,4},{5,7},{7,5}} | collective-permute-start | bytes 4718600 | tf_op jit(solution)/shard_map/ppermute | solution.py:418
  225.5 92.7 %collective-permute-start.11 = (bf16[192,4096]{1,0:T(8,128)(2,1)}, bf16[192,4096]{1,0:T(8,128)(2,1)S(1)}, u32[]{:S(2)}, u32[]{:S(2)}) collective-permute-start(bf16[192,4096]{1,0:T(8,128)(2,1)} %get-tuple-element.214), channel_id=1, source_target_pairs={{0,2},{2,0},{1,3},{3,1},{4,6},{6,4},{5,7},{7,5}} | collective-permute-start | bytes 4718600 | tf_op jit(solution)/shard_map/ppermute | solution.py:418
  226.0 93.4 %collective-permute-start.12 = (bf16[192,4096]{1,0:T(8,128)(2,1)}, bf16[192,4096]{1,0:T(8,128)(2,1)S(1)}, u32[]{:S(2)}, u32[]{:S(2)}) collective-permute-start(bf16[192,4096]{1,0:T(8,128)(2,1)} %get-tuple-element.213), channel_id=1, source_target_pairs={{0,4},{4,0},{1,5},{5,1},{2,6},{6,2},{3,7},{7,3}} | collective-permute-start | bytes 4718600 | tf_op jit(solution)/shard_map/ppermute | solution.py:421
  320.5 54.2 %collective-permute-start.21 = (bf16[192,4096]{1,0:T(8,128)(2,1)}, bf16[192,4096]{1,0:T(8,128)(2,1)}, u32[]{:S(2)}, u32[]{:S(2)}) collective-permute-start(bf16[192,4096]{1,0:T(8,128)(2,1)} %pad_maximum_fusion.3), channel_id=1, source_target_pairs={{0,2},{2,0},{1,3},{3,1},{4,6},{6,4},{5,7},{7,5}} | collective-permute-start | bytes 4718600 | tf_op jit(solution)/shard_map/ppermute | solution.py:418
  359.5 73.7 %collective-permute-start.19 = (bf16[96,4096]{1,0:T(8,128)(2,1)S(1)}, bf16[96,4096]{1,0:T(8,128)(2,1)S(1)}, u32[]{:S(2)}, u32[]{:S(2)}) collective-permute-start(bf16[96,4096]{1,0:T(8,128)(2,1)S(1)} %get-tuple-element.249), channel_id=1, source_target_pairs={{0,4},{4,0},{1,5},{5,1},{2,6},{6,2},{3,7},{7,3}} | collective-permute-start | bytes 2359304 | tf_op jit(solution)/shard_map/ppermute | solution.py:421
  360.9 111.5 %collective-permute-start.27 = (bf16[192,4096]{1,0:T(8,128)(2,1)}, bf16[192,4096]{1,0:T(8,128)(2,1)S(1)}, u32[]{:S(2)}, u32[]{:S(2)}) collective-permute-start(bf16[192,4096]{1,0:T(8,128)(2,1)} %get-tuple-element.208), channel_id=1, source_target_pairs={{0,2},{2,0},{1,3},{3,1},{4,6},{6,4},{5,7},{7,5}} | collective-permute-start | bytes 4718600 | tf_op jit(solution)/shard_map/ppermute | solution.py:418
  361.5 112.3 %collective-permute-start.28 = (bf16[192,4096]{1,0:T(8,128)(2,1)}, bf16[192,4096]{1,0:T(8,128)(2,1)S(1)}, u32[]{:S(2)}, u32[]{:S(2)}) collective-permute-start(bf16[192,4096]{1,0:T(8,128)(2,1)} %get-tuple-element.207), channel_id=1, source_target_pairs={{0,4},{4,0},{1,5},{5,1},{2,6},{6,2},{3,7},{7,3}} | collective-permute-start | bytes 4718600 | tf_op jit(solution)/shard_map/ppermute | solution.py:421
  374.8 58.5 %collective-permute-start.20 = (bf16[96,4096]{1,0:T(8,128)(2,1)S(1)}, bf16[96,4096]{1,0:T(8,128)(2,1)S(1)}, u32[]{:S(2)}, u32[]{:S(2)}) collective-permute-start(bf16[96,4096]{1,0:T(8,128)(2,1)S(1)} %get-tuple-element.251), channel_id=1, source_target_pairs={{0,2},{2,0},{1,3},{3,1},{4,6},{6,4},{5,7},{7,5}} | collective-permute-start | bytes 2359304 | tf_op jit(solution)/shard_map/ppermute | solution.py:418
  396.2 121.7 %collective-permute-start.37 = (bf16[1024,512]{1,0:T(8,128)(2,1)}, bf16[1024,512]{1,0:T(8,128)(2,1)S(1)}, u32[]{:S(2)}, u32[]{:S(2)}) collective-permute-start(bf16[1024,512]{1,0:T(8,128)(2,1)} %collective-permute-done.31.refs_2_), channel_id=1, source_target_pairs={{0,1},{1,0},{2,3},{3,2},{4,5},{5,4},{6,7},{7,6}} | collective-permute-start | bytes 3145736 | tf_op jit(solution)/shard_map/ppermute | solution.py:424
  469.4 95.9 %collective-permute-start.38 = (bf16[1024,512]{1,0:T(8,128)(2,1)S(1)}, bf16[1024,512]{1,0:T(8,128)(2,1)S(1)}, u32[]{:S(2)}, u32[]{:S(2)}) collective-permute-start(bf16[1024,512]{1,0:T(8,128)(2,1)S(1)} %copy-done.6), channel_id=1, source_target_pairs={{0,1},{1,0},{2,3},{3,2},{4,5},{5,4},{6,7},{7,6}} | collective-permute-start | bytes 3145736 | tf_op jit(solution)/shard_map/ppermute | solution.py:424
  469.5 96.5 %collective-permute-start.39 = (bf16[1024,512]{1,0:T(8,128)(2,1)S(1)}, bf16[1024,512]{1,0:T(8,128)(2,1)S(1)}, u32[]{:S(2)}, u32[]{:S(2)}) collective-permute-start(bf16[1024,512]{1,0:T(8,128)(2,1)S(1)} %copy-done.4), channel_id=1, source_target_pairs={{0,1},{1,0},{2,3},{3,2},{4,5},{5,4},{6,7},{7,6}} | collective-permute-start | bytes 3145736 | tf_op jit(solution)/shard_map/ppermute | solution.py:424
  517.9 49.2 %collective-permute-start.40 = (bf16[1024,512]{1,0:T(8,128)(2,1)S(1)}, bf16[1024,512]{1,0:T(8,128)(2,1)S(1)}, u32[]{:S(2)}, u32[]{:S(2)}) collective-permute-start(bf16[1024,512]{1,0:T(8,128)(2,1)S(1)} %collective-permute-done.34.refs_5_), channel_id=1, source_target_pairs={{0,1},{1,0},{2,3},{3,2},{4,5},{5,4},{6,7},{7,6}} | collective-permute-start | bytes 3145736 | tf_op jit(solution)/shard_map/ppermute | solution.py:424
  566.0 46.7 %collective-permute-start.44 = (bf16[192,4096]{1,0:T(8,128)(2,1)}, bf16[192,4096]{1,0:T(8,128)(2,1)}, u32[]{:S(2)}, u32[]{:S(2)}) collective-permute-start(bf16[192,4096]{1,0:T(8,128)(2,1)} %get-tuple-element.201), channel_id=1, source_target_pairs={{0,4},{4,0},{1,5},{5,1},{2,6},{6,2},{3,7},{7,3}} | collective-permute-start | bytes 4718600 | tf_op jit(solution)/shard_map/ppermute | solution.py:421
  576.4 115.9 %collective-permute-start.47 = (bf16[3,768,512]{2,1,0:T(8,128)(2,1)}, bf16[3,768,512]{2,1,0:T(8,128)(2,1)S(1)}, u32[]{:S(2)}, u32[]{:S(2)}) collective-permute-start(bf16[3,768,512]{2,1,0:T(8,128)(2,1)} %pad_maximum_fusion), channel_id=1, source_target_pairs={{0,1},{3,3},{4,5},{7,7}} | collective-permute-start | bytes 7077896 | tf_op jit(solution)/shard_map/ppermute | solution.py:600
  578.4 114.6 %collective-permute-start.48 = (bf16[3,768,512]{2,1,0:T(8,128)(2,1)}, bf16[3,768,512]{2,1,0:T(8,128)(2,1)S(1)}, u32[]{:S(2)}, u32[]{:S(2)}) collective-permute-start(bf16[3,768,512]{2,1,0:T(8,128)(2,1)} %pad_maximum_fusion), channel_id=1, source_target_pairs={{2,1},{1,3},{6,5},{5,7}} | collective-permute-start | bytes 7077896 | tf_op jit(solution)/shard_map/ppermute | solution.py:600
  753.9 70.7 %collective-permute-start.60 = (bf16[2,192,1024]{2,1,0:T(8,128)(2,1)}, bf16[2,192,1024]{2,1,0:T(8,128)(2,1)}, u32[]{:S(2)}, u32[]{:S(2)}) collective-permute-start(bf16[2,192,1024]{2,1,0:T(8,128)(2,1)} %pad_maximum_fusion.13), channel_id=1, source_target_pairs={{0,1},{3,3},{4,5},{7,7}} | collective-permute-start | bytes 2359304 | tf_op jit(solution)/shard_map/ppermute | solution.py:600
  756.1 68.4 %collective-permute-start.61 = (bf16[2,192,1024]{2,1,0:T(8,128)(2,1)}, bf16[2,192,1024]{2,1,0:T(8,128)(2,1)}, u32[]{:S(2)}, u32[]{:S(2)}) collective-permute-start(bf16[2,192,1024]{2,1,0:T(8,128)(2,1)} %pad_maximum_fusion.13), channel_id=1, source_target_pairs={{2,1},{1,3},{6,5},{5,7}} | collective-permute-start | bytes 2359304 | tf_op jit(solution)/shard_map/ppermute | solution.py:600
  761.2 69.9 %collective-permute-start.57 = (bf16[2,192,1024]{2,1,0:T(8,128)(2,1)}, bf16[2,192,1024]{2,1,0:T(8,128)(2,1)}, u32[]{:S(2)}, u32[]{:S(2)}) collective-permute-start(bf16[2,192,1024]{2,1,0:T(8,128)(2,1)} %pad_maximum_fusion.12), channel_id=1, source_target_pairs={{0,1},{3,3},{4,5},{7,7}} | collective-permute-start | bytes 2359304 | tf_op jit(solution)/shard_map/ppermute | solution.py:600
  765.4 65.7 %collective-permute-start.58 = (bf16[2,192,1024]{2,1,0:T(8,128)(2,1)}, bf16[2,192,1024]{2,1,0:T(8,128)(2,1)}, u32[]{:S(2)}, u32[]{:S(2)}) collective-permute-start(bf16[2,192,1024]{2,1,0:T(8,128)(2,1)} %pad_maximum_fusion.12), channel_id=1, source_target_pairs={{2,1},{1,3},{6,5},{5,7}} | collective-permute-start | bytes 2359304 | tf_op jit(solution)/shard_map/ppermute | solution.py:600
  (91 other events, 2641.5 us)

commit v2 on v1

--- a/solution.py
+++ b/solution.py
@@ -11,6 +11,7 @@
 HEAD_DIM = 128
 ROPE_BASE = 500000.0
 NORM_EPS = 1e-5
+MIB = 1 << 20
 SWAP = [(0, 1), (1, 0)]
 FROM_FAR = [(2, 1), (1, 3)]
 FROM_NEAR = [(0, 1), (3, 3)]
@@ -34,6 +35,23 @@
     return jnp.dot(left, right, preferred_element_type=jnp.float32)
 
 
+def params(mebibytes, **extra):
+    return pltpu.CompilerParams(vmem_limit_bytes=mebibytes * MIB, **extra)
+
+
+def cost(flops, bytes_accessed):
+    return pl.CostEstimate(flops=flops, bytes_accessed=bytes_accessed, transcendentals=0)
+
+
+def normalised(as_f32, gain_ref):
+    inv_rms = lax.rsqrt(jnp.mean(as_f32 * as_f32, axis=-1, keepdims=True) + NORM_EPS)
+    return (as_f32 * inv_rms * gain_ref[:]).astype(jnp.bfloat16)
+
+
+def gated(gate, up):
+    return (gate * (1.0 / (1.0 + jnp.exp(-gate))) * up).astype(jnp.bfloat16)
+
+
 def add_rounded(left, right):
     return (left.astype(jnp.float32) + right.astype(jnp.float32)).astype(jnp.bfloat16)
 
@@ -48,24 +66,31 @@
 
     @pl.when(step == 0)
     def _():
-        kr_ref[...] = rotate(k_ref[...].astype(jnp.float32), cos_ref[...], sin_ref[...])
+        kr_ref[:] = rotate(k_ref[:].astype(jnp.float32), cos_ref[:], sin_ref[:])
 
     for i in range(seq_len // q_block):
         @pl.when(step == i)
         def _(i=i):
+            clear = i * q_block // 128 * 128
             keys = min(seq_len, -(-(i + 1) * q_block // 128) * 128)
             rows = pl.ds(i * q_block, q_block)
             cos_rows, sin_rows = cos_ref[rows, :], sin_ref[rows, :]
+            row = lax.broadcasted_iota(jnp.int32, (q_block, keys - clear), 0) + i * q_block
+            col = lax.broadcasted_iota(jnp.int32, (q_block, keys - clear), 1) + clear
+            visible = row >= col
             q = jnp.concatenate([
                 rotate(q_ref[:, g * HEAD_DIM:(g + 1) * HEAD_DIM].astype(jnp.float32), cos_rows, sin_rows)
-                for g in range(group)], axis=0)
-            row = lax.rem(lax.broadcasted_iota(jnp.int32, (group * q_block, keys), 0), q_block) + i * q_block
-            col = lax.broadcasted_iota(jnp.int32, (group * q_block, keys), 1)
+                for g in range(group)])
             scores = lax.dot_general(q, kr_ref[:keys, :], (((1,), (1,)), ((), ())), preferred_element_type=jnp.float32)
-            scores = jnp.where(row >= col, scores * HEAD_DIM ** -0.5, -1e30)
-            probs = jnp.exp(scores - jnp.max(scores, axis=-1, keepdims=True))
-            probs = probs * (1.0 / jnp.sum(probs, axis=-1, keepdims=True))
-            mix = jnp.dot(probs.astype(jnp.bfloat16), v_ref[:keys, :], preferred_element_type=jnp.float32).astype(jnp.bfloat16)
+            rounded = []
+            for g in range(group):
+                part = scores[g * q_block:(g + 1) * q_block]
+                edge = jnp.where(visible, part[:, clear:], -1e30)
+                part = edge if clear == 0 else jnp.concatenate([part[:, :clear], edge], axis=1)
+                part = part * HEAD_DIM ** -0.5
+                probs = jnp.exp(part - jnp.max(part, axis=-1, keepdims=True))
+                rounded.append((probs * (1.0 / jnp.sum(probs, axis=-1, keepdims=True))).astype(jnp.bfloat16))
+            mix = jnp.dot(jnp.concatenate(rounded), v_ref[:keys, :], preferred_element_type=jnp.float32).astype(jnp.bfloat16)
             for g in range(group):
                 o_ref[:, g * HEAD_DIM:(g + 1) * HEAD_DIM] = mix[g * q_block:(g + 1) * q_block]
 
@@ -93,31 +118,191 @@
             ],
         ),
         out_shape=[jax.ShapeDtypeStruct(q.shape, jnp.bfloat16), jax.ShapeDtypeStruct(k.shape, jnp.bfloat16)],
-        compiler_params=pltpu.CompilerParams(vmem_limit_bytes=32 * 1024 * 1024),
-        cost_estimate=pl.CostEstimate(flops=9_000_000_000, bytes_accessed=5_000_000, transcendentals=4_000_000),
+        compiler_params=params(32),
+        cost_estimate=cost(9_000_000_000, 5_000_000),
     )(order, q, k, v, cos_t, sin_t)
+
+
+def project_kernel(request, next_request, embeds_hbm, moved_hbm, gain_ref, wq_ref, wk_ref, wv_ref, q_ref, k_ref, v_ref, own_ref, *rest):
+    a, b, s = lax.axis_index('a'), lax.axis_index('b'), lax.axis_index('stage')
+    if next_request is not None:
+        next_hbm, x, normed, sems, send_sem, recv_sem = rest
+        passed = pltpu.make_async_remote_copy(
+            src_ref=embeds_hbm.at[0, next_request], dst_ref=next_hbm, send_sem=send_sem, recv_sem=recv_sem,
+            device_id={'stage': 1 - s}, device_id_type=pl.DeviceIdType.MESH)
+    else:
+        x, normed, sems = rest
+    step = pl.program_id(0)
+    last = pl.num_programs(0) - 1
+    pieces = sems.shape[0]
+    rows = x.shape[0] // pieces
+    block = own_ref.shape[0] // 2
+
+    @pl.when(step == 0)
+    def _():
+        def fetch(source, i):
+            return pltpu.make_async_copy(source.at[pl.ds(i * rows, rows)], x.at[pl.ds(i * rows, rows)], sems.at[i])
+
+        @pl.when(s == 0)
+        def _():
+            for i in range(pieces):
+                fetch(embeds_hbm.at[0, request], i).start()
+
+        @pl.when(s == 1)
+        def _():
+            for i in range(pieces):
+                fetch(moved_hbm, i).start()
+
+        if next_request is not None:
+            barrier = pltpu.get_barrier_semaphore()
+            pl.semaphore_signal(barrier, inc=1, device_id={'stage': 1 - s}, device_id_type=pl.DeviceIdType.MESH)
+            pl.semaphore_wait(barrier, 1)
+
+            @pl.when(s == 0)
+            def _():
+                passed.start()
+
+        for i in range(pieces):
+            fetch(moved_hbm, i).wait()
+            normed[pl.ds(i * rows, rows), :] = normalised(x[pl.ds(i * rows, rows), :].astype(jnp.float32), gain_ref)
+        for i, own in enumerate((2 * a + b, 4 + 2 * b + a)):
+            own_ref[i * block:(i + 1) * block, :] = x[pl.ds(pl.multiple_of(own * block, 32), block), :]
+
+    @pl.when(step < last)
+    def _():
+        q_ref[:] = matmul(normed[:], wq_ref[0]).astype(jnp.bfloat16)
+
+    @pl.when(step == last)
+    def _():
+        k_ref[:] = matmul(normed[:], wk_ref[0]).astype(jnp.bfloat16)
+        v_ref[:] = matmul(normed[:], wv_ref[0]).astype(jnp.bfloat16)
+        if next_request is not None:
+            @pl.when(s == 0)
+            def _():
+                passed.wait_send()
+
+            @pl.when(s == 1)
+            def _():
+                passed.wait_recv()
+
+
+def projections(embeds, moved, request, next_request, gain, w_query, w_key, w_value):
+    seq_len, width = moved.shape
+    q_width, kv_width = w_query.shape[2], w_key.shape[2]
+    tile = 2 * kv_width
+    q_steps = q_width // tile
+    hbm = pl.BlockSpec(memory_space=pltpu.HBM)
+
+    def first(shape):
+        return pl.BlockSpec(shape, lambda j: (0,) * len(shape))
+
+    def bf16(*shape):
+        return jax.ShapeDtypeStruct(shape, jnp.bfloat16)
+
+    out_specs = [
+        pl.BlockSpec((seq_len, tile), lambda j: (0, jnp.minimum(j, q_steps - 1))),
+        first((seq_len, kv_width)), first((seq_len, kv_width)), first((seq_len // 4, width))]
+    out_shape = [bf16(seq_len, q_width), bf16(seq_len, kv_width), bf16(seq_len, kv_width), bf16(seq_len // 4, width)]
+    scratch = [pltpu.VMEM((seq_len, width), jnp.bfloat16), pltpu.VMEM((seq_len, width), jnp.bfloat16), pltpu.SemaphoreType.DMA((4,))]
+    extra = {}
+    if next_request is not None:
+        out_specs.append(hbm)
+        out_shape.append(bf16(seq_len, width))
+        scratch += [pltpu.SemaphoreType.DMA, pltpu.SemaphoreType.DMA]
+        extra = dict(collective_id=1 + request, has_side_effects=True)
+    return pl.pallas_call(
+        functools.partial(project_kernel, request, next_request),
+        grid=(q_steps + 1,),
+        in_specs=[
+            hbm, hbm, first((1, width)),
+            pl.BlockSpec((1, width, tile), lambda j: (0, 0, jnp.minimum(j, q_steps - 1))),
+            first((1, width, kv_width)), first((1, width, kv_width)),
+        ],
+        out_specs=out_specs,
+        out_shape=out_shape,
+        scratch_shapes=scratch,
+        compiler_params=params(56, **extra),
+        cost_estimate=cost(10_000_000_000, 30_000_000),
+    )(embeds, moved, gain, w_query, w_key, w_value)
+
+
+def gate_up_kernel(own_hbm, near_1_hbm, near_2_hbm, far_1_hbm, far_2_hbm, wg_ref, wu_ref, o_ref, rows, sems):
+    block = near_1_hbm.shape[0]
+
+    @pl.when(pl.program_id(0) == 0)
+    def _():
+        copies = []
+        for i, (source, start) in enumerate((
+                (own_hbm.at[pl.ds(0, block)], 0), (near_1_hbm, block), (far_1_hbm, 2 * block),
+                (own_hbm.at[pl.ds(block, block)], 4 * block), (near_2_hbm, 5 * block), (far_2_hbm, 6 * block))):
+            copies.append(pltpu.make_async_copy(source, rows.at[pl.ds(start, source.shape[0])], sems.at[i]))
+            copies[-1].start()
+        for copy in copies:
+            copy.wait()
+
+    gate = jnp.dot(rows[:], wg_ref[0], preferred_element_type=jnp.float32).astype(jnp.bfloat16).astype(jnp.float32)
+    up = jnp.dot(rows[:], wu_ref[0], preferred_element_type=jnp.float32).astype(jnp.bfloat16).astype(jnp.float32)
+    o_ref[:] = gated(gate, up)
+
+
+def gate_up(own, near_1, near_2, far_1, far_2, w_gate, w_up, first, count, tile):
+    block, width = near_1.shape
+    hbm = pl.BlockSpec(memory_space=pltpu.HBM)
+    weight = pl.BlockSpec((1, width, tile), lambda j: (0, 0, first + j))
+    return pl.pallas_call(
+        gate_up_kernel,
+        grid=(count,),
+        in_specs=[hbm] * 5 + [weight] * 2,
+        out_specs=pl.BlockSpec((8 * block, tile), lambda j: (0, j)),
+        out_shape=jax.ShapeDtypeStruct((8 * block, count * tile), jnp.bfloat16),
+        scratch_shapes=[pltpu.VMEM((8 * block, width), jnp.bfloat16), pltpu.SemaphoreType.DMA((6,))],
+        compiler_params=params(56),
+        cost_estimate=cost(32 * block * width * count * tile, 4 * width * count * tile),
+    )(own, near_1, near_2, far_1, far_2, w_gate, w_up)
+
+
+def down_kernel(act_1_ref, act_2_ref, w_ref, *o_refs):
+    cut = act_1_ref.shape[1]
+    product = jnp.dot(act_1_ref[:], w_ref[0, :cut, :], preferred_element_type=jnp.float32)
+    product = (product + jnp.dot(act_2_ref[:], w_ref[0, cut:, :], preferred_element_type=jnp.float32)).astype(jnp.bfloat16)
+    rows = o_refs[0].shape[0]
+    for i, o_ref in enumerate(o_refs):
+        o_ref[:] = product[i * rows:(i + 1) * rows]
+
+
+def down(act_1, act_2, w_down, tile):
+    rows, depth = act_1.shape[0], w_down.shape[1]
+    width = w_down.shape[2]
+    return pl.pallas_call(
+        down_kernel,
+        grid=(width // tile,),
+        in_specs=[pl.BlockSpec(act_1.shape, lambda j: (0, 0)), pl.BlockSpec(act_2.shape, lambda j: (0, 0)),
+                  pl.BlockSpec((1, depth, tile), lambda j: (0, 0, j))],
+        out_specs=[pl.BlockSpec((rows // 4, tile), lambda j: (0, j))] * 4,
+        out_shape=[jax.ShapeDtypeStruct((rows // 4, width), jnp.bfloat16)] * 4,
+        compiler_params=params(56),
+        cost_estimate=cost(2 * rows * depth * width, 2 * depth * width),
+    )(act_1, act_2, w_down)
 
 
 def kv_kernel(part_ref, x_ref, gain_ref, cos_ref, sin_ref, *refs):
     mine, other, o_ref, normed = refs[:8], refs[8:16], refs[16], refs[17]
     depth, columns = mine[0].shape
     half = 2 * depth
-    as_f32 = x_ref[...].astype(jnp.float32)
-    inv_rms = lax.rsqrt(jnp.mean(as_f32 * as_f32, axis=-1, keepdims=True) + NORM_EPS)
-    whole = (as_f32 * inv_rms * gain_ref[...]).astype(jnp.bfloat16)
+    whole = normalised(x_ref[:].astype(jnp.float32), gain_ref)
     normed[0] = whole[:, :half]
     normed[1] = whole[:, half:]
     part = part_ref[0]
     for piece in range(4):
-        product = jnp.dot(normed[part, :, :depth], mine[2 * piece][...], preferred_element_type=jnp.float32)
-        product += jnp.dot(normed[part, :, depth:], mine[2 * piece + 1][...], preferred_element_type=jnp.float32)
-        product += jnp.dot(normed[1 - part, :, :depth], other[2 * piece][...], preferred_element_type=jnp.float32)
-        product += jnp.dot(normed[1 - part, :, depth:], other[2 * piece + 1][...], preferred_element_type=jnp.float32)
+        product = jnp.dot(normed[part, :, :depth], mine[2 * piece][:], preferred_element_type=jnp.float32)
+        product += jnp.dot(normed[part, :, depth:], mine[2 * piece + 1][:], preferred_element_type=jnp.float32)
+        product += jnp.dot(normed[1 - part, :, :depth], other[2 * piece][:], preferred_element_type=jnp.float32)
+        product += jnp.dot(normed[1 - part, :, depth:], other[2 * piece + 1][:], preferred_element_type=jnp.float32)
         rounded = product.astype(jnp.bfloat16)
         base = piece * columns
         for h in range(columns // 2 // HEAD_DIM):
             cols = slice(h * HEAD_DIM, (h + 1) * HEAD_DIM)
-            o_ref[:, base + h * HEAD_DIM:base + (h + 1) * HEAD_DIM] = rotate(rounded[:, cols].astype(jnp.float32), cos_ref[...], sin_ref[...])
+            o_ref[:, base + h * HEAD_DIM:base + (h + 1) * HEAD_DIM] = rotate(rounded[:, cols].astype(jnp.float32), cos_ref[:], sin_ref[:])
         o_ref[:, base + columns // 2:base + columns] = rounded[:, columns // 2:]
 
 
@@ -131,8 +316,8 @@
         out_specs=vmem,
         out_shape=jax.ShapeDtypeStruct((rows, 4 * columns), jnp.bfloat16),
         scratch_shapes=[pltpu.VMEM((2, rows, 2 * depth), jnp.bfloat16)],
-        compiler_params=pltpu.CompilerParams(vmem_limit_bytes=40 * 1024 * 1024),
-        cost_estimate=pl.CostEstimate(flops=32 * rows * depth * columns, bytes_accessed=32 * depth * columns, transcendentals=0),
+        compiler_params=params(40),
+        cost_estimate=cost(32 * rows * depth * columns, 32 * depth * columns),
     )(part, x, gain, cos_rows, sin_rows, *mine, *other)
 
 
@@ -184,22 +369,18 @@
             for i, (peer, where) in enumerate(peers)]
         for copy in copies:
             copy.start()
-        everyone[me] = source_of(me)[...]
+        everyone[me] = source_of(me)[:]
         for arrival in arrivals:
             arrival.wait_recv()
         for copy in copies:
             copy.wait_send()
-
-    def norm(rows, gain_ref):
-        inv_rms = lax.rsqrt(jnp.mean(rows * rows, axis=-1, keepdims=True) + NORM_EPS)
-        return (rows * inv_rms * gain_ref[...]).astype(jnp.bfloat16)
 
     row_index = lax.broadcasted_iota(jnp.int32, (n_rows, x0_ref.shape[1]), 0)
     rows = jnp.zeros((n_rows, x0_ref.shape[1]), jnp.float32)
     for c in range(n_chunk):
         last_row = x_refs[c][x_refs[c].shape[0] - 1:, :].astype(jnp.float32)
         rows = jnp.where(row_index == n_chunk * s + c, last_row, rows)
-    x_src[...] = rows.astype(jnp.bfloat16)
+    x_src[:] = rows.astype(jnp.bfloat16)
     is_owner = a + b == 2
 
     def x_copy(i):
@@ -211,7 +392,7 @@
     def _():
         for i in range(7):
             x_copy(i).start()
-        x_all[s] = x_src[...]
+        x_all[s] = x_src[:]
 
     for o in range(2):
         @pl.when(me != 6 + o)
@@ -227,8 +408,8 @@
 
     last = x_all[0].astype(jnp.float32) + x_all[1].astype(jnp.float32)
     fetches[0].wait()
-    q = jnp.dot(norm(last, gain_a_ref), wq[...], preferred_element_type=jnp.float32)
-    q_src[...] = q.astype(jnp.bfloat16).astype(jnp.float32)
+    q = jnp.dot(normalised(last, gain_a_ref), wq[:], preferred_element_type=jnp.float32)
+    q_src[:] = q.astype(jnp.bfloat16).astype(jnp.float32)
     exchange(lambda peer: q_src, q_all, q_send, q_recv)
 
     kv_width = kv_heads * HEAD_DIM
@@ -240,8 +421,8 @@
             low = 2 * piece * kv_width + h * HEAD_DIM
             for c in range(n_chunk):
                 q_row = q_all[head, pl.ds(n_chunk * s + c, 1), :]
-                q_heads = jnp.concatenate([q_row[:, g * HEAD_DIM:(g + 1) * HEAD_DIM] for g in range(group)], axis=0)
-                q_heads = rotate(q_heads, cos_ref[...], sin_ref[...])
+                q_heads = jnp.concatenate([q_row[:, g * HEAD_DIM:(g + 1) * HEAD_DIM] for g in range(group)])
+                q_heads = rotate(q_heads, cos_ref[:], sin_ref[:])
                 k = kv_refs[c][:, low:low + HEAD_DIM]
                 v = kv_refs[c][:, low + kv_width:low + kv_width + HEAD_DIM]
                 scores = lax.dot_general(q_heads, k, (((1,), (1,)), ((), ())), preferred_element_type=jnp.float32) * HEAD_DIM ** -0.5
@@ -253,7 +434,7 @@
                 pk_src[head, c, :, 2 * HEAD_DIM:] = jnp.broadcast_to(total, (group, HEAD_DIM))
     exchange(lambda peer: pk_src.at[peer], pk_all, pk_send, pk_recv)
 
-    mix[...] = jnp.zeros_like(mix)
+    mix[:] = jnp.zeros_like(mix)
     for stage in range(2):
         for c in range(n_chunk):
             found = [pk_all[2 * i + stage, c] for i in range(4)]
@@ -276,19 +457,19 @@
         return total.astype(jnp.bfloat16).astype(jnp.float32)
 
     fetches[1].wait()
-    p_src[...] = jnp.dot(mix[...].astype(jnp.bfloat16), wo[...], preferred_element_type=jnp.float32).astype(jnp.bfloat16)
+    p_src[:] = jnp.dot(mix[:].astype(jnp.bfloat16), wo[:], preferred_element_type=jnp.float32).astype(jnp.bfloat16)
     exchange(lambda peer: p_src, p_all, p_send, p_recv)
     last = (last + summed(p_all)).astype(jnp.bfloat16).astype(jnp.float32)
-    normed = norm(last, gain_m_ref)
+    normed = normalised(last, gain_m_ref)
     fetches[2].wait()
-    gate = jnp.dot(normed, wg[...], preferred_element_type=jnp.float32).astype(jnp.bfloat16).astype(jnp.float32)
+    gate = jnp.dot(normed, wg[:], preferred_element_type=jnp.float32).astype(jnp.bfloat16).astype(jnp.float32)
     fetches[3].wait()
-    up = jnp.dot(normed, wu[...], preferred_element_type=jnp.float32).astype(jnp.bfloat16).astype(jnp.float32)
-    act = (gate * (1.0 / (1.0 + jnp.exp(-gate))) * up).astype(jnp.bfloat16)
+    up = jnp.dot(normed, wu[:], preferred_element_type=jnp.float32).astype(jnp.bfloat16).astype(jnp.float32)
+    act = gated(gate, up)
     fetches[4].wait()
-    r_src[...] = jnp.dot(act, wd[...], preferred_element_type=jnp.float32).astype(jnp.bfloat16)
+    r_src[:] = jnp.dot(act, wd[:], preferred_element_type=jnp.float32).astype(jnp.bfloat16)
     exchange(lambda peer: r_src, r_all, r_send, r_recv)
-    o_ref[...] = (last + summed(r_all)).astype(jnp.bfloat16)
+    o_ref[:] = (last + summed(r_all)).astype(jnp.bfloat16)
 
 
 def last_rows(finals, kvs, gain_a, gain_m, cos_row, sin_row, w_query, w_out, w_gate, w_up, w_down, kv_heads):
@@ -332,8 +513,8 @@
             pltpu.SemaphoreType.DMA((5,)),
             seven, pltpu.SemaphoreType.DMA((2,)), seven, seven, seven, seven, seven, seven, seven, seven,
         ],
-        compiler_params=pltpu.CompilerParams(collective_id=0, has_side_effects=True, vmem_limit_bytes=63 * 1024 * 1024),
-        cost_estimate=pl.CostEstimate(flops=9_000_000_000, bytes_accessed=60_000_000, transcendentals=0),
+        compiler_params=params(63, collective_id=0, has_side_effects=True),
+        cost_estimate=cost(9_000_000_000, 60_000_000),
     )(*finals, *kvs, gain_a, gain_m, cos_row, sin_row, w_query, w_out, w_gate, w_up, w_down)
 
 
@@ -360,8 +541,8 @@
         first_cut_kernel,
         grid_spec=pltpu.PrefetchScalarGridSpec(num_scalar_prefetch=1, grid=(n_chunk, 2), in_specs=[source] * 2, out_specs=[target] * 2),
         out_shape=[jax.ShapeDtypeStruct((1, 2, n_chunk, seq_len, heads, HEAD_DIM), jnp.bfloat16)] * 2,
-        compiler_params=pltpu.CompilerParams(vmem_limit_bytes=32 * 1024 * 1024),
-        cost_estimate=pl.CostEstimate(flops=1_000_000_000, bytes_accessed=19_000_000, transcendentals=0),
+        compiler_params=params(32),
+        cost_estimate=cost(1_000_000_000, 19_000_000),
     )(where, near, far)
 
 
@@ -401,8 +582,8 @@
             num_scalar_prefetch=1, grid=(2, 2, 2), in_specs=[source] * 2 + [whole] * 2, out_specs=[target] * 2),
         out_shape=[jax.ShapeDtypeStruct(k_cache.shape, jnp.bfloat16)] * 2,
         input_output_aliases={3: 0, 4: 1},
-        compiler_params=pltpu.CompilerParams(vmem_limit_bytes=32 * 1024 * 1024),
-        cost_estimate=pl.CostEstimate(flops=300_000_000, bytes_accessed=5_000_000, transcendentals=0),
+        compiler_params=params(32),
+        cost_estimate=cost(300_000_000, 5_000_000),
     )(where, near, far, k_cache, v_cache)
 
 
@@ -447,37 +628,35 @@
         def own_rows(value):
             return jnp.concatenate([
                 lax.dynamic_slice_in_dim(value, block * (2 * a + b), block, 0),
-                lax.dynamic_slice_in_dim(value, half_rows + block * chip, block, 0)], axis=0)
-
-        def send_parts(part_sum):
-            quarter = 2 * block
-            return part_sum[quarter:2 * quarter], part_sum[3 * quarter:]
+                lax.dynamic_slice_in_dim(value, half_rows + block * chip, block, 0)])
+
+        def quarters(part_sum):
+            return [part_sum[2 * i * block:2 * (i + 1) * block] for i in range(4)]
+
+        def send_parts(parts):
+            return parts[1], parts[3]
 
         def send_wide(sends):
             return over_x(sends[0]), over_y(sends[1])
 
-        def add_wide(part_sum, got):
-            quarter = 2 * block
-            return add_rounded(part_sum[:quarter], got[0]), add_rounded(part_sum[2 * quarter:3 * quarter], got[1])
+        def add_wide(parts, got):
+            return add_rounded(parts[0], got[0]), add_rounded(parts[2], got[1])
 
         def send_narrow(sums):
             return over_y(sums[0][block:]), over_x(sums[1][block:])
 
         def add_narrow(residual, sums, got):
-            kept = jnp.concatenate([sums[0][:block], sums[1][:block]], axis=0)
-            return add_rounded(residual, add_rounded(kept, jnp.concatenate(got, axis=0)))
+            kept = jnp.concatenate([sums[0][:block], sums[1][:block]])
+            return add_rounded(residual, add_rounded(kept, jnp.concatenate(got)))
 
         def gather_near(own):
             return over_y(own[:block]), over_x(own[block:])
 
         def join_near(own, got):
-            return jnp.concatenate([own[:block], got[0]], axis=0), jnp.concatenate([own[block:], got[1]], axis=0)
+            return jnp.concatenate([own[:block], got[0]]), jnp.concatenate([own[block:], got[1]])
 
         def gather_far(near):
             return over_x(near[0]), over_y(near[1])
-
-        def join_far(near, far):
-            return jnp.concatenate([near[0], far[0], near[1], far[1]], axis=0)
 
         def take(value):
             return lax.ppermute(value, 'stage', [(0, 1)])
@@ -494,49 +673,39 @@
         top_y, bottom_x = over_y(w_top), over_x(w_bottom)
         top_x, bottom_y = over_x(w_top), over_y(w_bottom)
 
-        def project(x):
-            normed = rms_norm(x, attn_gain[0])
-            q = matmul(normed, w_query[0]).astype(jnp.bfloat16)
-            k = matmul(normed, w_key[0]).astype(jnp.bfloat16)
-            v = matmul(normed, w_value[0]).astype(jnp.bfloat16)
-            return q, k, v
+        def project(moved, request):
+            following = n_chunk + request + 1 if request + 1 < n_chunk else None
+            q, k, v, own, *passed = projections(embeds, moved, request, following, attn_gain[:1], w_query, w_key, w_value)
+            return (q, k, v), own, passed
 
         def attend(qkv):
             mix, k_rot = attention(*qkv, cos_t, sin_t, order)
             return mix, jnp.concatenate([k_rot, qkv[2]], axis=1)
 
         def out_of(mix):
-            return matmul(mix, w_out[0]).astype(jnp.bfloat16)
-
-        def gate_of(normed):
-            return matmul(normed, w_gate[0]).astype(jnp.bfloat16)
-
-        def act_of(normed, gate):
-            up = matmul(normed, w_up[0]).astype(jnp.bfloat16)
-            return (jax.nn.silu(gate.astype(jnp.float32)) * up.astype(jnp.float32)).astype(jnp.bfloat16)
-
-        def down_of(act):
-            return matmul(act, w_down[0]).astype(jnp.bfloat16)
-
-        def hidden_of(first, second):
-            return jnp.where(s == 0, first, second)
+            return quarters(matmul(mix, w_out[0]).astype(jnp.bfloat16))
+
+        mlp_tile = 512
+        n_tiles = w_gate.shape[2] // mlp_tile
+        first_tiles = n_tiles // 2
+
+        def act_of(h, got, far, second):
+            start, count = (first_tiles, n_tiles - first_tiles) if second else (0, first_tiles)
+            return gate_up(h, got[0], got[1], far[0], far[1], w_gate, w_up, start, count, mlp_tile)
+
+        def down_of(act_1, act_2):
+            return down(act_1, act_2, w_down, mlp_tile)
 
         own_cos, own_sin = own_rows(cos_t), own_rows(sin_t)
 
-        x0 = hidden_of(hold(embeds, moved0)[0, 0], moved0)
-        qkv0 = project(x0)
-        moved1 = take(hold(embeds, qkv0)[0, n_chunk + 1])
+        qkv0, own_x0, (moved1,) = project(moved0, 0)
         top_d, bottom_d = over_x(hold(top_y, qkv0)), over_y(hold(bottom_x, qkv0))
         mix0, kv0_0 = attend(qkv0)
         p0 = out_of(mix0)
-        own_x0 = own_rows(x0)
         send = send_parts(p0)
         wide0 = send_wide(send)
 
-        moved2 = take(hold(embeds, send)[0, n_chunk + 2])
-        embeds_1, moved1 = hold((embeds, moved1), send, moved1)
-        x1 = hidden_of(embeds_1[0, 1], moved1)
-        qkv1 = project(x1)
+        qkv1, own_x1, (moved2,) = project(hold(moved1, send), 1)
         sums0 = add_wide(p0, hold(wide0, qkv1))
         narrow0 = send_narrow(sums0)
         mix1, kv0_1 = attend(hold(qkv1, sums0))
@@ -544,34 +713,30 @@
         h0 = rms_norm(own1_0, mlp_gain[0])
         near_got0 = gather_near(h0)
         p1 = out_of(hold(mix1, h0))
-        own_x1 = own_rows(x1)
         send = send_parts(p1)
         wide1 = send_wide(send)
         near0 = join_near(h0, hold(near_got0, send))
         far0 = gather_far(near0)
 
-        embeds_2, moved2 = hold((embeds, moved2), near0, moved2)
-        x2 = hidden_of(embeds_2[0, 2], moved2)
-        qkv2 = project(x2)
+        qkv2, own_x2, _ = project(hold(moved2, near0), 2)
         mix2, kv0_2 = attend(qkv2)
         sums1 = add_wide(p1, hold(wide1, mix2))
         narrow1 = send_narrow(sums1)
         p2 = out_of(hold(mix2, sums1))
-        own_x2 = own_rows(x2)
         send = send_parts(p2)
         wide2 = send_wide(send)
 
-        normed = join_far(near0, hold(far0, send))
-        gate = gate_of(normed)
+        rows = (h0, near_got0, hold(far0, send))
+        gate = act_of(*rows, False)
         own1_1 = add_narrow(own_x1, sums1, hold(narrow1, gate))
         h1 = rms_norm(own1_1, mlp_gain[0])
         near_got1 = gather_near(h1)
-        act = act_of(hold(normed, h1), gate)
+        act = act_of(*hold(rows, h1), True)
         near1 = join_near(h1, hold(near_got1, act))
         far1 = gather_far(near1)
         sums2 = add_wide(p2, hold(wide2, near1))
         narrow2 = send_narrow(sums2)
-        d0 = down_of(hold(act, sums2))
+        d0 = down_of(gate, hold(act, sums2))
         send = send_parts(d0)
         wide0 = send_wide(send)
 
@@ -579,17 +744,17 @@
         w_mine = [w_top, w_bottom] + list(fetched)
         w_other = [w_block(1 - s, 0), w_block(1 - s, 1)] + [across(piece) for piece in fetched]
 
-        normed = join_far(near1, hold(far1, send))
-        gate = gate_of(normed)
+        rows = (h1, near_got1, hold(far1, send))
+        gate = act_of(*rows, False)
         own1_2 = add_narrow(own_x2, sums2, hold(narrow2, gate))
         h2 = rms_norm(own1_2, mlp_gain[0])
         near_got2 = gather_near(h2)
-        act = act_of(hold(normed, h2), gate)
+        act = act_of(*hold(rows, h2), True)
         near2 = join_near(h2, hold(near_got2, act))
         far2 = gather_far(near2)
         sums0 = add_wide(d0, hold(wide0, near2))
         narrow0 = send_narrow(sums0)
-        d1 = down_of(hold(act, sums0))
+        d1 = down_of(gate, hold(act, sums0))
         send = send_parts(d1)
         wide1 = send_wide(send)
 
@@ -605,17 +770,17 @@
         def to_decode_rows(kv, got):
             return to_decode(jnp.stack([kv[:, :2 * kv2], got]))
 
-        normed = join_far(near2, hold(far2, send))
-        gate = gate_of(normed)
+        rows = (h2, near_got2, hold(far2, send))
+        gate = act_of(*rows, False)
         final0 = add_narrow(own1_0, sums0, hold(narrow0, gate))
         kv1_0 = keys_values_of(final0)
         got_0 = along_y(kv1_0)
         cut0 = to_decode(hold(jnp.stack([kv0_0, kv0_1, kv0_2]), kv1_0))
-        act = act_of(hold(normed, kv1_0), gate)
+        act = act_of(*hold(rows, kv1_0), True)
         sums1 = add_wide(d1, hold(wide1, act))
         narrow1 = send_narrow(sums1)
         cut1_0 = to_decode_rows(kv1_0, hold(got_0, sums1))
-        d2 = down_of(hold(act, sums1))
+        d2 = down_of(gate, hold(act, sums1))
         send = send_parts(d2)
         wide2 = send_wide(send)
         final1 = add_narrow(own1_1, sums1, hold(narrow1, send))

time: 848 us -> 837 us (0.987)
  Pallas kernels: 147 us -> 492 us
  matrix products: 350 us -> 27.9 us
  local copies, waits for them, and re-layouts: 87.2 us -> 57.3 us
  waiting for transfers between devices: 106 us -> 89.2 us
  starting transfers between devices: 80.4 us -> 89.7 us
    pallas_call x0 -> x12, Pallas kernels: none -> 345 us  [the longest x6 195 us: gate_up(): pl.pallas_call(gate_up_kernel, grid=(count,), in_specs=[hbm] * 5 + [weigh...]
    dot_general x21 -> x3, matrix products: 350 us -> 27.9 us  [matmul(): return jnp.dot(left, right, preferred_element_type=jnp.float32)]
    ppermute x24, waiting for transfers between devices: 71.9 us -> 51.3 us  [over_y(): return lax.ppermute(value, 'b', SWAP)]
    ppermute x4, starting transfers between devices: 9.94 us -> 28.1 us  [to_decode(): lax.ppermute(value, ('a', 'stage'), FROM_NEAR)]
    squeeze x2 -> x0, local copies, waits for them, and re-layouts: 12.5 us -> none  [the longest x1 6.29 us: stage_program(): moved1 = take(hold(embeds, qkv0)[0, n_chunk + 1])]
    reduce_sum x6 -> x3, other arithmetic: 18.7 us -> 6.64 us  [rms_norm(): jnp.mean(as_f32 * as_f32, axis=-1, keepdims=True) + NORM_EPS]
    ppermute x3 -> x1, starting transfers between devices: 14.1 us -> 5.4 us  [take(): return lax.ppermute(value, 'stage', [(0, 1)])]
    unnamed x118 -> x142, local copies, waits for them, and re-layouts: 27.3 us -> 19.2 us
  transfers between devices with their start and end apart: 62 -> 60, of which waited for: 13 -> 12; matrix products, arithmetic and copies ran while one was open for 58% -> 14% of each run, Pallas kernels for 17% -> 59%
where the time goes in v2:
time: 837 us; the launch traced here: 825 us
  Pallas kernels  492 us (59%)
  starting transfers between devices  89.7 us (11%)
  waiting for transfers between devices  89.2 us (11%)
  other arithmetic  66.9 us (8%)
  local copies, waits for them, and re-layouts  57.3 us (7%)
  matrix products  27.9 us (3%)
    pallas_call x6, Pallas kernels, gate_up(): pl.pallas_call(gate_up_kernel, grid=(count,), in_specs=[hbm] * 5 + [weigh...  195 us
    pallas_call x3, Pallas kernels, down(): pl.pallas_call(down_kernel, grid=(width // tile,), in_specs=[pl.BlockSpec...  86.3 us
    pallas_call x3, Pallas kernels, projections(): pl.pallas_call(functools.partial(project_kernel, request, next_request),...  63.8 us
    pallas_call x1, Pallas kernels, last_rows(): pl.pallas_call(functools.partial(tail_kernel, kv_heads), grid=(1,), in_sp...  52.2 us
    ppermute x24, waiting for transfers between devices, over_y(): return lax.ppermute(value, 'b', SWAP)  51.3 us
    pallas_call x3, Pallas kernels, attention(): pl.pallas_call(functools.partial(attention_kernel, q_block, group), grid_...  46.3 us
    ppermute x21, waiting for transfers between devices, over_x(): return lax.ppermute(value, 'a', SWAP)  37.8 us
    convert_element_type x12, other arithmetic, add_rounded(): (left.astype(jnp.float32) + right.astype(jnp.float32)).astype(jnp.bfloat16)  32.8 us
  transfers between devices with their start and end apart: 60, of which 12 were waited for; matrix products, arithmetic and copies ran while one was open for 14% of the time, Pallas kernels for 59%

profile of v2, /device:TPU:0, one launch (start us, length us, event | category | flops | bytes accessed | tf_op | source)
XLA Modules:
  0.0 825.2 jit_solution(432544855388416170)
XLA Ops:
  29.0 21.1 %shard_map.121 = (bf16[768,1024]{1,0:T(8,128)(2,1)}, bf16[768,256]{1,0:T(8,128)(2,1)}, bf16[768,256]{1,0:T(8,128)(2,1)}, bf16[192,4096]{1,0:T(8,128)(2,1)}, bf16[768,4096]{1,0:T(8,128)(2,1)}) custom-call(bf16[1,6,768,4096]{3,2,1,0:T(8,128)(2,1)} %embeds_hbm.5, bf16[768,4096]{1,0:T(8,128)(2,1)} %collective-permute-done.moved_hbm, ...), custom_call_target="tpu_custom_call" | custom-call | flops 10000000000 | bytes 30000000 | tf_op jit(solution)/shard_map/pallas_call | solution.py:213
  53.5 15.4 %shard_map.122 = (bf16[768,1024]{1,0:T(8,128)(2,1)S(1)}, bf16[768,256]{1,0:T(8,128)(2,1)S(1)}) custom-call(s32[8]{0:T(128)S(1)} %pad_add_fusion.1._, bf16[768,1024]{1,0:T(8,128)(2,1)S(1)} %copy-done.19, bf16[768,256]{1,0:T(8,128)(2,1)S(1)} %copy-done.22, bf16[768,256]{1,0:T(8,128)(2,1)S(1)} %copy-done.11, f32[768,128]{1,0:T(8,128)S(1)} %get-tuple-element.324.cos_ref, ...), custom_call_target="tpu_custom_call" | custom-call | flops 8999999488 | bytes 5000000 | tf_op jit(solution)/shard_map/pallas_call | solution.py:103
  68.9 10.5 %fusion.6 = bf16[768,4096]{1,0:T(8,128)(2,1)S(1)} fusion(bf16[768,1024]{1,0:T(8,128)(2,1)S(1)} %get-tuple-element.130, bf16[2,1024,4096]{2,1,0:T(8,128)(2,1)} %wo_hbm.1), kind=kOutput, calls=%fused_computation.6 | convolution fusion | flops 6445596672 | bytes 16252928 | tf_op jit(solution)/shard_map/dot_general | solution.py:35
  87.0 21.5 %shard_map.123 = (bf16[768,1024]{1,0:T(8,128)(2,1)}, bf16[768,256]{1,0:T(8,128)(2,1)}, bf16[768,256]{1,0:T(8,128)(2,1)}, bf16[192,4096]{1,0:T(8,128)(2,1)}, bf16[768,4096]{1,0:T(8,128)(2,1)}) custom-call(bf16[1,6,768,4096]{3,2,1,0:T(8,128)(2,1)} %embeds_hbm.5, bf16[768,4096]{1,0:T(8,128)(2,1)} %get-tuple-element.131.moved_hbm, ...), custom_call_target="tpu_custom_call" | custom-call | flops 10000000000 | bytes 30000000 | tf_op jit(solution)/shard_map/pallas_call | solution.py:213
  108.4 9.9 %collective-permute-done.2 = bf16[192,4096]{1,0:T(8,128)(2,1)} collective-permute-done((bf16[192,4096]{1,0:T(8,128)(2,1)}, bf16[192,4096]{1,0:T(8,128)(2,1)}, u32[]{:S(2)}, u32[]{:S(2)}) %collective-permute-start.2) | collective-permute-done | bytes 1572896 | tf_op jit(solution)/shard_map/ppermute | solution.py:602
  125.9 15.4 %shard_map.124 = (bf16[768,1024]{1,0:T(8,128)(2,1)S(1)}, bf16[768,256]{1,0:T(8,128)(2,1)S(1)}) custom-call(s32[8]{0:T(128)S(1)} %pad_add_fusion.1._, bf16[768,1024]{1,0:T(8,128)(2,1)S(1)} %copy-done.17, bf16[768,256]{1,0:T(8,128)(2,1)S(1)} %copy-done.20, bf16[768,256]{1,0:T(8,128)(2,1)S(1)} %copy-done.13, f32[768,128]{1,0:T(8,128)S(1)} %get-tuple-element.324.cos_ref, ...), custom_call_target="tpu_custom_call" | custom-call | flops 8999999488 | bytes 5000000 | tf_op jit(solution)/shard_map/pallas_call | solution.py:103
  146.6 8.7 %fusion.9 = bf16[768,4096]{1,0:T(8,128)(2,1)} fusion(bf16[768,1024]{1,0:T(8,128)(2,1)S(1)} %get-tuple-element.145, bf16[2,1024,4096]{2,1,0:T(8,128)(2,1)S(1)} %bitcast.56), kind=kOutput, calls=%fused_computation.7 | convolution fusion | flops 6445596672 | bytes 16252928 | tf_op jit(solution)/shard_map/dot_general | solution.py:35
  169.8 21.2 %shard_map.125 = (bf16[768,1024]{1,0:T(8,128)(2,1)}, bf16[768,256]{1,0:T(8,128)(2,1)}, bf16[768,256]{1,0:T(8,128)(2,1)}, bf16[192,4096]{1,0:T(8,128)(2,1)}) custom-call(bf16[1,6,768,4096]{3,2,1,0:T(8,128)(2,1)} %embeds_hbm.5, bf16[768,4096]{1,0:T(8,128)(2,1)} %get-tuple-element.148.moved_hbm, f32[1,4096]{1,0:T(1,128)} %get-tuple-element.318.gain_ref, ...), custom_call_target="tpu_custom_call" | custom-call | flops 10000000000 | bytes 30000000 | tf_op jit(solution)/shard_map/pallas_call | solution.py:213
  194.4 15.6 %shard_map.126 = (bf16[768,1024]{1,0:T(8,128)(2,1)S(1)}, bf16[768,256]{1,0:T(8,128)(2,1)S(1)}) custom-call(s32[8]{0:T(128)S(1)} %pad_add_fusion.1._, bf16[768,1024]{1,0:T(8,128)(2,1)S(1)} %copy-done.18, bf16[768,256]{1,0:T(8,128)(2,1)S(1)} %copy-done.21, bf16[768,256]{1,0:T(8,128)(2,1)S(1)} %copy-done.14, f32[768,128]{1,0:T(8,128)S(1)} %get-tuple-element.324.cos_ref, ...), custom_call_target="tpu_custom_call" | custom-call | flops 8999999488 | bytes 5000000 | tf_op jit(solution)/shard_map/pallas_call | solution.py:103
  221.5 8.7 %fusion.12 = bf16[768,4096]{1,0:T(8,128)(2,1)} fusion(bf16[768,1024]{1,0:T(8,128)(2,1)S(1)} %get-tuple-element.156, bf16[2,1024,4096]{2,1,0:T(8,128)(2,1)S(1)} %bitcast.58), kind=kOutput, calls=%fused_computation.8 | convolution fusion | flops 6445596672 | bytes 16252928 | tf_op jit(solution)/shard_map/dot_general | solution.py:35
  236.2 29.2 %shard_map.127.act_1_ref = bf16[768,1536]{1,0:T(8,128)(2,1)} custom-call(bf16[192,4096]{1,0:T(8,128)(2,1)} %copy-done.24, bf16[96,4096]{1,0:T(8,128)(2,1)} %copy-done.34, bf16[96,4096]{1,0:T(8,128)(2,1)} %copy-done.32, bf16[192,4096]{1,0:T(8,128)(2,1)} %collective-permute-done.13.far_1_hbm, bf16[192,4096]{1,0:T(8,128)(2,1)} %copy-done.37, ...), custom_call_target="tpu_custom_call" | custom-call | flops 19327352832 | bytes 25165824 | tf_op jit(solution)/shard_map/pallas_call | solution.py:252
  271.9 35.9 %shard_map.128.act_2_ref = bf16[768,2048]{1,0:T(8,128)(2,1)} custom-call(bf16[192,4096]{1,0:T(8,128)(2,1)} %copy-done.24, bf16[96,4096]{1,0:T(8,128)(2,1)} %copy-done.34, bf16[96,4096]{1,0:T(8,128)(2,1)} %copy-done.32, bf16[192,4096]{1,0:T(8,128)(2,1)} %collective-permute-done.13.far_1_hbm, bf16[192,4096]{1,0:T(8,128)(2,1)} %copy-done.37, ...), custom_call_target="tpu_custom_call" | custom-call | flops 25769803776 | bytes 33554432 | tf_op jit(solution)/shard_map/pallas_call | solution.py:252
  322.2 28.9 %shard_map.129 = (bf16[192,4096]{1,0:T(8,128)(2,1)}, bf16[192,4096]{1,0:T(8,128)(2,1)}, bf16[192,4096]{1,0:T(8,128)(2,1)}, bf16[192,4096]{1,0:T(8,128)(2,1)}) custom-call(bf16[768,1536]{1,0:T(8,128)(2,1)} %shard_map.127.act_1_ref, bf16[768,2048]{1,0:T(8,128)(2,1)} %shard_map.128.act_2_ref, bf16[2,3584,4096]{2,1,0:T(8,128)(2,1)} %wd_hbm.1), custom_call_target="tpu_custom_call" | custom-call | flops 22548578304 | bytes 29360128 | tf_op jit(solution)/shard_map/pallas_call | solution.py:276
  360.2 30.0 %collective-permute-done.20.far_2_hbm = bf16[192,4096]{1,0:T(8,128)(2,1)} collective-permute-done((bf16[192,4096]{1,0:T(8,128)(2,1)}, bf16[192,4096]{1,0:T(8,128)(2,1)}, u32[]{:S(2)}, u32[]{:S(2)}) %collective-permute-start.20) | collective-permute-done | bytes 1572896 | tf_op jit(solution)/shard_map/ppermute | solution.py:602
  392.0 29.0 %shard_map.130.act_1_ref = bf16[768,1536]{1,0:T(8,128)(2,1)} custom-call(bf16[192,4096]{1,0:T(8,128)(2,1)} %copy-done.25, bf16[96,4096]{1,0:T(8,128)(2,1)} %copy-done.35, bf16[96,4096]{1,0:T(8,128)(2,1)} %copy-done.33, bf16[192,4096]{1,0:T(8,128)(2,1)} %collective-permute-done.19.far_1_hbm, bf16[192,4096]{1,0:T(8,128)(2,1)} %collective-permute-done.20.far_2_hbm, ...), custom_call_target="tpu_custom_call" | custom-call | flops 19327352832 | bytes 25165824 | tf_op jit(solution)/shard_map/pallas_call | solution.py:252
  439.6 36.1 %shard_map.131.act_2_ref = bf16[768,2048]{1,0:T(8,128)(2,1)} custom-call(bf16[192,4096]{1,0:T(8,128)(2,1)} %copy-done.25, bf16[96,4096]{1,0:T(8,128)(2,1)} %copy-done.35, bf16[96,4096]{1,0:T(8,128)(2,1)} %copy-done.33, bf16[192,4096]{1,0:T(8,128)(2,1)} %collective-permute-done.19.far_1_hbm, bf16[192,4096]{1,0:T(8,128)(2,1)} %collective-permute-done.20.far_2_hbm, ...), custom_call_target="tpu_custom_call" | custom-call | flops 25769803776 | bytes 33554432 | tf_op jit(solution)/shard_map/pallas_call | solution.py:252
  492.2 28.7 %shard_map.132 = (bf16[192,4096]{1,0:T(8,128)(2,1)}, bf16[192,4096]{1,0:T(8,128)(2,1)}, bf16[192,4096]{1,0:T(8,128)(2,1)}, bf16[192,4096]{1,0:T(8,128)(2,1)}) custom-call(bf16[768,1536]{1,0:T(8,128)(2,1)} %shard_map.130.act_1_ref, bf16[768,2048]{1,0:T(8,128)(2,1)} %shard_map.131.act_2_ref, bf16[2,3584,4096]{2,1,0:T(8,128)(2,1)} %wd_hbm.1), custom_call_target="tpu_custom_call" | custom-call | flops 22548578304 | bytes 29360128 | tf_op jit(solution)/shard_map/pallas_call | solution.py:276
  531.5 29.0 %shard_map.133.act_1_ref = bf16[768,1536]{1,0:T(8,128)(2,1)} custom-call(bf16[192,4096]{1,0:T(8,128)(2,1)} %copy-done.26, bf16[96,4096]{1,0:T(8,128)(2,1)} %collective-permute-done.21.near_1_hbm, bf16[96,4096]{1,0:T(8,128)(2,1)} %copy-done.36, bf16[192,4096]{1,0:T(8,128)(2,1)} %collective-permute-done.23.far_1_hbm, ...), custom_call_target="tpu_custom_call" | custom-call | flops 19327352832 | bytes 25165824 | tf_op jit(solution)/shard_map/pallas_call | solution.py:252
  576.0 35.9 %shard_map.135.act_2_ref = bf16[768,2048]{1,0:T(8,128)(2,1)} custom-call(bf16[192,4096]{1,0:T(8,128)(2,1)} %copy-done.26, bf16[96,4096]{1,0:T(8,128)(2,1)} %collective-permute-done.21.near_1_hbm, bf16[96,4096]{1,0:T(8,128)(2,1)} %copy-done.36, bf16[192,4096]{1,0:T(8,128)(2,1)} %collective-permute-done.23.far_1_hbm, ...), custom_call_target="tpu_custom_call" | custom-call | flops 25769803776 | bytes 33554432 | tf_op jit(solution)/shard_map/pallas_call | solution.py:252
  627.8 28.7 %shard_map.136 = (bf16[192,4096]{1,0:T(8,128)(2,1)}, bf16[192,4096]{1,0:T(8,128)(2,1)}, bf16[192,4096]{1,0:T(8,128)(2,1)}, bf16[192,4096]{1,0:T(8,128)(2,1)}) custom-call(bf16[768,1536]{1,0:T(8,128)(2,1)} %shard_map.133.act_1_ref, bf16[768,2048]{1,0:T(8,128)(2,1)} %shard_map.135.act_2_ref, bf16[2,3584,4096]{2,1,0:T(8,128)(2,1)} %wd_hbm.1), custom_call_target="tpu_custom_call" | custom-call | flops 22548578304 | bytes 29360128 | tf_op jit(solution)/shard_map/pallas_call | solution.py:276
  673.2 8.4 %shard_map.137.kv1_ref = bf16[192,2048]{1,0:T(8,128)(2,1)S(1)} custom-call(s32[1]{0:T(128)} %bitcast.2.part_ref, bf16[192,4096]{1,0:T(8,128)(2,1)} %fusion.25.x_ref.x1_ref, f32[1,4096]{1,0:T(1,128)S(1)} %copy-done.10, f32[192,128]{1,0:T(8,128)S(1)} %pad_maximum_fusion.16.cos_ref, f32[192,128]{1,0:T(8,128)S(1)} %pad_maximum_fusion.17.sin_ref, ...), custom_call_target="tpu_custom_call" | custom-call | flops 3221225472 | bytes 16777216 | tf_op jit(solution)/shard_map/pallas_call | solution.py:313
  709.7 12.9 %collective-permute-done.50 = bf16[96,4096]{1,0:T(8,128)(2,1)S(1)} collective-permute-done((bf16[96,4096]{1,0:T(8,128)(2,1)S(1)}, bf16[96,4096]{1,0:T(8,128)(2,1)S(1)}, u32[]{:S(2)}, u32[]{:S(2)}) %collective-permute-start.50) | collective-permute-done | bytes 786464 | tf_op jit(solution)/shard_map/ppermute | solution.py:599
  724.6 8.5 %shard_map.140.kv2_ref = bf16[192,2048]{1,0:T(8,128)(2,1)S(1)} custom-call(s32[1]{0:T(128)} %bitcast.2.part_ref, bf16[192,4096]{1,0:T(8,128)(2,1)} %fusion.29.x_ref.x2_ref, f32[1,4096]{1,0:T(1,128)S(1)} %copy-done.10, f32[192,128]{1,0:T(8,128)S(1)} %pad_maximum_fusion.16.cos_ref, f32[192,128]{1,0:T(8,128)S(1)} %pad_maximum_fusion.17.sin_ref, ...), custom_call_target="tpu_custom_call" | custom-call | flops 3221225472 | bytes 16777216 | tf_op jit(solution)/shard_map/pallas_call | solution.py:313
  758.4 52.2 %shard_map.141 = bf16[8,4096]{1,0:T(8,128)(2,1)} custom-call(bf16[192,4096]{1,0:T(8,128)(2,1)} %fusion.21.x_ref.x0_ref, bf16[192,4096]{1,0:T(8,128)(2,1)} %fusion.25.x_ref.x1_ref, bf16[192,4096]{1,0:T(8,128)(2,1)} %fusion.29.x_ref.x2_ref, bf16[192,2048]{1,0:T(8,128)(2,1)} %copy-done.6, bf16[192,2048]{1,0:T(8,128)(2,1)} %copy-done.7, ...), custom_call_target="tpu_custom_call" | custom-call | flops 8999999488 | bytes 60000000 | tf_op jit(solution)/shard_map/pallas_call | solution.py:489
  (343 shorter events, 281.9 us)
Async XLA Ops:
  21.1 64.2 %collective-permute-start.31 = (bf16[1024,512]{1,0:T(8,128)(2,1)}, bf16[1024,512]{1,0:T(8,128)(2,1)S(1)}, u32[]{:S(2)}, u32[]{:S(2)}) collective-permute-start(bf16[1024,512]{1,0:T(8,128)(2,1)} %pad_maximum_fusion.7.refs_0_), channel_id=1, source_target_pairs={{0,4},{4,0},{1,5},{5,1},{2,6},{6,2},{3,7},{7,3}} | collective-permute-start | bytes 3145736 | tf_op jit(solution)/shard_map/ppermute | solution.py:602
  23.4 327.7 %collective-permute-start.29 = (bf16[1024,512]{1,0:T(8,128)(2,1)}, bf16[1024,512]{1,0:T(8,128)(2,1)}, u32[]{:S(2)}, u32[]{:S(2)}) collective-permute-start(bf16[1024,512]{1,0:T(8,128)(2,1)} %pad_maximum_fusion.7.refs_0_), channel_id=1, source_target_pairs={{0,2},{2,0},{1,3},{3,1},{4,6},{6,4},{5,7},{7,5}} | collective-permute-start | bytes 3145736 | tf_op jit(solution)/shard_map/ppermute | solution.py:599
  24.9 60.3 %collective-permute-start.30 = (bf16[1024,512]{1,0:T(8,128)(2,1)S(1)}, bf16[1024,512]{1,0:T(8,128)(2,1)S(1)}, u32[]{:S(2)}, u32[]{:S(2)}) collective-permute-start(bf16[1024,512]{1,0:T(8,128)(2,1)S(1)} %pad_maximum_fusion.8.refs_1_), channel_id=1, source_target_pairs={{0,2},{2,0},{1,3},{3,1},{4,6},{6,4},{5,7},{7,5}} | collective-permute-start | bytes 3145736 | tf_op jit(solution)/shard_map/ppermute | solution.py:599
  159.2 53.8 %collective-permute-start.8 = (bf16[192,4096]{1,0:T(8,128)(2,1)}, bf16[192,4096]{1,0:T(8,128)(2,1)}, u32[]{:S(2)}, u32[]{:S(2)}) collective-permute-start(bf16[192,4096]{1,0:T(8,128)(2,1)} %get-tuple-element.261), channel_id=1, source_target_pairs={{0,4},{4,0},{1,5},{5,1},{2,6},{6,2},{3,7},{7,3}} | collective-permute-start | bytes 4718600 | tf_op jit(solution)/shard_map/ppermute | solution.py:602
  160.4 52.6 %collective-permute-start.7 = (bf16[192,4096]{1,0:T(8,128)(2,1)}, bf16[192,4096]{1,0:T(8,128)(2,1)}, u32[]{:S(2)}, u32[]{:S(2)}) collective-permute-start(bf16[192,4096]{1,0:T(8,128)(2,1)} %get-tuple-element.262), channel_id=1, source_target_pairs={{0,2},{2,0},{1,3},{3,1},{4,6},{6,4},{5,7},{7,5}} | collective-permute-start | bytes 4718600 | tf_op jit(solution)/shard_map/ppermute | solution.py:599
  167.5 66.6 %collective-permute-start.14 = (bf16[192,4096]{1,0:T(8,128)(2,1)}, bf16[192,4096]{1,0:T(8,128)(2,1)S(1)}, u32[]{:S(2)}, u32[]{:S(2)}) collective-permute-start(bf16[192,4096]{1,0:T(8,128)(2,1)} %pad_maximum_fusion.2), channel_id=1, source_target_pairs={{0,4},{4,0},{1,5},{5,1},{2,6},{6,2},{3,7},{7,3}} | collective-permute-start | bytes 4718600 | tf_op jit(solution)/shard_map/ppermute | solution.py:602
  169.6 66.4 %collective-permute-start.13 = (bf16[192,4096]{1,0:T(8,128)(2,1)}, bf16[192,4096]{1,0:T(8,128)(2,1)}, u32[]{:S(2)}, u32[]{:S(2)}) collective-permute-start(bf16[192,4096]{1,0:T(8,128)(2,1)} %pad_maximum_fusion.1), channel_id=1, source_target_pairs={{0,2},{2,0},{1,3},{3,1},{4,6},{6,4},{5,7},{7,5}} | collective-permute-start | bytes 4718600 | tf_op jit(solution)/shard_map/ppermute | solution.py:599
  219.5 45.9 %collective-permute-start.12 = (bf16[96,4096]{1,0:T(8,128)(2,1)}, bf16[96,4096]{1,0:T(8,128)(2,1)S(1)}, u32[]{:S(2)}, u32[]{:S(2)}) collective-permute-start(bf16[96,4096]{1,0:T(8,128)(2,1)} %get-tuple-element.298), channel_id=1, source_target_pairs={{0,2},{2,0},{1,3},{3,1},{4,6},{6,4},{5,7},{7,5}} | collective-permute-start | bytes 2359304 | tf_op jit(solution)/shard_map/ppermute | solution.py:599
  221.3 44.0 %collective-permute-start.11 = (bf16[96,4096]{1,0:T(8,128)(2,1)}, bf16[96,4096]{1,0:T(8,128)(2,1)}, u32[]{:S(2)}, u32[]{:S(2)}) collective-permute-start(bf16[96,4096]{1,0:T(8,128)(2,1)} %get-tuple-element.296), channel_id=1, source_target_pairs={{0,4},{4,0},{1,5},{5,1},{2,6},{6,2},{3,7},{7,3}} | collective-permute-start | bytes 2359304 | tf_op jit(solution)/shard_map/ppermute | solution.py:602
  234.1 80.0 %collective-permute-start.10 = (bf16[192,4096]{1,0:T(8,128)(2,1)}, bf16[192,4096]{1,0:T(8,128)(2,1)}, u32[]{:S(2)}, u32[]{:S(2)}) collective-permute-start(bf16[192,4096]{1,0:T(8,128)(2,1)} %get-tuple-element.257), channel_id=1, source_target_pairs={{0,4},{4,0},{1,5},{5,1},{2,6},{6,2},{3,7},{7,3}} | collective-permute-start | bytes 4718600 | tf_op jit(solution)/shard_map/ppermute | solution.py:602
  236.0 79.7 %collective-permute-start.9 = (bf16[192,4096]{1,0:T(8,128)(2,1)}, bf16[192,4096]{1,0:T(8,128)(2,1)}, u32[]{:S(2)}, u32[]{:S(2)}) collective-permute-start(bf16[192,4096]{1,0:T(8,128)(2,1)} %get-tuple-element.258), channel_id=1, source_target_pairs={{0,2},{2,0},{1,3},{3,1},{4,6},{6,4},{5,7},{7,5}} | collective-permute-start | bytes 4718600 | tf_op jit(solution)/shard_map/ppermute | solution.py:599
  307.9 44.4 %collective-permute-start.32 = (bf16[1024,512]{1,0:T(8,128)(2,1)S(1)}, bf16[1024,512]{1,0:T(8,128)(2,1)S(1)}, u32[]{:S(2)}, u32[]{:S(2)}) collective-permute-start(bf16[1024,512]{1,0:T(8,128)(2,1)S(1)} %copy-done.1), channel_id=1, source_target_pairs={{0,4},{4,0},{1,5},{5,1},{2,6},{6,2},{3,7},{7,3}} | collective-permute-start | bytes 3145736 | tf_op jit(solution)/shard_map/ppermute | solution.py:602
  315.6 74.5 %collective-permute-start.20 = (bf16[192,4096]{1,0:T(8,128)(2,1)}, bf16[192,4096]{1,0:T(8,128)(2,1)}, u32[]{:S(2)}, u32[]{:S(2)}) collective-permute-start(bf16[192,4096]{1,0:T(8,128)(2,1)} %pad_maximum_fusion.4), channel_id=1, source_target_pairs={{0,4},{4,0},{1,5},{5,1},{2,6},{6,2},{3,7},{7,3}} | collective-permute-start | bytes 4718600 | tf_op jit(solution)/shard_map/ppermute | solution.py:602
  352.3 129.0 %collective-permute-start.25 = (bf16[192,4096]{1,0:T(8,128)(2,1)}, bf16[192,4096]{1,0:T(8,128)(2,1)}, u32[]{:S(2)}, u32[]{:S(2)}) collective-permute-start(bf16[192,4096]{1,0:T(8,128)(2,1)} %get-tuple-element.172), channel_id=1, source_target_pairs={{0,2},{2,0},{1,3},{3,1},{4,6},{6,4},{5,7},{7,5}} | collective-permute-start | bytes 4718600 | tf_op jit(solution)/shard_map/ppermute | solution.py:599
  353.1 128.1 %collective-permute-start.26 = (bf16[192,4096]{1,0:T(8,128)(2,1)}, bf16[192,4096]{1,0:T(8,128)(2,1)}, u32[]{:S(2)}, u32[]{:S(2)}) collective-permute-start(bf16[192,4096]{1,0:T(8,128)(2,1)} %get-tuple-element.173), channel_id=1, source_target_pairs={{0,4},{4,0},{1,5},{5,1},{2,6},{6,2},{3,7},{7,3}} | collective-permute-start | bytes 4718600 | tf_op jit(solution)/shard_map/ppermute | solution.py:602
  356.5 166.5 %collective-permute-start.35 = (bf16[1024,512]{1,0:T(8,128)(2,1)}, bf16[1024,512]{1,0:T(8,128)(2,1)}, u32[]{:S(2)}, u32[]{:S(2)}) collective-permute-start(bf16[1024,512]{1,0:T(8,128)(2,1)} %collective-permute-done.29.refs_2_), channel_id=1, source_target_pairs={{0,1},{1,0},{2,3},{3,2},{4,5},{5,4},{6,7},{7,6}} | collective-permute-start | bytes 3145736 | tf_op jit(solution)/shard_map/ppermute | solution.py:605
  564.5 47.4 %collective-permute-start.41 = (bf16[192,4096]{1,0:T(8,128)(2,1)}, bf16[192,4096]{1,0:T(8,128)(2,1)}, u32[]{:S(2)}, u32[]{:S(2)}) collective-permute-start(bf16[192,4096]{1,0:T(8,128)(2,1)} %get-tuple-element.190), channel_id=1, source_target_pairs={{0,2},{2,0},{1,3},{3,1},{4,6},{6,4},{5,7},{7,5}} | collective-permute-start | bytes 4718600 | tf_op jit(solution)/shard_map/ppermute | solution.py:599
  565.9 46.0 %collective-permute-start.42 = (bf16[192,4096]{1,0:T(8,128)(2,1)}, bf16[192,4096]{1,0:T(8,128)(2,1)}, u32[]{:S(2)}, u32[]{:S(2)}) collective-permute-start(bf16[192,4096]{1,0:T(8,128)(2,1)} %get-tuple-element.191), channel_id=1, source_target_pairs={{0,4},{4,0},{1,5},{5,1},{2,6},{6,2},{3,7},{7,3}} | collective-permute-start | bytes 4718600 | tf_op jit(solution)/shard_map/ppermute | solution.py:602
  619.2 62.4 %collective-permute-start.46 = (bf16[3,768,512]{2,1,0:T(8,128)(2,1)}, bf16[3,768,512]{2,1,0:T(8,128)(2,1)}, u32[]{:S(2)}, u32[]{:S(2)}) collective-permute-start(bf16[3,768,512]{2,1,0:T(8,128)(2,1)} %pad_maximum_fusion), channel_id=1, source_target_pairs={{2,1},{1,3},{6,5},{5,7}} | collective-permute-start | bytes 7077896 | tf_op jit(solution)/shard_map/ppermute | solution.py:765
  621.4 68.4 %collective-permute-start.45 = (bf16[3,768,512]{2,1,0:T(8,128)(2,1)}, bf16[3,768,512]{2,1,0:T(8,128)(2,1)}, u32[]{:S(2)}, u32[]{:S(2)}) collective-permute-start(bf16[3,768,512]{2,1,0:T(8,128)(2,1)} %pad_maximum_fusion), channel_id=1, source_target_pairs={{0,1},{3,3},{4,5},{7,7}} | collective-permute-start | bytes 7077896 | tf_op jit(solution)/shard_map/ppermute | solution.py:765
  739.2 72.9 %collective-permute-start.59 = (bf16[2,192,1024]{2,1,0:T(8,128)(2,1)}, bf16[2,192,1024]{2,1,0:T(8,128)(2,1)}, u32[]{:S(2)}, u32[]{:S(2)}) collective-permute-start(bf16[2,192,1024]{2,1,0:T(8,128)(2,1)} %pad_maximum_fusion.13), channel_id=1, source_target_pairs={{2,1},{1,3},{6,5},{5,7}} | collective-permute-start | bytes 2359304 | tf_op jit(solution)/shard_map/ppermute | solution.py:765
  740.8 71.3 %collective-permute-start.58 = (bf16[2,192,1024]{2,1,0:T(8,128)(2,1)}, bf16[2,192,1024]{2,1,0:T(8,128)(2,1)}, u32[]{:S(2)}, u32[]{:S(2)}) collective-permute-start(bf16[2,192,1024]{2,1,0:T(8,128)(2,1)} %pad_maximum_fusion.13), channel_id=1, source_target_pairs={{0,1},{3,3},{4,5},{7,7}} | collective-permute-start | bytes 2359304 | tf_op jit(solution)/shard_map/ppermute | solution.py:765
  749.6 69.0 %collective-permute-start.56 = (bf16[2,192,1024]{2,1,0:T(8,128)(2,1)}, bf16[2,192,1024]{2,1,0:T(8,128)(2,1)S(1)}, u32[]{:S(2)}, u32[]{:S(2)}) collective-permute-start(bf16[2,192,1024]{2,1,0:T(8,128)(2,1)} %pad_maximum_fusion.12), channel_id=1, source_target_pairs={{2,1},{1,3},{6,5},{5,7}} | collective-permute-start | bytes 2359304 | tf_op jit(solution)/shard_map/ppermute | solution.py:765
  750.3 68.3 %collective-permute-start.55 = (bf16[2,192,1024]{2,1,0:T(8,128)(2,1)}, bf16[2,192,1024]{2,1,0:T(8,128)(2,1)}, u32[]{:S(2)}, u32[]{:S(2)}) collective-permute-start(bf16[2,192,1024]{2,1,0:T(8,128)(2,1)} %pad_maximum_fusion.12), channel_id=1, source_target_pairs={{0,1},{3,3},{4,5},{7,7}} | collective-permute-start | bytes 2359304 | tf_op jit(solution)/shard_map/ppermute | solution.py:765
  (108 other events, 2143.1 us)

commit v3 on v2

--- a/solution.py
+++ b/solution.py
@@ -118,7 +118,7 @@
             ],
         ),
         out_shape=[jax.ShapeDtypeStruct(q.shape, jnp.bfloat16), jax.ShapeDtypeStruct(k.shape, jnp.bfloat16)],
-        compiler_params=params(32),
+        compiler_params=params(16),
         cost_estimate=cost(9_000_000_000, 5_000_000),
     )(order, q, k, v, cos_t, sin_t)
 
@@ -221,7 +221,7 @@
         out_specs=out_specs,
         out_shape=out_shape,
         scratch_shapes=scratch,
-        compiler_params=params(56, **extra),
+        compiler_params=params(38, **extra),
         cost_estimate=cost(10_000_000_000, 30_000_000),
     )(embeds, moved, gain, w_query, w_key, w_value)
 
@@ -256,7 +256,7 @@
         out_specs=pl.BlockSpec((8 * block, tile), lambda j: (0, j)),
         out_shape=jax.ShapeDtypeStruct((8 * block, count * tile), jnp.bfloat16),
         scratch_shapes=[pltpu.VMEM((8 * block, width), jnp.bfloat16), pltpu.SemaphoreType.DMA((6,))],
-        compiler_params=params(56),
+        compiler_params=params(20),
         cost_estimate=cost(32 * block * width * count * tile, 4 * width * count * tile),
     )(own, near_1, near_2, far_1, far_2, w_gate, w_up)
 
@@ -280,7 +280,7 @@
                   pl.BlockSpec((1, depth, tile), lambda j: (0, 0, j))],
         out_specs=[pl.BlockSpec((rows // 4, tile), lambda j: (0, j))] * 4,
         out_shape=[jax.ShapeDtypeStruct((rows // 4, width), jnp.bfloat16)] * 4,
-        compiler_params=params(56),
+        compiler_params=params(24),
         cost_estimate=cost(2 * rows * depth * width, 2 * depth * width),
     )(act_1, act_2, w_down)
 
@@ -316,7 +316,7 @@
         out_specs=vmem,
         out_shape=jax.ShapeDtypeStruct((rows, 4 * columns), jnp.bfloat16),
         scratch_shapes=[pltpu.VMEM((2, rows, 2 * depth), jnp.bfloat16)],
-        compiler_params=params(40),
+        compiler_params=params(26),
         cost_estimate=cost(32 * rows * depth * columns, 32 * depth * columns),
     )(part, x, gain, cos_rows, sin_rows, *mine, *other)
 
@@ -541,7 +541,7 @@
         first_cut_kernel,
         grid_spec=pltpu.PrefetchScalarGridSpec(num_scalar_prefetch=1, grid=(n_chunk, 2), in_specs=[source] * 2, out_specs=[target] * 2),
         out_shape=[jax.ShapeDtypeStruct((1, 2, n_chunk, seq_len, heads, HEAD_DIM), jnp.bfloat16)] * 2,
-        compiler_params=params(32),
+        compiler_params=params(16),
         cost_estimate=cost(1_000_000_000, 19_000_000),
     )(where, near, far)
 
@@ -582,7 +582,7 @@
             num_scalar_prefetch=1, grid=(2, 2, 2), in_specs=[source] * 2 + [whole] * 2, out_specs=[target] * 2),
         out_shape=[jax.ShapeDtypeStruct(k_cache.shape, jnp.bfloat16)] * 2,
         input_output_aliases={3: 0, 4: 1},
-        compiler_params=params(32),
+        compiler_params=params(16),
         cost_estimate=cost(300_000_000, 5_000_000),
     )(where, near, far, k_cache, v_cache)
 
@@ -685,7 +685,7 @@
         def out_of(mix):
             return quarters(matmul(mix, w_out[0]).astype(jnp.bfloat16))
 
-        mlp_tile = 512
+        mlp_tile = w_key.shape[2]
         n_tiles = w_gate.shape[2] // mlp_tile
         first_tiles = n_tiles // 2
 
@@ -694,7 +694,7 @@
             return gate_up(h, got[0], got[1], far[0], far[1], w_gate, w_up, start, count, mlp_tile)
 
         def down_of(act_1, act_2):
-            return down(act_1, act_2, w_down, mlp_tile)
+            return down(act_1, act_2, w_down, 2 * mlp_tile)
 
         own_cos, own_sin = own_rows(cos_t), own_rows(sin_t)
 

time: 837 us -> 779 us (0.931)
  Pallas kernels: 492 us -> 442 us
  waiting for transfers between devices: 89.2 us -> 137 us
  other arithmetic: 66.9 us -> 36 us
  local copies, waits for them, and re-layouts: 57.3 us -> 32.2 us
    ppermute x24, waiting for transfers between devices: 51.3 us -> 90.1 us  [over_y(): return lax.ppermute(value, 'b', SWAP)]
    pallas_call x6, Pallas kernels: 195 us -> 167 us  [gate_up(): pl.pallas_call(gate_up_kernel, grid=(count,), in_specs=[hbm] * 5 + [weigh...]
    convert_element_type x12, other arithmetic: 32.8 us -> 16.2 us  [add_rounded(): (left.astype(jnp.float32) + right.astype(jnp.float32)).astype(jnp.bfloat16)]
    ppermute x21, waiting for transfers between devices: 37.8 us -> 46.5 us  [over_x(): return lax.ppermute(value, 'a', SWAP)]
    unnamed x142 -> x84, local copies, waits for them, and re-layouts: 19.2 us -> 11.2 us
  transfers between devices with their start and end apart: 60 -> 60, of which waited for: 12 -> 17; matrix products, arithmetic and copies ran while one was open for 14% -> 10% of each run, Pallas kernels for 59% -> 57%
where the time goes in v3:
time: 779 us; the launch traced here: 768 us
  Pallas kernels  442 us (57%)
  waiting for transfers between devices  137 us (18%)
  starting transfers between devices  86 us (11%)
  other arithmetic  36 us (5%)
  matrix products  32.9 us (4%)
  local copies, waits for them, and re-layouts  32.2 us (4%)
    pallas_call x6, Pallas kernels, gate_up(): pl.pallas_call(gate_up_kernel, grid=(count,), in_specs=[hbm] * 5 + [weigh...  167 us
    ppermute x24, waiting for transfers between devices, over_y(): return lax.ppermute(value, 'b', SWAP)  90.1 us
    pallas_call x3, Pallas kernels, down(): pl.pallas_call(down_kernel, grid=(width // tile,), in_specs=[pl.BlockSpec...  79.4 us
    pallas_call x3, Pallas kernels, projections(): pl.pallas_call(functools.partial(project_kernel, request, next_request),...  55.8 us
    pallas_call x1, Pallas kernels, last_rows(): pl.pallas_call(functools.partial(tail_kernel, kv_heads), grid=(1,), in_sp...  52.2 us
    ppermute x21, waiting for transfers between devices, over_x(): return lax.ppermute(value, 'a', SWAP)  46.5 us
    pallas_call x3, Pallas kernels, attention(): pl.pallas_call(functools.partial(attention_kernel, q_block, group), grid_...  46.5 us
    dot_general x3, matrix products, matmul(): return jnp.dot(left, right, preferred_element_type=jnp.float32)  32.9 us
  transfers between devices with their start and end apart: 60, of which 17 were waited for; matrix products, arithmetic and copies ran while one was open for 10% of the time, Pallas kernels for 57%

profile of v3, /device:TPU:0, one launch (start us, length us, event | category | flops | bytes accessed | tf_op | source)
XLA Modules:
  0.0 768.2 jit_solution(9660669614987060922)
XLA Ops:
  30.9 18.3 %shard_map.121 = (bf16[768,1024]{1,0:T(8,128)(2,1)S(1)}, bf16[768,256]{1,0:T(8,128)(2,1)S(1)}, bf16[768,256]{1,0:T(8,128)(2,1)S(1)}, bf16[192,4096]{1,0:T(8,128)(2,1)S(1)}, bf16[768,4096]{1,0:T(8,128)(2,1)}) custom-call(bf16[1,6,768,4096]{3,2,1,0:T(8,128)(2,1)} %embeds_hbm.5, bf16[768,4096]{1,0:T(8,128)(2,1)} %collective-permute-done.moved_hbm, ...), custom_call_target="tpu_custom_call" | custom-call | flops 10000000000 | bytes 30000000 | tf_op jit(solution)/shard_map/pallas_call | solution.py:213
  49.2 15.7 %shard_map.122 = (bf16[768,1024]{1,0:T(8,128)(2,1)S(1)}, bf16[768,256]{1,0:T(8,128)(2,1)S(1)}) custom-call(s32[8]{0:T(128)S(1)} %pad_add_fusion.1._, bf16[768,1024]{1,0:T(8,128)(2,1)S(1)} %get-tuple-element.127.q_ref, bf16[768,256]{1,0:T(8,128)(2,1)S(1)} %get-tuple-element.128.k_ref, bf16[768,256]{1,0:T(8,128)(2,1)S(1)} %get-tuple-element.129.v_ref, ...), custom_call_target="tpu_custom_call" | custom-call | flops 8999999488 | bytes 5000000 | tf_op jit(solution)/shard_map/pallas_call | solution.py:103
  80.3 18.9 %shard_map.123 = (bf16[768,1024]{1,0:T(8,128)(2,1)S(1)}, bf16[768,256]{1,0:T(8,128)(2,1)S(1)}, bf16[768,256]{1,0:T(8,128)(2,1)S(1)}, bf16[192,4096]{1,0:T(8,128)(2,1)S(1)}, bf16[768,4096]{1,0:T(8,128)(2,1)}) custom-call(bf16[1,6,768,4096]{3,2,1,0:T(8,128)(2,1)} %embeds_hbm.5, bf16[768,4096]{1,0:T(8,128)(2,1)} %get-tuple-element.131.moved_hbm, ...), custom_call_target="tpu_custom_call" | custom-call | flops 10000000000 | bytes 30000000 | tf_op jit(solution)/shard_map/pallas_call | solution.py:213
  99.2 13.6 %collective-permute-done.2 = bf16[192,4096]{1,0:T(8,128)(2,1)S(1)} collective-permute-done((bf16[192,4096]{1,0:T(8,128)(2,1)S(1)}, bf16[192,4096]{1,0:T(8,128)(2,1)S(1)}, u32[]{:S(2)}, u32[]{:S(2)}) %collective-permute-start.2) | collective-permute-done | bytes 1572896 | tf_op jit(solution)/shard_map/ppermute | solution.py:602
  119.5 15.4 %shard_map.124 = (bf16[768,1024]{1,0:T(8,128)(2,1)S(1)}, bf16[768,256]{1,0:T(8,128)(2,1)S(1)}) custom-call(s32[8]{0:T(128)S(1)} %pad_add_fusion.1._, bf16[768,1024]{1,0:T(8,128)(2,1)S(1)} %get-tuple-element.139.q_ref, bf16[768,256]{1,0:T(8,128)(2,1)S(1)} %get-tuple-element.140.k_ref, bf16[768,256]{1,0:T(8,128)(2,1)S(1)} %get-tuple-element.141.v_ref, ...), custom_call_target="tpu_custom_call" | custom-call | flops 8999999488 | bytes 5000000 | tf_op jit(solution)/shard_map/pallas_call | solution.py:103
  138.8 12.0 %fusion.9 = bf16[768,4096]{1,0:T(8,128)(2,1)} fusion(bf16[768,1024]{1,0:T(8,128)(2,1)S(1)} %get-tuple-element.145, bf16[2,1024,4096]{2,1,0:T(8,128)(2,1)} %wo_hbm.1), kind=kOutput, calls=%fused_computation.7 | convolution fusion | flops 6445596672 | bytes 16252928 | tf_op jit(solution)/shard_map/dot_general | solution.py:35
  161.3 18.6 %shard_map.125 = (bf16[768,1024]{1,0:T(8,128)(2,1)S(1)}, bf16[768,256]{1,0:T(8,128)(2,1)S(1)}, bf16[768,256]{1,0:T(8,128)(2,1)S(1)}, bf16[192,4096]{1,0:T(8,128)(2,1)S(1)}) custom-call(bf16[1,6,768,4096]{3,2,1,0:T(8,128)(2,1)} %embeds_hbm.5, bf16[768,4096]{1,0:T(8,128)(2,1)} %get-tuple-element.148.moved_hbm, f32[1,4096]{1,0:T(1,128)S(1)} %get-tuple-element.318.gain_ref, ...), custom_call_target="tpu_custom_call" | custom-call | flops 10000000000 | bytes 30000000 | tf_op jit(solution)/shard_map/pallas_call | solution.py:213
  180.0 15.4 %shard_map.126 = (bf16[768,1024]{1,0:T(8,128)(2,1)S(1)}, bf16[768,256]{1,0:T(8,128)(2,1)S(1)}) custom-call(s32[8]{0:T(128)S(1)} %pad_add_fusion.1._, bf16[768,1024]{1,0:T(8,128)(2,1)S(1)} %get-tuple-element.150.q_ref, bf16[768,256]{1,0:T(8,128)(2,1)S(1)} %get-tuple-element.151.k_ref, bf16[768,256]{1,0:T(8,128)(2,1)S(1)} %get-tuple-element.152.v_ref, ...), custom_call_target="tpu_custom_call" | custom-call | flops 8999999488 | bytes 5000000 | tf_op jit(solution)/shard_map/pallas_call | solution.py:103
  202.8 10.5 %fusion.12 = bf16[768,4096]{1,0:T(8,128)(2,1)S(1)} fusion(bf16[768,1024]{1,0:T(8,128)(2,1)S(1)} %get-tuple-element.156, bf16[2,1024,4096]{2,1,0:T(8,128)(2,1)} %wo_hbm.1), kind=kOutput, calls=%fused_computation.8 | convolution fusion | flops 6445596672 | bytes 16252928 | tf_op jit(solution)/shard_map/dot_general | solution.py:35
  228.2 27.8 %shard_map.127.act_1_ref = bf16[768,1792]{1,0:T(8,128)(2,1)S(1)} custom-call(bf16[192,4096]{1,0:T(8,128)(2,1)S(1)} %fusion.20.own_hbm, bf16[96,4096]{1,0:T(8,128)(2,1)S(1)} %collective-permute-done.5.near_1_hbm, bf16[96,4096]{1,0:T(8,128)(2,1)S(1)} %collective-permute-done.6.near_2_hbm, bf16[192,4096]{1,0:T(8,128)(2,1)S(1)} %collective-permute-done.13.far_1_hbm, ...), custom_call_target="tpu_custom_call" | custom-call | flops 22548578304 | bytes 29360128 | tf_op jit(solution)/shard_map/pallas_call | solution.py:252
  260.0 27.6 %shard_map.128.act_2_ref = bf16[768,1792]{1,0:T(8,128)(2,1)S(1)} custom-call(bf16[192,4096]{1,0:T(8,128)(2,1)S(1)} %fusion.20.own_hbm, bf16[96,4096]{1,0:T(8,128)(2,1)S(1)} %collective-permute-done.5.near_1_hbm, bf16[96,4096]{1,0:T(8,128)(2,1)S(1)} %collective-permute-done.6.near_2_hbm, bf16[192,4096]{1,0:T(8,128)(2,1)S(1)} %collective-permute-done.13.far_1_hbm, ...), custom_call_target="tpu_custom_call" | custom-call | flops 22548578304 | bytes 29360128 | tf_op jit(solution)/shard_map/pallas_call | solution.py:252
  299.9 26.5 %shard_map.129 = (bf16[192,4096]{1,0:T(8,128)(2,1)S(1)}, bf16[192,4096]{1,0:T(8,128)(2,1)S(1)}, bf16[192,4096]{1,0:T(8,128)(2,1)S(1)}, bf16[192,4096]{1,0:T(8,128)(2,1)S(1)}) custom-call(bf16[768,1792]{1,0:T(8,128)(2,1)S(1)} %shard_map.127.act_1_ref, bf16[768,1792]{1,0:T(8,128)(2,1)S(1)} %shard_map.128.act_2_ref, bf16[2,3584,4096]{2,1,0:T(8,128)(2,1)} %wd_hbm.1), custom_call_target="tpu_custom_call" | custom-call | flops 22548578304 | bytes 29360128 | tf_op jit(solution)/shard_map/pallas_call | solution.py:276
  340.2 33.4 %collective-permute-done.20.far_2_hbm = bf16[192,4096]{1,0:T(8,128)(2,1)S(1)} collective-permute-done((bf16[192,4096]{1,0:T(8,128)(2,1)}, bf16[192,4096]{1,0:T(8,128)(2,1)S(1)}, u32[]{:S(2)}, u32[]{:S(2)}) %collective-permute-start.20) | collective-permute-done | bytes 1572896 | tf_op jit(solution)/shard_map/ppermute | solution.py:602
  375.1 27.8 %shard_map.130.act_1_ref = bf16[768,1792]{1,0:T(8,128)(2,1)S(1)} custom-call(bf16[192,4096]{1,0:T(8,128)(2,1)S(1)} %fusion.24.own_hbm, bf16[96,4096]{1,0:T(8,128)(2,1)S(1)} %collective-permute-done.15.near_1_hbm, bf16[96,4096]{1,0:T(8,128)(2,1)S(1)} %collective-permute-done.16.near_2_hbm, bf16[192,4096]{1,0:T(8,128)(2,1)S(1)} %collective-permute-done.19.far_1_hbm, ...), custom_call_target="tpu_custom_call" | custom-call | flops 22548578304 | bytes 29360128 | tf_op jit(solution)/shard_map/pallas_call | solution.py:252
  405.5 12.3 %collective-permute-done.17 = bf16[96,4096]{1,0:T(8,128)(2,1)S(1)} collective-permute-done((bf16[96,4096]{1,0:T(8,128)(2,1)S(1)}, bf16[96,4096]{1,0:T(8,128)(2,1)S(1)}, u32[]{:S(2)}, u32[]{:S(2)}) %collective-permute-start.17) | collective-permute-done | bytes 786464 | tf_op jit(solution)/shard_map/ppermute | solution.py:602
  422.7 28.0 %shard_map.131.act_2_ref = bf16[768,1792]{1,0:T(8,128)(2,1)S(1)} custom-call(bf16[192,4096]{1,0:T(8,128)(2,1)S(1)} %fusion.24.own_hbm, bf16[96,4096]{1,0:T(8,128)(2,1)S(1)} %collective-permute-done.15.near_1_hbm, bf16[96,4096]{1,0:T(8,128)(2,1)S(1)} %collective-permute-done.16.near_2_hbm, bf16[192,4096]{1,0:T(8,128)(2,1)S(1)} %collective-permute-done.19.far_1_hbm, ...), custom_call_target="tpu_custom_call" | custom-call | flops 22548578304 | bytes 29360128 | tf_op jit(solution)/shard_map/pallas_call | solution.py:252
  456.5 26.5 %shard_map.132 = (bf16[192,4096]{1,0:T(8,128)(2,1)S(1)}, bf16[192,4096]{1,0:T(8,128)(2,1)S(1)}, bf16[192,4096]{1,0:T(8,128)(2,1)S(1)}, bf16[192,4096]{1,0:T(8,128)(2,1)S(1)}) custom-call(bf16[768,1792]{1,0:T(8,128)(2,1)S(1)} %shard_map.130.act_1_ref, bf16[768,1792]{1,0:T(8,128)(2,1)S(1)} %shard_map.131.act_2_ref, bf16[2,3584,4096]{2,1,0:T(8,128)(2,1)} %wd_hbm.1), custom_call_target="tpu_custom_call" | custom-call | flops 22548578304 | bytes 29360128 | tf_op jit(solution)/shard_map/pallas_call | solution.py:276
  500.0 27.6 %shard_map.133.act_1_ref = bf16[768,1792]{1,0:T(8,128)(2,1)S(1)} custom-call(bf16[192,4096]{1,0:T(8,128)(2,1)S(1)} %fusion.28.own_hbm, bf16[96,4096]{1,0:T(8,128)(2,1)S(1)} %collective-permute-done.21.near_1_hbm, bf16[96,4096]{1,0:T(8,128)(2,1)S(1)} %collective-permute-done.22.near_2_hbm, bf16[192,4096]{1,0:T(8,128)(2,1)S(1)} %collective-permute-done.23.far_1_hbm, ...), custom_call_target="tpu_custom_call" | custom-call | flops 22548578304 | bytes 29360128 | tf_op jit(solution)/shard_map/pallas_call | solution.py:252
  536.8 27.8 %shard_map.135.act_2_ref = bf16[768,1792]{1,0:T(8,128)(2,1)S(1)} custom-call(bf16[192,4096]{1,0:T(8,128)(2,1)S(1)} %fusion.28.own_hbm, bf16[96,4096]{1,0:T(8,128)(2,1)S(1)} %collective-permute-done.21.near_1_hbm, bf16[96,4096]{1,0:T(8,128)(2,1)S(1)} %collective-permute-done.22.near_2_hbm, bf16[192,4096]{1,0:T(8,128)(2,1)S(1)} %collective-permute-done.23.far_1_hbm, ...), custom_call_target="tpu_custom_call" | custom-call | flops 22548578304 | bytes 29360128 | tf_op jit(solution)/shard_map/pallas_call | solution.py:252
  575.3 26.5 %shard_map.136 = (bf16[192,4096]{1,0:T(8,128)(2,1)S(1)}, bf16[192,4096]{1,0:T(8,128)(2,1)S(1)}, bf16[192,4096]{1,0:T(8,128)(2,1)S(1)}, bf16[192,4096]{1,0:T(8,128)(2,1)S(1)}) custom-call(bf16[768,1792]{1,0:T(8,128)(2,1)S(1)} %shard_map.133.act_1_ref, bf16[768,1792]{1,0:T(8,128)(2,1)S(1)} %shard_map.135.act_2_ref, bf16[2,3584,4096]{2,1,0:T(8,128)(2,1)} %wd_hbm.1), custom_call_target="tpu_custom_call" | custom-call | flops 22548578304 | bytes 29360128 | tf_op jit(solution)/shard_map/pallas_call | solution.py:276
  603.9 10.7 %collective-permute-done.48 = bf16[96,4096]{1,0:T(8,128)(2,1)S(1)} collective-permute-done((bf16[96,4096]{1,0:T(8,128)(2,1)S(1)}, bf16[96,4096]{1,0:T(8,128)(2,1)S(1)}, u32[]{:S(2)}, u32[]{:S(2)}) %collective-permute-start.48) | collective-permute-done | bytes 786464 | tf_op jit(solution)/shard_map/ppermute | solution.py:599
  625.4 11.0 %collective-permute-start.52 = (bf16[2,192,1024]{2,1,0:T(8,128)(2,1)}, bf16[2,192,1024]{2,1,0:T(8,128)(2,1)S(1)}, u32[]{:S(2)}, u32[]{:S(2)}) collective-permute-start(bf16[2,192,1024]{2,1,0:T(8,128)(2,1)} %pad_maximum_fusion.11), channel_id=1, source_target_pairs={{0,1},{3,3},{4,5},{7,7}} | collective-permute-start | bytes 2359304 | tf_op jit(solution)/shard_map/ppermute | solution.py:765
  654.7 18.8 %collective-permute-done.50 = bf16[96,4096]{1,0:T(8,128)(2,1)S(1)} collective-permute-done((bf16[96,4096]{1,0:T(8,128)(2,1)S(1)}, bf16[96,4096]{1,0:T(8,128)(2,1)S(1)}, u32[]{:S(2)}, u32[]{:S(2)}) %collective-permute-start.50) | collective-permute-done | bytes 786464 | tf_op jit(solution)/shard_map/ppermute | solution.py:599
  701.3 52.2 %shard_map.141 = bf16[8,4096]{1,0:T(8,128)(2,1)} custom-call(bf16[192,4096]{1,0:T(8,128)(2,1)} %copy-done.5, bf16[192,4096]{1,0:T(8,128)(2,1)} %copy-done.6, bf16[192,4096]{1,0:T(8,128)(2,1)} %copy-done.7, bf16[192,2048]{1,0:T(8,128)(2,1)} %copy-done.12, bf16[192,2048]{1,0:T(8,128)(2,1)} %copy-done.13, bf16[192,2048]{1,0:T(8,128)(2,1)} %copy-done.14, ...), custom_call_target="tpu_custom_call" | custom-call | flops 8999999488 | bytes 60000000 | tf_op jit(solution)/shard_map/pallas_call | solution.py:489
  (284 shorter events, 243.0 us)
Async XLA Ops:
  21.0 59.2 %collective-permute-start.31 = (bf16[1024,512]{1,0:T(8,128)(2,1)}, bf16[1024,512]{1,0:T(8,128)(2,1)S(1)}, u32[]{:S(2)}, u32[]{:S(2)}) collective-permute-start(bf16[1024,512]{1,0:T(8,128)(2,1)} %pad_maximum_fusion.7.refs_0_), channel_id=1, source_target_pairs={{0,4},{4,0},{1,5},{5,1},{2,6},{6,2},{3,7},{7,3}} | collective-permute-start | bytes 3145736 | tf_op jit(solution)/shard_map/ppermute | solution.py:602
  23.3 303.0 %collective-permute-start.29 = (bf16[1024,512]{1,0:T(8,128)(2,1)}, bf16[1024,512]{1,0:T(8,128)(2,1)}, u32[]{:S(2)}, u32[]{:S(2)}) collective-permute-start(bf16[1024,512]{1,0:T(8,128)(2,1)} %pad_maximum_fusion.7.refs_0_), channel_id=1, source_target_pairs={{0,2},{2,0},{1,3},{3,1},{4,6},{6,4},{5,7},{7,5}} | collective-permute-start | bytes 3145736 | tf_op jit(solution)/shard_map/ppermute | solution.py:599
  24.8 55.3 %collective-permute-start.30 = (bf16[1024,512]{1,0:T(8,128)(2,1)S(1)}, bf16[1024,512]{1,0:T(8,128)(2,1)S(1)}, u32[]{:S(2)}, u32[]{:S(2)}) collective-permute-start(bf16[1024,512]{1,0:T(8,128)(2,1)S(1)} %pad_maximum_fusion.8.refs_1_), channel_id=1, source_target_pairs={{0,2},{2,0},{1,3},{3,1},{4,6},{6,4},{5,7},{7,5}} | collective-permute-start | bytes 3145736 | tf_op jit(solution)/shard_map/ppermute | solution.py:599
  159.6 66.3 %collective-permute-start.14 = (bf16[192,4096]{1,0:T(8,128)(2,1)}, bf16[192,4096]{1,0:T(8,128)(2,1)S(1)}, u32[]{:S(2)}, u32[]{:S(2)}) collective-permute-start(bf16[192,4096]{1,0:T(8,128)(2,1)} %pad_maximum_fusion.2), channel_id=1, source_target_pairs={{0,4},{4,0},{1,5},{5,1},{2,6},{6,2},{3,7},{7,3}} | collective-permute-start | bytes 4718600 | tf_op jit(solution)/shard_map/ppermute | solution.py:602
  160.8 66.0 %collective-permute-start.13 = (bf16[192,4096]{1,0:T(8,128)(2,1)}, bf16[192,4096]{1,0:T(8,128)(2,1)S(1)}, u32[]{:S(2)}, u32[]{:S(2)}) collective-permute-start(bf16[192,4096]{1,0:T(8,128)(2,1)} %pad_maximum_fusion.1), channel_id=1, source_target_pairs={{0,2},{2,0},{1,3},{3,1},{4,6},{6,4},{5,7},{7,5}} | collective-permute-start | bytes 4718600 | tf_op jit(solution)/shard_map/ppermute | solution.py:599
  200.5 55.6 %collective-permute-start.12 = (bf16[96,4096]{1,0:T(8,128)(2,1)S(1)}, bf16[96,4096]{1,0:T(8,128)(2,1)S(1)}, u32[]{:S(2)}, u32[]{:S(2)}) collective-permute-start(bf16[96,4096]{1,0:T(8,128)(2,1)S(1)} %get-tuple-element.298), channel_id=1, source_target_pairs={{0,2},{2,0},{1,3},{3,1},{4,6},{6,4},{5,7},{7,5}} | collective-permute-start | bytes 2359304 | tf_op jit(solution)/shard_map/ppermute | solution.py:599
  202.0 54.1 %collective-permute-start.11 = (bf16[96,4096]{1,0:T(8,128)(2,1)S(1)}, bf16[96,4096]{1,0:T(8,128)(2,1)S(1)}, u32[]{:S(2)}, u32[]{:S(2)}) collective-permute-start(bf16[96,4096]{1,0:T(8,128)(2,1)S(1)} %get-tuple-element.296), channel_id=1, source_target_pairs={{0,4},{4,0},{1,5},{5,1},{2,6},{6,2},{3,7},{7,3}} | collective-permute-start | bytes 2359304 | tf_op jit(solution)/shard_map/ppermute | solution.py:602
  225.9 68.5 %collective-permute-start.10 = (bf16[192,4096]{1,0:T(8,128)(2,1)S(1)}, bf16[192,4096]{1,0:T(8,128)(2,1)S(1)}, u32[]{:S(2)}, u32[]{:S(2)}) collective-permute-start(bf16[192,4096]{1,0:T(8,128)(2,1)S(1)} %get-tuple-element.257), channel_id=1, source_target_pairs={{0,4},{4,0},{1,5},{5,1},{2,6},{6,2},{3,7},{7,3}} | collective-permute-start | bytes 4718600 | tf_op jit(solution)/shard_map/ppermute | solution.py:602
  226.8 70.0 %collective-permute-start.9 = (bf16[192,4096]{1,0:T(8,128)(2,1)S(1)}, bf16[192,4096]{1,0:T(8,128)(2,1)S(1)}, u32[]{:S(2)}, u32[]{:S(2)}) collective-permute-start(bf16[192,4096]{1,0:T(8,128)(2,1)S(1)} %get-tuple-element.258), channel_id=1, source_target_pairs={{0,2},{2,0},{1,3},{3,1},{4,6},{6,4},{5,7},{7,5}} | collective-permute-start | bytes 4718600 | tf_op jit(solution)/shard_map/ppermute | solution.py:599
  294.8 45.1 %collective-permute-start.34 = (bf16[1024,512]{1,0:T(8,128)(2,1)S(1)}, bf16[1024,512]{1,0:T(8,128)(2,1)S(1)}, u32[]{:S(2)}, u32[]{:S(2)}) collective-permute-start(bf16[1024,512]{1,0:T(8,128)(2,1)S(1)} %copy-done.11), channel_id=1, source_target_pairs={{0,4},{4,0},{1,5},{5,1},{2,6},{6,2},{3,7},{7,3}} | collective-permute-start | bytes 3145736 | tf_op jit(solution)/shard_map/ppermute | solution.py:602
  296.8 76.9 %collective-permute-start.20 = (bf16[192,4096]{1,0:T(8,128)(2,1)}, bf16[192,4096]{1,0:T(8,128)(2,1)S(1)}, u32[]{:S(2)}, u32[]{:S(2)}) collective-permute-start(bf16[192,4096]{1,0:T(8,128)(2,1)} %pad_maximum_fusion.4), channel_id=1, source_target_pairs={{0,4},{4,0},{1,5},{5,1},{2,6},{6,2},{3,7},{7,3}} | collective-permute-start | bytes 4718600 | tf_op jit(solution)/shard_map/ppermute | solution.py:602
  326.4 48.7 %collective-permute-start.19 = (bf16[192,4096]{1,0:T(8,128)(2,1)S(1)}, bf16[192,4096]{1,0:T(8,128)(2,1)S(1)}, u32[]{:S(2)}, u32[]{:S(2)}) collective-permute-start(bf16[192,4096]{1,0:T(8,128)(2,1)S(1)} %pad_maximum_fusion.3), channel_id=1, source_target_pairs={{0,2},{2,0},{1,3},{3,1},{4,6},{6,4},{5,7},{7,5}} | collective-permute-start | bytes 4718600 | tf_op jit(solution)/shard_map/ppermute | solution.py:599
  326.9 124.1 %collective-permute-start.25 = (bf16[192,4096]{1,0:T(8,128)(2,1)S(1)}, bf16[192,4096]{1,0:T(8,128)(2,1)S(1)}, u32[]{:S(2)}, u32[]{:S(2)}) collective-permute-start(bf16[192,4096]{1,0:T(8,128)(2,1)S(1)} %get-tuple-element.172), channel_id=1, source_target_pairs={{0,2},{2,0},{1,3},{3,1},{4,6},{6,4},{5,7},{7,5}} | collective-permute-start | bytes 4718600 | tf_op jit(solution)/shard_map/ppermute | solution.py:599
  328.4 122.7 %collective-permute-start.26 = (bf16[192,4096]{1,0:T(8,128)(2,1)S(1)}, bf16[192,4096]{1,0:T(8,128)(2,1)S(1)}, u32[]{:S(2)}, u32[]{:S(2)}) collective-permute-start(bf16[192,4096]{1,0:T(8,128)(2,1)S(1)} %get-tuple-element.173), channel_id=1, source_target_pairs={{0,4},{4,0},{1,5},{5,1},{2,6},{6,2},{3,7},{7,3}} | collective-permute-start | bytes 4718600 | tf_op jit(solution)/shard_map/ppermute | solution.py:602
  339.9 151.1 %collective-permute-start.35 = (bf16[1024,512]{1,0:T(8,128)(2,1)}, bf16[1024,512]{1,0:T(8,128)(2,1)S(1)}, u32[]{:S(2)}, u32[]{:S(2)}) collective-permute-start(bf16[1024,512]{1,0:T(8,128)(2,1)} %collective-permute-done.29.refs_2_), channel_id=1, source_target_pairs={{0,1},{1,0},{2,3},{3,2},{4,5},{5,4},{6,7},{7,6}} | collective-permute-start | bytes 3145736 | tf_op jit(solution)/shard_map/ppermute | solution.py:605
  375.1 42.7 %collective-permute-start.17 = (bf16[96,4096]{1,0:T(8,128)(2,1)S(1)}, bf16[96,4096]{1,0:T(8,128)(2,1)S(1)}, u32[]{:S(2)}, u32[]{:S(2)}) collective-permute-start(bf16[96,4096]{1,0:T(8,128)(2,1)S(1)} %get-tuple-element.290), channel_id=1, source_target_pairs={{0,4},{4,0},{1,5},{5,1},{2,6},{6,2},{3,7},{7,3}} | collective-permute-start | bytes 2359304 | tf_op jit(solution)/shard_map/ppermute | solution.py:602
  454.2 45.3 %collective-permute-start.28 = (bf16[96,4096]{1,0:T(8,128)(2,1)S(1)}, bf16[96,4096]{1,0:T(8,128)(2,1)S(1)}, u32[]{:S(2)}, u32[]{:S(2)}) collective-permute-start(bf16[96,4096]{1,0:T(8,128)(2,1)S(1)} %get-tuple-element.283), channel_id=1, source_target_pairs={{0,2},{2,0},{1,3},{3,1},{4,6},{6,4},{5,7},{7,5}} | collective-permute-start | bytes 2359304 | tf_op jit(solution)/shard_map/ppermute | solution.py:599
  456.2 43.3 %collective-permute-start.27 = (bf16[96,4096]{1,0:T(8,128)(2,1)S(1)}, bf16[96,4096]{1,0:T(8,128)(2,1)S(1)}, u32[]{:S(2)}, u32[]{:S(2)}) collective-permute-start(bf16[96,4096]{1,0:T(8,128)(2,1)S(1)} %get-tuple-element.285), channel_id=1, source_target_pairs={{0,4},{4,0},{1,5},{5,1},{2,6},{6,2},{3,7},{7,3}} | collective-permute-start | bytes 2359304 | tf_op jit(solution)/shard_map/ppermute | solution.py:602
  567.9 57.4 %collective-permute-start.46 = (bf16[3,768,512]{2,1,0:T(8,128)(2,1)}, bf16[3,768,512]{2,1,0:T(8,128)(2,1)S(1)}, u32[]{:S(2)}, u32[]{:S(2)}) collective-permute-start(bf16[3,768,512]{2,1,0:T(8,128)(2,1)} %pad_maximum_fusion), channel_id=1, source_target_pairs={{2,1},{1,3},{6,5},{5,7}} | collective-permute-start | bytes 7077896 | tf_op jit(solution)/shard_map/ppermute | solution.py:765
  568.7 67.6 %collective-permute-start.45 = (bf16[3,768,512]{2,1,0:T(8,128)(2,1)}, bf16[3,768,512]{2,1,0:T(8,128)(2,1)}, u32[]{:S(2)}, u32[]{:S(2)}) collective-permute-start(bf16[3,768,512]{2,1,0:T(8,128)(2,1)} %pad_maximum_fusion), channel_id=1, source_target_pairs={{0,1},{3,3},{4,5},{7,7}} | collective-permute-start | bytes 7077896 | tf_op jit(solution)/shard_map/ppermute | solution.py:765
  686.2 68.8 %collective-permute-start.59 = (bf16[2,192,1024]{2,1,0:T(8,128)(2,1)}, bf16[2,192,1024]{2,1,0:T(8,128)(2,1)}, u32[]{:S(2)}, u32[]{:S(2)}) collective-permute-start(bf16[2,192,1024]{2,1,0:T(8,128)(2,1)} %pad_maximum_fusion.13), channel_id=1, source_target_pairs={{2,1},{1,3},{6,5},{5,7}} | collective-permute-start | bytes 2359304 | tf_op jit(solution)/shard_map/ppermute | solution.py:765
  687.8 67.2 %collective-permute-start.58 = (bf16[2,192,1024]{2,1,0:T(8,128)(2,1)}, bf16[2,192,1024]{2,1,0:T(8,128)(2,1)}, u32[]{:S(2)}, u32[]{:S(2)}) collective-permute-start(bf16[2,192,1024]{2,1,0:T(8,128)(2,1)} %pad_maximum_fusion.13), channel_id=1, source_target_pairs={{0,1},{3,3},{4,5},{7,7}} | collective-permute-start | bytes 2359304 | tf_op jit(solution)/shard_map/ppermute | solution.py:765
  693.7 67.9 %collective-permute-start.56 = (bf16[2,192,1024]{2,1,0:T(8,128)(2,1)}, bf16[2,192,1024]{2,1,0:T(8,128)(2,1)S(1)}, u32[]{:S(2)}, u32[]{:S(2)}) collective-permute-start(bf16[2,192,1024]{2,1,0:T(8,128)(2,1)} %pad_maximum_fusion.12), channel_id=1, source_target_pairs={{2,1},{1,3},{6,5},{5,7}} | collective-permute-start | bytes 2359304 | tf_op jit(solution)/shard_map/ppermute | solution.py:765
  694.4 67.2 %collective-permute-start.55 = (bf16[2,192,1024]{2,1,0:T(8,128)(2,1)}, bf16[2,192,1024]{2,1,0:T(8,128)(2,1)}, u32[]{:S(2)}, u32[]{:S(2)}) collective-permute-start(bf16[2,192,1024]{2,1,0:T(8,128)(2,1)} %pad_maximum_fusion.12), channel_id=1, source_target_pairs={{0,1},{3,3},{4,5},{7,7}} | collective-permute-start | bytes 2359304 | tf_op jit(solution)/shard_map/ppermute | solution.py:765
  (79 other events, 1665.5 us)
